TPU v7x, 64 devices: a 2x2x8 block of a 4x4x8 slice. The times are simulated.
64 devices in a mesh: rep: 8 (over x, y, core), dp: 8 (over z).
Axes of the slice: x: 2, y: 2, z: 8, core: 2. Of those that a mesh axis runs over, the one named last changes fastest.
The devices are a block of a 4x4x8 slice.
Arguments:
- x: bfloat16 [64, 4096, 512], P(('rep', 'dp')), parts along dimension 0
- dy: bfloat16 [64, 4096, 512], P(('rep', 'dp')), parts along dimension 0
- w_gate: bfloat16 [2, 512, 2048], replicated
- w_up: bfloat16 [2, 512, 2048], replicated
- w_down: bfloat16 [2, 2048, 512], replicated
- m_w_gate: float32 [2, 512, 2048], replicated
- m_w_up: float32 [2, 512, 2048], replicated
- m_w_down: float32 [2, 2048, 512], replicated
- v_w_gate: float32 [2, 512, 2048], replicated
- v_w_up: float32 [2, 512, 2048], replicated
- v_w_down: float32 [2, 2048, 512], replicated
Outputs:
- output 1: bfloat16 [16, 512, 2048], P('rep'), parts along dimension 0
- output 2: bfloat16 [16, 512, 2048], P('rep'), parts along dimension 0
- output 3: bfloat16 [16, 2048, 512], P('rep'), parts along dimension 0
- output 4: float32 [16, 512, 2048], P('rep'), parts along dimension 0
- output 5: float32 [16, 512, 2048], P('rep'), parts along dimension 0
- output 6: float32 [16, 2048, 512], P('rep'), parts along dimension 0
- output 7: float32 [16, 512, 2048], P('rep'), parts along dimension 0
- output 8: float32 [16, 512, 2048], P('rep'), parts along dimension 0
- output 9: float32 [16, 2048, 512], P('rep'), parts along dimension 0
There are 8 independent parts. A program takes and returns all parts, laid end to end along the dimension named above; an argument that names none is the same for every part.
All inputs are finite; a program needn't handle non-finite values.
Results may differ from a plain program's by a relative error of at most 0.022.
Values are sent between devices in bfloat16 or wider.
A program may use at most 768 MiB of HBM per device.

v0:
```python
import jax
import jax.numpy as jnp
from jax import lax
from jax.sharding import PartitionSpec as P

NAMES = ("w_gate", "w_up", "w_down")


def matmul(a, w):
    return jnp.dot(a, w, preferred_element_type=jnp.float32).astype(jnp.bfloat16)


def normed(h):
    wide = h.astype(jnp.float32)
    scale = lax.rsqrt(jnp.mean(wide**2, -1, keepdims=True) + 1e-6)
    return (wide * scale).astype(jnp.bfloat16)


def layer(h, w):
    a = normed(h)
    gate = jnp.dot(a, w["w_gate"], preferred_element_type=jnp.float32)
    up = jnp.dot(a, w["w_up"], preferred_element_type=jnp.float32)
    return h + matmul((jax.nn.silu(gate) * up).astype(jnp.bfloat16), w["w_down"])


def adamw(w, m, v, g):
    m = 0.9 * m + 0.1 * g
    v = 0.95 * v + 0.05 * g * g
    step = m * lax.rsqrt(v + 1e-8) + 0.1 * w
    return (w - 0.02 * step).astype(jnp.bfloat16), m, v


def clipped(gradients, sum_of_squares, count):
    factor = jnp.minimum(1.0, 0.5 * lax.rsqrt(sum_of_squares / count + 1e-30))
    return [g * factor for g in gradients]


def solution(mesh):
    def step(x, dy, *arrays):
        weights, m, v = (arrays[i : i + 3] for i in (0, 3, 6))
        layers = weights[0].shape[0]
        h, kept = x[0], []
        for number in range(layers):
            kept.append(h)
            h = layer(h, {name: w[number] for name, w in zip(NAMES, weights, strict=True)})
        by_h, summed = dy[0], [None] * layers
        for number in reversed(range(layers)):
            _, back = jax.vjp(lambda w, h: layer(h, w), {name: w[number] for name, w in zip(NAMES, weights, strict=True)}, kept[number])
            by_w, by_h = back(by_h)
            summed[number] = [lax.psum(by_w[name], "dp") for name in NAMES]
        gradients = [jnp.stack([summed[number][i] for number in range(layers)]).astype(jnp.float32) for i in range(3)]
        gradients = clipped(gradients, sum(jnp.sum(g * g) for g in gradients), sum(g.size for g in gradients))
        new = [adamw(w.astype(jnp.float32), m, v, g) for w, m, v, g in zip(weights, m, v, gradients, strict=True)]
        return tuple(one[which] for which in range(3) for one in new)

    return jax.shard_map(
        step,
        mesh=mesh,
        in_specs=(P(("rep", "dp"), None, None),) * 2 + (P(None, None, None),) * 9,
        out_specs=(P("rep", None, None),) * 9,
        check_vma=False,
    )
```

profile of v0, /device:TPU:22, one launch (start us, length us, event | category | flops | bytes accessed | tf_op | source)
XLA Modules:
  0.0 680.1 jit_solution(938010925649791147)
XLA Ops:
  7.3 6.3 copy.20
  13.6 3.1 fusion.24
  16.7 6.3 copy.21
  23.0 15.1 %convolution_convert_fusion.1 = bf16[4096,2048]{1,0:T(8,128)(2,1)} fusion(bf16[1,4096,512]{2,1,0:T(8,128)(2,1)} %param.12, bf16[2,2048,512]{2,1,0:T(8,128)(2,1)} %param.15), kind=kOutput, calls=%fused_computation.25 | convolution fusion | flops 8598323200 | bytes 23068672 | tf_op jit(solution)/shard_map/transpose(jvp())/dot_general | solution.py:10
  38.1 17.8 %fusion.94 = f32[4096,2048]{1,0:T(8,128)} fusion(bf16[2,512,2048]{2,1,0:T(8,128)(2,1)S(1)} %copy-done.8, bf16[1,4096,512]{2,1,0:T(8,128)(2,1)} %param.11, f32[4096]{0:T(1024)S(1)} %add_rsqrt_fusion), kind=kOutput, calls=%fused_computation.112 | convolution fusion | flops 8596226048 | bytes 39862272 | tf_op jit(solution)/shard_map/dot_general | solution.py:21
  55.9 32.6 %multiply_convert_fusion.1 = (bf16[4096,2048]{1,0:T(8,128)(2,1)}, f32[4096,2048]{1,0:T(8,128)}) fusion(f32[4096,2048]{1,0:T(8,128)} %fusion.94, bf16[2,512,2048]{2,1,0:T(8,128)(2,1)S(1)} %copy-done.10, bf16[1,4096,512]{2,1,0:T(8,128)(2,1)} %param.11, f32[4096]{0:T(1024)S(1)} %add_rsqrt_fusion), kind=kOutput, calls=%fused_computation.17 | convolution fusion | flops 8646557696 | bytes 90193920 | tf_op jit(solution)/shard_map/dot_general | solution.py:22
  88.5 15.8 %fusion.40 = (f32[4096]{0:T(1024)S(1)}, bf16[4096,512]{0,1:T(8,128)(2,1)}) fusion(bf16[4096,2048]{1,0:T(8,128)(2,1)} %get-tuple-element.24, bf16[2,2048,512]{2,1,0:T(8,128)(2,1)} %param.15, bf16[1,4096,512]{1,2,0:T(8,128)(2,1)} %copy.20), kind=kOutput, calls=%fused_computation.73 | convolution fusion | flops 8600416256 | bytes 27279360 | tf_op jit(solution)/shard_map/dot_general | solution.py:10
  104.3 18.1 %fusion.81 = f32[4096,2048]{1,0:T(8,128)} fusion(bf16[4096,512]{0,1:T(8,128)(2,1)} %get-tuple-element.27, f32[4096]{0:T(1024)S(1)} %fusion.107, bf16[2,512,2048]{2,1,0:T(8,128)(2,1)} %param.14), kind=kOutput, calls=%fused_computation.101 | convolution fusion | flops 8596226048 | bytes 39862272 | tf_op jit(solution)/shard_map/jvp()/dot_general | solution.py:22
  122.4 41.0 %fusion.2 = (bf16[4096,2048]{1,0:T(8,128)(2,1)}, f32[4096,2048]{1,0:T(8,128)}) fusion(f32[4096,2048]{1,0:T(8,128)} %fusion.81, bf16[4096,2048]{1,0:T(8,128)(2,1)} %convolution_convert_fusion.1, bf16[2,512,2048]{2,1,0:T(8,128)(2,1)} %param.13, bf16[4096,512]{0,1:T(8,128)(2,1)} %get-tuple-element.27, f32[4096]{0:T(1024)S(1)} %fusion.107), kind=kOutput, calls=%fused_computation.8 | convolution fusion | flops 8696889344 | bytes 106971136 | tf_op jit(solution)/shard_map/jvp()/dot_general | solution.py:21
  163.5 26.0 %fusion.65 = bf16[1,2048,512]{2,1,0:T(8,128)(2,1)} fusion(bf16[1,4096,512]{2,1,0:T(8,128)(2,1)} %param.12, f32[4096,2048]{1,0:T(8,128)} %fusion.81, f32[4096,2048]{1,0:T(8,128)} %get-tuple-element.29), kind=kOutput, calls=%fused_computation.95 | convolution fusion | flops 8641314816 | bytes 73400320 | tf_op jit(solution)/shard_map/transpose(jvp())/dot_general | solution.py:10
  189.4 20.6 %fusion.68 = bf16[1,512,2048]{2,1,0:T(8,128)(2,1)} fusion(bf16[4096,2048]{1,0:T(8,128)(2,1)} %convolution_convert_fusion.1, bf16[4096,512]{0,1:T(8,128)(2,1)S(1)} %copy-done.11, f32[4096]{0:T(1024)S(1)} %fusion.107, f32[4096,2048]{1,0:T(8,128)} %get-tuple-element.29), kind=kOutput, calls=%fused_computation.96 | convolution fusion | flops 8647606272 | bytes 56639488 | tf_op jit(solution)/shard_map/transpose(jvp())/dot_general | solution.py:22
  210.0 21.8 %fusion.43 = bf16[4096,512]{0,1:T(8,128)(2,1)} fusion(bf16[4096,2048]{1,0:T(8,128)(2,1)} %convolution_convert_fusion.1, bf16[2,512,2048]{2,1,0:T(8,128)(2,1)} %param.14, f32[4096,2048]{1,0:T(8,128)} %get-tuple-element.29), kind=kOutput, calls=%fused_computation.77 | convolution fusion | flops 8642363392 | bytes 56623104 | tf_op jit(solution)/shard_map/transpose(jvp())/dot_general | solution.py:22
  231.8 14.9 %fusion.69 = bf16[1,512,2048]{2,1,0:T(8,128)(2,1)} fusion(bf16[4096,2048]{1,0:T(8,128)(2,1)} %get-tuple-element.28, bf16[4096,512]{0,1:T(8,128)(2,1)} %get-tuple-element.27, f32[4096]{0:T(1024)S(1)} %fusion.107), kind=kOutput, calls=%fused_computation.97 | convolution fusion | flops 8596226048 | bytes 23085056 | tf_op jit(solution)/shard_map/transpose(jvp())/dot_general | solution.py:21
  246.7 15.1 %fusion.42 = (f32[4096]{0:T(1024)S(1)}, bf16[4096,512]{0,1:T(8,128)(2,1)}) fusion(bf16[4096,512]{0,1:T(8,128)(2,1)S(1)} %copy-done.12, bf16[4096,512]{0,1:T(8,128)(2,1)} %fusion.43, bf16[4096,2048]{1,0:T(8,128)(2,1)} %get-tuple-element.28, bf16[2,512,2048]{2,1,0:T(8,128)(2,1)S(1)} %copy-done.9), kind=kOutput, calls=%fused_computation.75 | convolution fusion | flops 8600416256 | bytes 31473664 | tf_op jit(solution)/shard_map/transpose(jvp())/dot_general | solution.py:21
  261.8 4.3 fusion.48
  268.1 13.9 %fusion.70 = bf16[1,2048,512]{2,1,0:T(8,128)(2,1)} fusion(bf16[4096,2048]{1,0:T(8,128)(2,1)} %get-tuple-element.24, bf16[4096,512]{0,1:T(8,128)(2,1)S(1)} %fusion.48), kind=kOutput, calls=%fused_computation.98 | convolution fusion | flops 8590983168 | bytes 23068672 | tf_op jit(solution)/shard_map/transpose(jvp())/dot_general | solution.py:10
  282.0 14.8 %convolution_convert_fusion = bf16[4096,2048]{1,0:T(8,128)(2,1)} fusion(bf16[4096,512]{0,1:T(8,128)(2,1)} %copy-done.13, bf16[2,2048,512]{2,1,0:T(8,128)(2,1)S(1)} %copy-done.7), kind=kOutput, calls=%fused_computation.24 | convolution fusion | flops 8598323200 | bytes 23068672 | tf_op jit(solution)/shard_map/transpose(jvp())/dot_general | solution.py:10
  296.9 20.8 %fusion.71 = bf16[1,512,2048]{2,1,0:T(8,128)(2,1)} fusion(bf16[4096,2048]{1,0:T(8,128)(2,1)} %convolution_convert_fusion, f32[4096,2048]{1,0:T(8,128)} %fusion.94, bf16[1,4096,512]{1,2,0:T(8,128)(2,1)S(1)} %copy-done, f32[4096]{0:T(1024)S(1)} %copy-done.17), kind=kOutput, calls=%fused_computation.99 | convolution fusion | flops 8647606272 | bytes 56639488 | tf_op jit(solution)/shard_map/transpose(jvp())/dot_general | solution.py:22
  317.7 34.0 %fusion.74 = bf16[1,512,2048]{2,1,0:T(8,128)(2,1)} fusion(f32[4096,2048]{1,0:T(8,128)} %fusion.94, f32[4096,2048]{1,0:T(8,128)} %get-tuple-element.25, bf16[4096,2048]{1,0:T(8,128)(2,1)} %convolution_convert_fusion, bf16[1,4096,512]{1,2,0:T(8,128)(2,1)} %copy.20, f32[4096]{0:T(1024)S(1)} %copy-done.17), kind=kOutput, calls=%fused_computation.100 | convolution fusion | flops 8689549312 | bytes 90193920 | tf_op jit(solution)/shard_map/transpose(jvp())/dot_general | solution.py:21
  351.7 264.3 %all-reduce.3.cloned.1.call-done = (bf16[1,512,2048]{2,1,0:T(8,128)(2,1)}, bf16[1,512,2048]{2,1,0:T(8,128)(2,1)}, bf16[1,512,2048]{2,1,0:T(8,128)(2,1)}, bf16[1,...) async-done(((bf16[1,512,2048]{2,1,0:T(8,128)(2,1)}, bf16[1,512,2048]{2,1,0:T(8,128)(2,1)}, bf16[1,512,2048]{2,1,0:T(8,128)(2,1)}, ...) | async-done | bytes 12582928 | tf_op jit(solution)/shard_map/psum | solution.py:50
  616.0 4.5 fusion.30
  620.4 4.3 fusion.29
  629.5 15.8 %fusion.36 = (bf16[2,2048,512]{2,1,0:T(8,128)(2,1)}, f32[2,2048,512]{2,1,0:T(8,128)}, f32[2,2048,512]{2,1,0:T(8,128)}) fusion(bf16[2,2048,512]{2,1,0:T(8,128)(2,1)} %param.15, f32[]{:T(128)S(6)} %min_shard_map.3, bf16[1,2048,512]{2,1,0:T(8,128)(2,1)} %get-tuple-element.13, bf16[1,2048,512]{2,1,0:T(8,128)(2,1)} %get-tuple-element.14, ...), kind=kLoop, calls=%fused_computation.69 | loop fusion | flops 41943040 | bytes 46137348 | tf_op jit(solution)/shard_map/convert_element_type | solution.py:30
  645.4 27.4 %fusion.23 = (bf16[2,512,2048]{2,1,0:T(8,128)(2,1)}, f32[2,512,2048]{2,1,0:T(8,128)}, f32[2,512,2048]{2,1,0:T(8,128)}, bf16[2,512,2048]{2,1,0:T(8,128)(2,1)}, f3...) fusion(bf16[2,512,2048]{2,1,0:T(8,128)(2,1)} %param.13, f32[]{:T(128)S(6)} %min_shard_map.3, ...), kind=kLoop, calls=%fused_computation.56 | loop fusion | flops 83886080 | bytes 92274688 | tf_op jit(solution)/shard_map/convert_element_type | solution.py:30
  (42 shorter events, 5.0 us)
Async XLA Ops:
  7.2 608.8 %all-reduce.3.cloned.1.call-start = ((), (), s32[]{:S(2)}) async-start(), calls=%async_computation | async-start | bytes 25165824 | tf_op jit(solution)/shard_map/psum | solution.py:50
  16.7 39.2 %copy-start.16 = (f32[4096]{0:T(1024)}, f32[4096]{0:T(1024)S(1)}, u32[]{:S(2)}) copy-start(f32[4096]{0:T(1024)S(1)} %add_rsqrt_fusion) | copy-start | bytes 49156
  23.0 15.1 %copy-start.8 = (bf16[2,512,2048]{2,1,0:T(8,128)(2,1)S(1)}, bf16[2,512,2048]{2,1,0:T(8,128)(2,1)}, u32[]{:S(2)}) copy-start(bf16[2,512,2048]{2,1,0:T(8,128)(2,1)} %param.13) | copy-start | bytes 12582916
  38.1 17.8 %copy-start.10 = (bf16[2,512,2048]{2,1,0:T(8,128)(2,1)S(1)}, bf16[2,512,2048]{2,1,0:T(8,128)(2,1)}, u32[]{:S(2)}) copy-start(bf16[2,512,2048]{2,1,0:T(8,128)(2,1)} %param.14) | copy-start | bytes 12582916
  104.3 18.2 %copy-start.14 = (f32[4096]{0:T(1024)}, f32[4096]{0:T(1024)S(1)}, u32[]{:S(2)}) copy-start(f32[4096]{0:T(1024)S(1)} %get-tuple-element.26) | copy-start | bytes 49156
  163.5 26.0 %copy-start.11 = (bf16[4096,512]{0,1:T(8,128)(2,1)S(1)}, bf16[4096,512]{0,1:T(8,128)(2,1)}, u32[]{:S(2)}) copy-start(bf16[4096,512]{0,1:T(8,128)(2,1)} %get-tuple-element.27) | copy-start | bytes 12582916
  231.8 14.9 %copy-start.9 = (bf16[2,512,2048]{2,1,0:T(8,128)(2,1)S(1)}, bf16[2,512,2048]{2,1,0:T(8,128)(2,1)}, u32[]{:S(2)}) copy-start(bf16[2,512,2048]{2,1,0:T(8,128)(2,1)} %param.13) | copy-start | bytes 12582916
  231.8 14.9 %copy-start.12 = (bf16[4096,512]{0,1:T(8,128)(2,1)S(1)}, bf16[4096,512]{0,1:T(8,128)(2,1)}, u32[]{:S(2)}) copy-start(bf16[4096,512]{0,1:T(8,128)(2,1)} %get-tuple-element.27) | copy-start | bytes 12582916
  246.7 15.1 %copy-start.15 = (f32[4096]{0:T(1024)S(1)}, f32[4096]{0:T(1024)}, u32[]{:S(2)}) copy-start(f32[4096]{0:T(1024)} %copy-done.14) | copy-start | bytes 49156
  246.7 15.1 %copy-start.1 = (bf16[1,4096,512]{1,2,0:T(8,128)(2,1)S(1)}, bf16[1,4096,512]{1,2,0:T(8,128)(2,1)}, u32[]{:S(2)}) copy-start(bf16[1,4096,512]{1,2,0:T(8,128)(2,1)} %copy.21) | copy-start | bytes 12582916
  266.1 2.0 copy-start.13
  268.1 13.9 %copy-start.7 = (bf16[2,2048,512]{2,1,0:T(8,128)(2,1)S(1)}, bf16[2,2048,512]{2,1,0:T(8,128)(2,1)}, u32[]{:S(2)}) copy-start(bf16[2,2048,512]{2,1,0:T(8,128)(2,1)} %param.15) | copy-start | bytes 12582916
  282.0 14.8 %copy-start = (bf16[1,4096,512]{1,2,0:T(8,128)(2,1)S(1)}, bf16[1,4096,512]{1,2,0:T(8,128)(2,1)}, u32[]{:S(2)}) copy-start(bf16[1,4096,512]{1,2,0:T(8,128)(2,1)} %copy.20) | copy-start | bytes 12582916
  282.0 14.8 %copy-start.17 = (f32[4096]{0:T(1024)S(1)}, f32[4096]{0:T(1024)}, u32[]{:S(2)}) copy-start(f32[4096]{0:T(1024)} %copy-done.16) | copy-start | bytes 49156
  616.0 8.8 %copy-start.2 = (bf16[1,512,2048]{2,1,0:T(8,128)(2,1)S(1)}, bf16[1,512,2048]{2,1,0:T(8,128)(2,1)}, u32[]{:S(2)}) copy-start(bf16[1,512,2048]{2,1,0:T(8,128)(2,1)} %get-tuple-element.9) | copy-start | bytes 6291460
  616.0 8.8 %copy-start.3 = (bf16[1,512,2048]{2,1,0:T(8,128)(2,1)S(1)}, bf16[1,512,2048]{2,1,0:T(8,128)(2,1)}, u32[]{:S(2)}) copy-start(bf16[1,512,2048]{2,1,0:T(8,128)(2,1)} %get-tuple-element.10) | copy-start | bytes 6291460
  629.5 15.9 %copy-start.4 = (bf16[1,512,2048]{2,1,0:T(8,128)(2,1)S(1)}, bf16[1,512,2048]{2,1,0:T(8,128)(2,1)}, u32[]{:S(2)}) copy-start(bf16[1,512,2048]{2,1,0:T(8,128)(2,1)} %get-tuple-element.10) | copy-start | bytes 6291460
  629.5 15.9 %copy-start.5 = (bf16[1,512,2048]{2,1,0:T(8,128)(2,1)S(1)}, bf16[1,512,2048]{2,1,0:T(8,128)(2,1)}, u32[]{:S(2)}) copy-start(bf16[1,512,2048]{2,1,0:T(8,128)(2,1)} %get-tuple-element.11) | copy-start | bytes 6291460
  629.5 15.9 %copy-start.6 = (bf16[1,512,2048]{2,1,0:T(8,128)(2,1)S(1)}, bf16[1,512,2048]{2,1,0:T(8,128)(2,1)}, u32[]{:S(2)}) copy-start(bf16[1,512,2048]{2,1,0:T(8,128)(2,1)} %get-tuple-element.12) | copy-start | bytes 6291460
Sparse Core Ops, SparseCore 0:
  351.8 264.0 all-reduce.2
where the time goes:
time: 689 us; the launch traced here: 680 us
  matrix products  322 us (47%)
  waiting for transfers between devices  264 us (38%)
  other arithmetic  62.1 us (9%)
  between operations  16.7 us (2%)
  local copies, waits for them, and re-layouts  14.7 us (2%)
    psum x1, waiting for transfers between devices, step(): summed[number] = [lax.psum(by_w[name], 'dp') for name in NAMES]  264 us
    dot_general x5, matrix products, layer(): gate = jnp.dot(a, w['w_gate'], preferred_element_type=jnp.float32)  123 us
    dot_general x5, matrix products, layer(): up = jnp.dot(a, w['w_up'], preferred_element_type=jnp.float32)  114 us
    dot_general x5, matrix products, matmul(): jnp.dot(a, w, preferred_element_type=jnp.float32).astype(jnp.bfloat16)  85.6 us
    convert_element_type x2, other arithmetic, adamw(): return ((w - 0.02 * step).astype(jnp.bfloat16), m, v)  43.2 us
    unnamed x38, local copies, waits for them, and re-layouts  14.7 us
  transfers between devices with their start and end apart: 1, of which 1 were waited for; matrix products, arithmetic and copies ran while one was open for 0% of the time, Pallas kernels for 0%

commit v1 on v0

v1 whole, which is shorter than its diff:
```python
import functools

import jax
import jax.numpy as jnp
from jax import lax
from jax.experimental import pallas as pl
from jax.experimental.pallas import tpu as pltpu
from jax.sharding import PartitionSpec as P

F32, BF16 = jnp.float32, jnp.bfloat16
AXIS = "dp"
TILE = 512
CHUNK = 256
VMEM_LIMIT = 67043328


def mm(a, b):
    return jnp.dot(a, b, preferred_element_type=F32)


def mm_nt(a, b):
    return lax.dot_general(a, b, (((1,), (1,)), ((), ())), preferred_element_type=F32)


def mm_tn(a, b):
    return lax.dot_general(a, b, (((0,), (0,)), ((), ())), preferred_element_type=F32)


def sigmoid(x):
    return 0.5 * jnp.tanh(0.5 * x) + 0.5


def normed(wide):
    scale = lax.rsqrt(jnp.mean(wide * wide, -1, keepdims=True) + 1e-6)
    return (wide * scale).astype(BF16)


def gradients_body(n, x_hbm, dy_hbm, wg_hbm, wu_hbm, wd_hbm, full_hbm, own_hbm, squares_ref,
                   a0, a0t, a1, a1t, dy, h1, acc, w0g, w0u, w0d, w1, w1d, act, dgu, accd, accgu, grads, slots, sums, squares,
                   first_sem, w1_sem, rs_send, rs_recv, ag_send, ag_recv, sq_send, sq_recv, full_sem, own_sem):
    tokens, d = h1.shape
    ff = w0d.shape[0]
    tiles, chunks = tokens // TILE, ff // CHUNK
    groups = 2 * chunks
    hops = n // 2
    shard_rows = grads.shape[1] // n
    half = shard_rows // 2
    me = lax.axis_index(AXIS)
    to = (lax.rem(me + 1, n), lax.rem(me + n - 1, n))

    def rows(t):
        return pl.ds(pl.multiple_of(t * TILE, TILE), TILE)

    def cols(c):
        return pl.ds(pl.multiple_of(c * CHUNK, CHUNK), CHUNK)

    def shard(away):
        return pl.multiple_of(lax.rem(me + away + n, n) * shard_rows, shard_rows)

    def remote(src, dst, send, recv, way):
        return pltpu.make_async_remote_copy(src_ref=src, dst_ref=dst, send_sem=send, recv_sem=recv, device_id={AXIS: to[way]}, device_id_type=pl.DeviceIdType.MESH)

    def rs_copy(s, g, way):
        p = lax.rem(g, 2)
        if s == 1:
            part = pl.ds(way * half, half)
            src, dst = grads.at[g, pl.ds(shard(hops) + way * half, half)], slots.at[way, 0, p, part]
        else:
            src, dst = sums.at[way, s - 2, p], slots.at[way, s - 1, p]
        return remote(src, dst, rs_send.at[way, s - 1, p], rs_recv.at[way, s - 1, p], way)

    def rs_add(s, g):
        p = lax.rem(g, 2)
        for way in range(2):
            own = grads[g, pl.ds(shard((1 - 2 * way) * (hops + 1 - s)), shard_rows)]
            if s == 2:
                here = slice(way * half, way * half + half)
                there = slice(half - way * half, shard_rows - way * half)
                sums[way, 0, p, there] = own[there]
                sums[way, 0, p, here] = (slots[way, 0, p, here].astype(F32) + own[here].astype(F32)).astype(BF16)
            else:
                sums[way, s - 2, p] = (slots[way, s - 2, p].astype(F32) + own.astype(F32)).astype(BF16)

    def rs_final(g):
        p = lax.rem(g, 2)
        mine = pl.ds(shard(0), shard_rows)
        total = slots[0, hops - 1, p].astype(F32) + slots[1, hops - 1, p].astype(F32) + grads[g, mine].astype(F32)
        total = total.astype(BF16)
        grads[g, mine] = total
        wide = total.astype(F32)
        squares[0] += jnp.sum((wide * wide).reshape(shard_rows // 8, 8, CHUNK), axis=0)

    def ag_copies(k, whole):
        pair, j = k // hops, lax.rem(k, hops)
        copies = []
        for b in range(2):
            for way in range(2):
                at = shard((2 * way - 1) * j)
                part = pl.ds(at, shard_rows) if whole else pl.ds(at + way * half, half)
                ref = grads.at[2 * pair + b, part]
                copies.append(remote(ref, ref, ag_send.at[way, j, b], ag_recv.at[way, j, b], way))
        return copies

    def full_copy(pair):
        return pltpu.make_async_copy(grads.at[pl.ds(2 * pair, 2)], full_hbm.at[pl.ds(2 * pair, 2)], full_sem.at[pair])

    def own_copy(g):
        return pltpu.make_async_copy(grads.at[g, pl.ds(shard(0), shard_rows)], own_hbm.at[g - chunks], own_sem.at[g - chunks])

    gathers = hops * (chunks // 2)

    def tick(t):
        def group(g, f):
            pl.when((g >= 0) & (g < groups))(functools.partial(f, g))

        def arrived(s, g):
            for way in range(2):
                rs_copy(s, g, way).wait()

        def add(s, g):
            arrived(s - 1, g)
            rs_add(s, g)

        def final(g):
            arrived(hops, g)
            rs_final(g)

        def send(s, g):
            for way in range(2):
                rs_copy(s, g, way).start()

        for s in range(hops, 1, -1):
            group(t - s, functools.partial(add, s))
        group(t - hops - 1, final)
        for s in range(hops, 0, -1):
            group(t - s, functools.partial(send, s))

        k = t - hops - 2
        for whole in (True, False):
            last = hops - 1

            @pl.when((k >= 1) & (k <= gathers) & ((lax.rem(k - 1 + hops, hops) < last) == whole))
            def _():
                for copy in ag_copies(k - 1, whole):
                    copy.wait()

        for whole in (True, False):
            last = hops - 1

            @pl.when((k >= 0) & (k < gathers) & ((lax.rem(k + 2 * hops, hops) < last) == whole))
            def _():
                for copy in ag_copies(k, whole):
                    copy.start()

        @pl.when((k >= hops) & (k <= gathers) & (lax.rem(k + 2 * hops, hops) == 0))
        def _():
            full_copy(k // hops - 1).start()

        g = t - hops - 2

        @pl.when((g >= chunks) & (g < groups))
        def _():
            own_copy(g).start()

    def w1_copies(c):
        slot = lax.rem(c, 2)
        return (
            pltpu.make_async_copy(wg_hbm.at[1, :, cols(c)], w1.at[slot, :, pl.ds(0, CHUNK)], w1_sem.at[slot, 0]),
            pltpu.make_async_copy(wu_hbm.at[1, :, cols(c)], w1.at[slot, :, pl.ds(CHUNK, CHUNK)], w1_sem.at[slot, 1]),
            pltpu.make_async_copy(wd_hbm.at[1, cols(c), :], w1d.at[slot], w1_sem.at[slot, 2]),
        )

    squares[...] = jnp.zeros_like(squares)
    barrier = pltpu.get_barrier_semaphore()
    for away in range(1, n):
        pl.semaphore_signal(barrier, inc=1, device_id={AXIS: lax.rem(me + away, n)}, device_id_type=pl.DeviceIdType.MESH)

    first = (
        pltpu.make_async_copy(x_hbm.at[0], h1, first_sem.at[0]),
        pltpu.make_async_copy(wg_hbm.at[0], w0g, first_sem.at[1]),
        pltpu.make_async_copy(wu_hbm.at[0], w0u, first_sem.at[2]),
        pltpu.make_async_copy(wd_hbm.at[0], w0d, first_sem.at[3]),
        pltpu.make_async_copy(dy_hbm.at[0], dy, first_sem.at[4]),
    )
    for copy in first + w1_copies(0) + w1_copies(1):
        copy.start()

    def norm0(t):
        a = normed(h1[rows(t), :].astype(F32))
        a0[rows(t), :] = a
        a0t[:, rows(t)] = a.T

    first[0].wait()
    norm0(0)
    accd[...] = jnp.zeros_like(accd)
    accgu[...] = jnp.zeros_like(accgu)
    for copy in first[1:4]:
        copy.wait()

    def forward(t, _):
        a = a0[rows(t), :]

        @pl.when(t + 1 < tiles)
        def _():
            norm0(t + 1)

        for c in range(chunks):
            s = pl.ds(c * CHUNK, CHUNK)
            gate, up = mm(a, w0g[:, s]), mm(a, w0u[:, s])
            grads[c, :TILE, :] = (gate * sigmoid(gate) * up).astype(BF16)
        acc[rows(t), :] = jnp.zeros((TILE, d), F32)
        out = mm(grads[0, :TILE, :], w0d[:CHUNK, :])
        for c in range(1, chunks):
            out += mm(grads[c, :TILE, :], w0d[c * CHUNK : (c + 1) * CHUNK, :])
        h = (h1[rows(t), :].astype(F32) + out.astype(BF16).astype(F32)).astype(BF16)
        h1[rows(t), :] = h
        a = normed(h.astype(F32))
        a1[rows(t), :] = a
        a1t[:, rows(t)] = a.T
        return 0

    lax.fori_loop(0, tiles, forward, 0)
    first[4].wait()
    pl.semaphore_wait(barrier, n - 1)

    def elementwise(gate, up, dact, b):
        s = sigmoid(gate)
        p = gate * s
        act[b] = (p * up).astype(BF16)
        dact = dact.astype(BF16).astype(F32)
        dgu[b, :, CHUNK:] = (dact * p).astype(BF16)
        dgu[b, :, :CHUNK] = (dact * up * (s + p * (1.0 - s))).astype(BF16)

    def finish(g):
        rd, rf = d // n, CHUNK // n
        for r in range(n):
            at = r * shard_rows
            grads[g, at : at + rd, :] = accgu[r * rd : (r + 1) * rd, :CHUNK].astype(BF16)
            grads[g, at + rd : at + 2 * rd, :] = accgu[r * rd : (r + 1) * rd, CHUNK:].astype(BF16)
            for q in range(d // CHUNK):
                grads[g, at + 2 * rd + q * rf : at + 2 * rd + (q + 1) * rf, :] = accd[r * rf : (r + 1) * rf, q * CHUNK : (q + 1) * CHUNK].astype(BF16)
        accd[...] = jnp.zeros_like(accd)
        accgu[...] = jnp.zeros_like(accgu)

    total = chunks * tiles

    def front1(i):
        c, t, b = i // tiles, lax.rem(i, tiles), lax.rem(i, 2)
        slot = lax.rem(c, 2)
        a = a1[rows(t), :]
        elementwise(mm(a, w1[slot, :, :CHUNK]), mm(a, w1[slot, :, CHUNK:]), mm_nt(dy[rows(t), :], w1d[slot]), b)

    def back1(i):
        c, t, b = i // tiles, lax.rem(i, tiles), lax.rem(i, 2)
        accd[...] += mm_tn(act[b], dy[rows(t), :])
        accgu[...] += mm(a1t[:, rows(t)], dgu[b])
        acc[rows(t), :] += mm_nt(dgu[b], w1[lax.rem(c, 2)])

    def layer1(i, _):
        c, t = i // tiles, lax.rem(i, tiles)

        @pl.when((t == tiles - 1) & (c + 1 < chunks))
        def _():
            for copy in w1_copies(c + 1):
                copy.wait()

        front1(jnp.minimum(i + 1, total - 1))
        back1(i)

        @pl.when(t == tiles - 1)
        def _():
            finish(c)

            @pl.when(c + 2 < chunks)
            def _():
                for copy in w1_copies(c + 2):
                    copy.start()

            tick(c + 1)

        return 0

    for copy in w1_copies(0):
        copy.wait()
    front1(0)
    lax.fori_loop(0, total, layer1, 0)

    def between(t, _):
        da = acc[rows(t), :].astype(BF16).astype(F32)
        wide = h1[rows(t), :].astype(F32)
        scale = lax.rsqrt(jnp.mean(wide * wide, -1, keepdims=True) + 1e-6)
        along = jnp.sum(da * wide, -1, keepdims=True) * (scale * scale * scale / d)
        through = (da * scale - wide * along).astype(BF16).astype(F32)
        dy[rows(t), :] = (dy[rows(t), :].astype(F32) + through).astype(BF16)
        return 0

    lax.fori_loop(0, tiles, between, 0)

    def front0(i):
        c, t, b = i // tiles, lax.rem(i, tiles), lax.rem(i, 2)
        a = a0[rows(t), :]
        elementwise(mm(a, w0g[:, cols(c)]), mm(a, w0u[:, cols(c)]), mm_nt(dy[rows(t), :], w0d[cols(c), :]), b)

    def layer0(i, _):
        c, t, b = i // tiles, lax.rem(i, tiles), lax.rem(i, 2)
        front0(jnp.minimum(i + 1, total - 1))
        accd[...] += mm_tn(act[b], dy[rows(t), :])
        accgu[...] += mm(a0t[:, rows(t)], dgu[b])

        @pl.when(t == tiles - 1)
        def _():
            finish(chunks + c)
            tick(chunks + c + 1)

        return 0

    front0(0)
    lax.fori_loop(0, total, layer0, 0)

    def sq_copy(away, mine):
        q = me if mine else lax.rem(me + away, n)
        return pltpu.make_async_remote_copy(
            src_ref=squares.at[0], dst_ref=squares.at[1 + q], send_sem=sq_send.at[away - 1], recv_sem=sq_recv.at[q],
            device_id={AXIS: lax.rem(me + away, n)}, device_id_type=pl.DeviceIdType.MESH)

    last = max(groups + hops + 1, gathers + hops + 2)

    def drain(t, _):
        tick(t)

        @pl.when(t == groups + hops)
        def _():
            for away in range(1, n):
                sq_copy(away, True).start()

        return 0

    lax.fori_loop(groups + 1, last + 1, drain, 0)
    for away in range(1, n):
        sq_copy(away, True).wait_send()
        sq_copy(away, False).wait_recv()
    squares[pl.ds(1 + me, 1)] = squares[0:1]
    everyone = squares[1]
    for q in range(1, n):
        everyone += squares[1 + q]
    squares_ref[...] = everyone
    for pair in range(chunks // 2):
        full_copy(pair).wait()
    for g in range(chunks, groups):
        own_copy(g).wait()


def gradients_of(n, x, dy, wg, wu, wd):
    _, tokens, d = x.shape
    _, ff, _ = wd.shape
    chunks, hops = ff // CHUNK, n // 2
    shard_rows = 3 * d // n
    v, dma = pltpu.VMEM, pltpu.SemaphoreType.DMA
    anyspace = pl.BlockSpec(memory_space=pl.ANY)
    return pl.pallas_call(
        functools.partial(gradients_body, n),
        out_shape=(
            jax.ShapeDtypeStruct((chunks, n * shard_rows, CHUNK), BF16),
            jax.ShapeDtypeStruct((chunks, shard_rows, CHUNK), BF16),
            jax.ShapeDtypeStruct((8, CHUNK), F32),
        ),
        in_specs=[anyspace] * 5,
        out_specs=(anyspace, anyspace, pl.BlockSpec(memory_space=pltpu.VMEM)),
        scratch_shapes=[
            v((tokens, d), BF16), v((d, tokens), BF16), v((tokens, d), BF16), v((d, tokens), BF16),
            v((tokens, d), BF16), v((tokens, d), BF16), v((tokens, d), F32),
            v((d, ff), BF16), v((d, ff), BF16), v((ff, d), BF16),
            v((2, d, 2 * CHUNK), BF16), v((2, CHUNK, d), BF16),
            v((2, TILE, CHUNK), BF16), v((2, TILE, 2 * CHUNK), BF16),
            v((CHUNK, d), F32), v((d, 2 * CHUNK), F32),
            v((2 * chunks, n * shard_rows, CHUNK), BF16),
            v((2, hops, 2, shard_rows, CHUNK), BF16), v((2, hops - 1, 2, shard_rows, CHUNK), BF16),
            v((n + 1, 8, CHUNK), F32),
            dma((5,)), dma((2, 3)), dma((2, hops, 2)), dma((2, hops, 2)), dma((2, hops, 2)), dma((2, hops, 2)),
            dma((n - 1,)), dma((n,)), dma((chunks // 2,)), dma((chunks,)),
        ],
        compiler_params=pltpu.CompilerParams(vmem_limit_bytes=VMEM_LIMIT, collective_id=0, has_side_effects=True),
        name="gradients",
    )(x, dy, wg, wu, wd)


def adamw_body(n, factor_ref, g_ref, *refs):
    wmv, new = refs[:9], refs[-9:]
    factor = factor_ref[0]
    rows_g = g_ref.shape[1] // n
    d = wmv[0].shape[1]
    rd, rf = d // n, CHUNK // n

    def update(i, r, c, g):
        g = g.astype(F32) * factor
        w, m, v = (wmv[3 * k + i][0, r, c].astype(F32) for k in range(3))
        m = 0.9 * m + 0.1 * g
        v = 0.95 * v + 0.05 * g * g
        w = w - 0.02 * (m * lax.rsqrt(v + 1e-8) + 0.1 * w)
        for k, value in enumerate((w, m, v)):
            new[3 * k + i][0, r, c] = value.astype(new[3 * k + i].dtype)

    for r in range(n):
        at = r * rows_g
        for i in range(2):
            update(i, slice(r * rd, (r + 1) * rd), slice(None), g_ref[0, at + i * rd : at + (i + 1) * rd, :])
        for q in range(d // CHUNK):
            update(2, slice(r * rf, (r + 1) * rf), slice(q * CHUNK, (q + 1) * CHUNK), g_ref[0, at + 2 * rd + q * rf : at + 2 * rd + (q + 1) * rf, :])


def adamw(n, layer, factor, g, wmv, before):
    layers, d, ff = wmv[0].shape
    wide = pl.BlockSpec((1, d, CHUNK), lambda c: (layer, 0, c))
    tall = pl.BlockSpec((1, CHUNK, d), lambda c: (layer, c, 0))
    nine = [wide, wide, tall] * 3
    count = layers * d * ff
    return pl.pallas_call(
        functools.partial(adamw_body, n),
        grid=(ff // CHUNK,),
        out_shape=[jax.ShapeDtypeStruct(a.shape, a.dtype) for a in wmv],
        in_specs=[pl.BlockSpec(memory_space=pltpu.SMEM), pl.BlockSpec((1, g.shape[1], CHUNK), lambda c: (c, 0, 0)), *nine]
        + [pl.BlockSpec(memory_space=pl.ANY)] * len(before),
        out_specs=nine,
        input_output_aliases={11 + i: i for i in range(len(before))},
        compiler_params=pltpu.CompilerParams(vmem_limit_bytes=VMEM_LIMIT, dimension_semantics=("arbitrary",)),
        cost_estimate=pl.CostEstimate(flops=60 * count, bytes_accessed=33 * count, transcendentals=3 * count),
        name=f"adamw{layer}",
    )(factor, g, *wmv, *before)


def gathered(n, own):
    hops = n // 2
    half = own.shape[1] // 2
    right = [(i, (i + 1) % n) for i in range(n)]
    left = [(i, (i - 1) % n) for i in range(n)]
    me = lax.axis_index(AXIS)
    parts = {0: own}
    a = b = own
    for j in range(1, hops):
        a, b = lax.ppermute(a, AXIS, right), lax.ppermute(b, AXIS, left)
        parts[-j], parts[j] = a, b
    a, b = lax.ppermute(a[:, :half], AXIS, right), lax.ppermute(b[:, half:], AXIS, left)
    parts[hops] = jnp.concatenate([a, b], axis=1)
    by_away = jnp.stack([parts[j] for j in range(1 - hops, hops + 1)])
    return jnp.roll(by_away, me + 1 - hops, axis=0).transpose(1, 0, 2, 3).reshape(own.shape[0], -1, own.shape[2])


def solution(mesh):
    n = mesh.shape[AXIS]

    def step(x, dy, *wmv):
        full, own, squares = gradients_of(n, x, dy, *wmv[:3])
        count = sum(w.size for w in wmv[:3])
        factor = jnp.minimum(1.0, 0.5 * lax.rsqrt(jnp.sum(squares) / count + 1e-30)).reshape(1)
        new = adamw(n, 1, factor, full, wmv, ())
        new = adamw(n, 0, factor, gathered(n, own), wmv, new)
        return tuple(new)

    return jax.shard_map(
        step,
        mesh=mesh,
        in_specs=(P(("rep", "dp"), None, None),) * 2 + (P(None, None, None),) * 9,
        out_specs=(P("rep", None, None),) * 9,
        check_vma=False,
    )
```

time: 689 us -> 413 us (0.60); the launches traced: 680 us -> 412 us
  Pallas kernels: 0 us -> 348 us
  matrix products: 322 us -> 0 us
  waiting for transfers between devices: 264 us -> 29.7 us
  other arithmetic: 62.1 us -> 1.41 us
  between operations: 16.7 us -> 1.73 us
  starting transfers between devices: 0.06 us -> 11.4 us
    pallas_call x0 -> x3, Pallas kernels: none -> 348 us  [the longest x1 299 us: gradients_of(): pl.pallas_call(functools.partial(gradients_body, n), out_shape=(jax.Shape...]
    dot_general x15 -> x0, matrix products: 322 us -> none  [the longest x5 123 us: layer(): gate = jnp.dot(a, w['w_gate'], preferred_element_type=jnp.float32)]
    psum x1 -> x0, waiting for transfers between devices: 264 us -> none  [step(): summed[number] = [lax.psum(by_w[name], 'dp') for name in NAMES]]
    convert_element_type x2 -> x0, other arithmetic: 43.2 us -> none  [adamw(): return ((w - 0.02 * step).astype(jnp.bfloat16), m, v)]
    ppermute x0 -> x8, waiting for transfers between devices: none -> 29.7 us  [the longest x6 29.2 us: gathered(): a, b = (lax.ppermute(a, AXIS, right), lax.ppermute(b, AXIS, left))]
    reduce_sum x4 -> x1, other arithmetic: 14.6 us -> 1.3 us  [step(): jnp.sum(squares) / count + 1e-30]
    ppermute x0 -> x8, starting transfers between devices: none -> 11.4 us  [the longest x6 7.99 us: gathered(): a, b = (lax.ppermute(a, AXIS, right), lax.ppermute(b, AXIS, left))]
    unnamed x38 -> x24, local copies, waits for them, and re-layouts: 14.7 us -> 14.1 us
  transfers between devices with their start and end apart: 1 -> 8, of which waited for: 1 -> 3; matrix products, arithmetic and copies ran while one was open for 0% -> 3% of each run, Pallas kernels for 0% -> 6%
where the time goes in v1:
time: 413 us; the launch traced here: 412 us
  Pallas kernels  348 us (84%)
  waiting for transfers between devices  29.7 us (7%)
  local copies, waits for them, and re-layouts  20.1 us (5%)
  starting transfers between devices  11.4 us (3%)
    pallas_call x1, Pallas kernels, gradients_of(): pl.pallas_call(functools.partial(gradients_body, n), out_shape=(jax.Shape...  299 us
    pallas_call x2, Pallas kernels, adamw(): pl.pallas_call(functools.partial(adamw_body, n), grid=(ff // CHUNK,), out...  49.3 us
    ppermute x6, waiting for transfers between devices, gathered(): a, b = (lax.ppermute(a, AXIS, right), lax.ppermute(b, AXIS, left))  29.2 us
    unnamed x24, local copies, waits for them, and re-layouts  14.1 us
  transfers between devices with their start and end apart: 8, of which 3 were waited for; matrix products, arithmetic and copies ran while one was open for 3% of the time, Pallas kernels for 6%

profile of v1, /device:TPU:22, one launch (start us, length us, event | category | flops | bytes accessed | tf_op | source)
XLA Modules:
  0.0 412.5 jit_solution(5373627027278430103)
XLA Ops:
  0.6 298.7 %gradients.1 = (bf16[8,1536,256]{2,1,0:T(8,128)(2,1)}, bf16[8,192,256]{2,1,0:T(8,128)(2,1)}, f32[8,256]{1,0:T(8,128)}) custom-call(bf16[1,4096,512]{2,1,0:T(8,128)(2,1)} %x_hbm.1, bf16[1,4096,512]{2,1,0:T(8,128)(2,1)} %dy_hbm.1, bf16[2,512,2048]{2,1,0:T(8,128)(2,1)} %refs_0_.3, bf16[2,512,2048]{2,1,0:T(8,128)(2,1)} %refs_1_.3, bf16[2,2048,512]{2,1,0:T(8,128)(2,1)} %refs_2_.3), custom_call_target="tpu_custom_call" | custom-call | tf_op jit(solution)/shard_map/gradients/pallas_call | solution.py:360
  299.4 2.7 collective-permute-start.3
  302.1 14.2 %collective-permute-done.3 = bf16[8,192,256]{2,1,0:T(8,128)(2,1)S(1)} collective-permute-done((bf16[8,192,256]{2,1,0:T(8,128)(2,1)}, bf16[8,192,256]{2,1,0:T(8,128)(2,1)S(1)}, u32[]{:S(2)}, u32[]{:S(2)}) %collective-permute-start.3) | collective-permute-done | bytes 786464 | tf_op jit(solution)/shard_map/ppermute | solution.py:440
  317.2 2.6 collective-permute-start.4
  319.8 15.0 %collective-permute-done.4 = bf16[8,192,256]{2,1,0:T(8,128)(2,1)} collective-permute-done((bf16[8,192,256]{2,1,0:T(8,128)(2,1)S(1)}, bf16[8,192,256]{2,1,0:T(8,128)(2,1)}, u32[]{:S(2)}, u32[]{:S(2)}) %collective-permute-start.4) | collective-permute-done | bytes 786464 | tf_op jit(solution)/shard_map/ppermute | solution.py:440
  334.8 2.6 collective-permute-start.5
  337.4 1.3 reduce_sum.9
  339.4 24.7 %adamw1.1 = (bf16[2,512,2048]{2,1,0:T(8,128)(2,1)}, bf16[2,512,2048]{2,1,0:T(8,128)(2,1)}, bf16[2,2048,512]{2,1,0:T(8,128)(2,1)}, f32[2,512,2048]{2,1,0:T(8,128)...) custom-call(f32[1]{0:T(128)} %bitcast.factor_ref, ...), custom_call_target="tpu_custom_call" | custom-call | flops 125829120 | bytes 69206016 | tf_op jit(solution)/shard_map/adamw1/pallas_call | solution.py:417
  364.1 1.2 slice.9
  365.3 3.3 collective-permute-start.7
  368.6 1.0 slice.8
  369.8 1.2 bitcast_dynamic-update-slice_fusion.12
  371.0 1.2 bitcast_dynamic-update-slice_fusion.10
  372.2 1.2 bitcast_dynamic-update-slice_fusion.8
  373.4 1.2 bitcast_dynamic-update-slice_fusion.6
  374.6 1.2 bitcast_dynamic-update-slice_fusion.4
  375.8 1.2 bitcast_dynamic-update-slice_fusion.2
  377.0 1.2 bitcast_dynamic-update-slice_fusion
  378.8 1.2 bitcast_dynamic-update-slice_fusion.13
  380.0 1.2 bitcast_dynamic-update-slice_fusion.11
  381.4 1.2 bitcast_dynamic-update-slice_fusion.3
  382.6 1.2 bitcast_dynamic-update-slice_fusion.1
  384.6 3.1 copy.29
  387.7 24.6 %adamw0.1 = (bf16[2,512,2048]{2,1,0:T(8,128)(2,1)}, bf16[2,512,2048]{2,1,0:T(8,128)(2,1)}, bf16[2,2048,512]{2,1,0:T(8,128)(2,1)}, f32[2,512,2048]{2,1,0:T(8,128)...) custom-call(f32[1]{0:T(128)} %bitcast.factor_ref, ...), custom_call_target="tpu_custom_call", output_to_operand_aliasing={{0}: (11, {}), {1}: (12, {}), {2}: (13, {}), {3}: (14, {}),... | custom-call | flops 125829120 | bytes 69206016 | tf_op jit(solution)/shard_map/adamw0/pallas_call | solution.py:417
  (26 shorter events, 2.6 us)
Async XLA Ops:
  299.4 16.9 %collective-permute-start.3 = (bf16[8,192,256]{2,1,0:T(8,128)(2,1)}, bf16[8,192,256]{2,1,0:T(8,128)(2,1)S(1)}, u32[]{:S(2)}, u32[]{:S(2)}) collective-permute-start(bf16[8,192,256]{2,1,0:T(8,128)(2,1)} %get-tuple-element.22), channel_id=1, source_target_pairs={{0,7},{1,0},{2,1},{3,2},{4,3},{5,4},{6,5},{7,6},{8,15},{9,8},{10,9... | collective-permute-start | bytes 2359304 | tf_op jit(solution)/shard_map/ppermute | solution.py:440
  302.1 17.7 %collective-permute-start = (bf16[8,192,256]{2,1,0:T(8,128)(2,1)}, bf16[8,192,256]{2,1,0:T(8,128)(2,1)S(1)}, u32[]{:S(2)}, u32[]{:S(2)}) collective-permute-start(bf16[8,192,256]{2,1,0:T(8,128)(2,1)} %get-tuple-element.22), channel_id=1, source_target_pairs={{0,1},{1,2},{2,3},{3,4},{4,5},{5,6},{6,7},{7,0},{8,9},{9,10},{10,1... | collective-permute-start | bytes 2359304 | tf_op jit(solution)/shard_map/ppermute | solution.py:440
  316.3 0.9 copy-start.1
  317.2 17.6 %collective-permute-start.4 = (bf16[8,192,256]{2,1,0:T(8,128)(2,1)S(1)}, bf16[8,192,256]{2,1,0:T(8,128)(2,1)}, u32[]{:S(2)}, u32[]{:S(2)}) collective-permute-start(bf16[8,192,256]{2,1,0:T(8,128)(2,1)S(1)} %collective-permute-done.3), channel_id=1, source_target_pairs={{0,7},{1,0},{2,1},{3,2},{4,3},{5,4},{6,5},{7,6},{8,15},{9,8},{10,9... | collective-permute-start | bytes 2359304 | tf_op jit(solution)/shard_map/ppermute | solution.py:440
  319.8 15.0 %copy-start.3 = (bf16[8,192,256]{2,1,0:T(8,128)(2,1)}, bf16[8,192,256]{2,1,0:T(8,128)(2,1)S(1)}, u32[]{:S(2)}) copy-start(bf16[8,192,256]{2,1,0:T(8,128)(2,1)S(1)} %collective-permute-done) | copy-start | bytes 2359300
  319.8 17.6 %collective-permute-start.1 = (bf16[8,192,256]{2,1,0:T(8,128)(2,1)S(1)}, bf16[8,192,256]{2,1,0:T(8,128)(2,1)}, u32[]{:S(2)}, u32[]{:S(2)}) collective-permute-start(bf16[8,192,256]{2,1,0:T(8,128)(2,1)S(1)} %collective-permute-done), channel_id=1, source_target_pairs={{0,1},{1,2},{2,3},{3,4},{4,5},{5,6},{6,7},{7,0},{8,9},{9,10},{10,1... | collective-permute-start | bytes 2359304 | tf_op jit(solution)/shard_map/ppermute | solution.py:440
  334.8 29.3 %collective-permute-start.5 = (bf16[8,192,256]{2,1,0:T(8,128)(2,1)}, bf16[8,192,256]{2,1,0:T(8,128)(2,1)}, u32[]{:S(2)}, u32[]{:S(2)}) collective-permute-start(bf16[8,192,256]{2,1,0:T(8,128)(2,1)} %collective-permute-done.4), channel_id=1, source_target_pairs={{0,7},{1,0},{2,1},{3,2},{4,3},{5,4},{6,5},{7,6},{8,15},{9,8},{10,9... | collective-permute-start | bytes 2359304 | tf_op jit(solution)/shard_map/ppermute | solution.py:440
  337.4 31.2 %collective-permute-start.2 = (bf16[8,192,256]{2,1,0:T(8,128)(2,1)}, bf16[8,192,256]{2,1,0:T(8,128)(2,1)}, u32[]{:S(2)}, u32[]{:S(2)}) collective-permute-start(bf16[8,192,256]{2,1,0:T(8,128)(2,1)} %collective-permute-done.1), channel_id=1, source_target_pairs={{0,1},{1,2},{2,3},{3,4},{4,5},{5,6},{6,7},{7,0},{8,9},{9,10},{10,1... | collective-permute-start | bytes 2359304 | tf_op jit(solution)/shard_map/ppermute | solution.py:440
  364.1 17.1 %copy-start.4 = (bf16[8,192,256]{2,1,0:T(8,128)(2,1)S(1)}, bf16[8,192,256]{2,1,0:T(8,128)(2,1)}, u32[]{:S(2)}) copy-start(bf16[8,192,256]{2,1,0:T(8,128)(2,1)} %copy-done.3) | copy-start | bytes 2359300
  364.1 17.2 %copy-start = (bf16[8,192,256]{2,1,0:T(8,128)(2,1)S(1)}, bf16[8,192,256]{2,1,0:T(8,128)(2,1)}, u32[]{:S(2)}) copy-start(bf16[8,192,256]{2,1,0:T(8,128)(2,1)} %get-tuple-element.22) | copy-start | bytes 2359300
  364.1 17.2 %copy-start.2 = (bf16[8,192,256]{2,1,0:T(8,128)(2,1)S(1)}, bf16[8,192,256]{2,1,0:T(8,128)(2,1)}, u32[]{:S(2)}) copy-start(bf16[8,192,256]{2,1,0:T(8,128)(2,1)} %copy-done.1) | copy-start | bytes 2359300
  365.3 12.9 %collective-permute-start.7 = (bf16[8,96,256]{2,1,0:T(8,128)(2,1)S(1)}, bf16[8,96,256]{2,1,0:T(8,128)(2,1)S(1)}, u32[]{:S(2)}, u32[]{:S(2)}) collective-permute-start(bf16[8,96,256]{2,1,0:T(8,128)(2,1)S(1)} %slice.9), channel_id=1, source_target_pairs={{0,7},{1,0},{2,1},{3,2},{4,3},{5,4},{6,5},{7,6},{8,15},{9,8},{10,9... | collective-permute-start | bytes 1179656 | tf_op jit(solution)/shard_map/ppermute | solution.py:442
  369.7 9.1 %collective-permute-start.6 = (bf16[8,96,256]{2,1,0:T(8,128)(2,1)S(1)}, bf16[8,96,256]{2,1,0:T(8,128)(2,1)S(1)}, u32[]{:S(2)}, u32[]{:S(2)}) collective-permute-start(bf16[8,96,256]{2,1,0:T(8,128)(2,1)S(1)} %slice.8), channel_id=1, source_target_pairs={{0,1},{1,2},{2,3},{3,4},{4,5},{5,6},{6,7},{7,0},{8,9},{9,10},{10,1... | collective-permute-start | bytes 1179656 | tf_op jit(solution)/shard_map/ppermute | solution.py:442

commit v2 on v1

--- a/solution.py
+++ b/solution.py
@@ -9,9 +9,11 @@
 
 F32, BF16 = jnp.float32, jnp.bfloat16
 AXIS = "dp"
-TILE = 512
+FTILE = 512
+TILE = 1024
 CHUNK = 256
 VMEM_LIMIT = 67043328
+ADAMW_VMEM = VMEM_LIMIT
 
 
 def mm(a, b):
@@ -51,6 +53,9 @@
     def rows(t):
         return pl.ds(pl.multiple_of(t * TILE, TILE), TILE)
 
+    def frows(t):
+        return pl.ds(pl.multiple_of(t * FTILE, FTILE), FTILE)
+
     def cols(c):
         return pl.ds(pl.multiple_of(c * CHUNK, CHUNK), CHUNK)
 
@@ -90,15 +95,14 @@
         wide = total.astype(F32)
         squares[0] += jnp.sum((wide * wide).reshape(shard_rows // 8, 8, CHUNK), axis=0)
 
-    def ag_copies(k, whole):
-        pair, j = k // hops, lax.rem(k, hops)
+    def ag_copies(pair, j, whole):
         copies = []
         for b in range(2):
             for way in range(2):
                 at = shard((2 * way - 1) * j)
                 part = pl.ds(at, shard_rows) if whole else pl.ds(at + way * half, half)
                 ref = grads.at[2 * pair + b, part]
-                copies.append(remote(ref, ref, ag_send.at[way, j, b], ag_recv.at[way, j, b], way))
+                copies.append(remote(ref, ref, ag_send.at[way, j, b, lax.rem(pair, 2)], ag_recv.at[way, j, b, lax.rem(pair, 2)], way))
         return copies
 
     def full_copy(pair):
@@ -107,7 +111,7 @@
     def own_copy(g):
         return pltpu.make_async_copy(grads.at[g, pl.ds(shard(0), shard_rows)], own_hbm.at[g - chunks], own_sem.at[g - chunks])
 
-    gathers = hops * (chunks // 2)
+    pairs = chunks // 2
 
     def tick(t):
         def group(g, f):
@@ -135,26 +139,26 @@
         for s in range(hops, 0, -1):
             group(t - s, functools.partial(send, s))
 
-        k = t - hops - 2
-        for whole in (True, False):
-            last = hops - 1
-
-            @pl.when((k >= 1) & (k <= gathers) & ((lax.rem(k - 1 + hops, hops) < last) == whole))
-            def _():
-                for copy in ag_copies(k - 1, whole):
-                    copy.wait()
-
-        for whole in (True, False):
-            last = hops - 1
-
-            @pl.when((k >= 0) & (k < gathers) & ((lax.rem(k + 2 * hops, hops) < last) == whole))
-            def _():
-                for copy in ag_copies(k, whole):
-                    copy.start()
-
-        @pl.when((k >= hops) & (k <= gathers) & (lax.rem(k + 2 * hops, hops) == 0))
-        def _():
-            full_copy(k // hops - 1).start()
+        e = lax.rem(t + hops, 2)
+        u = (t - hops - 2 - 3 * e) // 2
+
+        def gathering(u, f):
+            pair, j = 2 * (u // hops) + e, lax.rem(u + 2 * hops, hops)
+            for whole in (True, False):
+                pl.when((u >= 0) & (pair < pairs) & ((j < hops - 1) == whole))(functools.partial(f, pair, j, whole))
+
+        def landed(pair, j, whole):
+            for copy in ag_copies(pair, j, whole):
+                copy.wait()
+            if not whole:
+                full_copy(pair).start()
+
+        def pass_on(pair, j, whole):
+            for copy in ag_copies(pair, j, whole):
+                copy.start()
+
+        gathering(u - 1, landed)
+        gathering(u, pass_on)
 
         g = t - hops - 2
 
@@ -186,50 +190,60 @@
         copy.start()
 
     def norm0(t):
-        a = normed(h1[rows(t), :].astype(F32))
-        a0[rows(t), :] = a
-        a0t[:, rows(t)] = a.T
-
-    first[0].wait()
-    norm0(0)
-    accd[...] = jnp.zeros_like(accd)
-    accgu[...] = jnp.zeros_like(accgu)
-    for copy in first[1:4]:
-        copy.wait()
-
-    def forward(t, _):
-        a = a0[rows(t), :]
-
-        @pl.when(t + 1 < tiles)
-        def _():
-            norm0(t + 1)
-
+        a = normed(h1[frows(t), :].astype(F32))
+        a0[frows(t), :] = a
+        a0t[:, frows(t)] = a.T
+
+    def expand(t):
+        a = a0[frows(t), :]
+        b = lax.rem(t, 2) * chunks
         for c in range(chunks):
             s = pl.ds(c * CHUNK, CHUNK)
             gate, up = mm(a, w0g[:, s]), mm(a, w0u[:, s])
-            grads[c, :TILE, :] = (gate * sigmoid(gate) * up).astype(BF16)
-        acc[rows(t), :] = jnp.zeros((TILE, d), F32)
-        out = mm(grads[0, :TILE, :], w0d[:CHUNK, :])
+            grads[b + c, :FTILE, :] = (gate * sigmoid(gate) * up).astype(BF16)
+
+    def contract(t):
+        b = lax.rem(t, 2) * chunks
+        out = mm(grads[b, :FTILE, :], w0d[:CHUNK, :])
         for c in range(1, chunks):
-            out += mm(grads[c, :TILE, :], w0d[c * CHUNK : (c + 1) * CHUNK, :])
-        h = (h1[rows(t), :].astype(F32) + out.astype(BF16).astype(F32)).astype(BF16)
-        h1[rows(t), :] = h
+            out += mm(grads[b + c, :FTILE, :], w0d[c * CHUNK : (c + 1) * CHUNK, :])
+        h = (h1[frows(t), :].astype(F32) + out.astype(BF16).astype(F32)).astype(BF16)
+        h1[frows(t), :] = h
         a = normed(h.astype(F32))
-        a1[rows(t), :] = a
-        a1t[:, rows(t)] = a.T
+        a1[frows(t), :] = a
+        a1t[:, frows(t)] = a.T
+        acc[frows(t), :] = jnp.zeros((FTILE, d), F32)
+
+    first[0].wait()
+    norm0(0)
+    norm0(1)
+    accd[...] = jnp.zeros_like(accd)
+    accgu[...] = jnp.zeros_like(accgu)
+    first[1].wait()
+    first[2].wait()
+    expand(0)
+    first[3].wait()
+
+    ftiles = tokens // FTILE
+
+    def forward(t, _):
+        contract(t)
+        expand(t + 1)
+        norm0(jnp.minimum(t + 2, ftiles - 1))
         return 0
 
-    lax.fori_loop(0, tiles, forward, 0)
+    lax.fori_loop(0, ftiles - 1, forward, 0)
+    contract(ftiles - 1)
     first[4].wait()
     pl.semaphore_wait(barrier, n - 1)
 
-    def elementwise(gate, up, dact, b):
+    def elementwise(gate, up, dact):
         s = sigmoid(gate)
         p = gate * s
-        act[b] = (p * up).astype(BF16)
+        act[...] = (p * up).astype(BF16)
         dact = dact.astype(BF16).astype(F32)
-        dgu[b, :, CHUNK:] = (dact * p).astype(BF16)
-        dgu[b, :, :CHUNK] = (dact * up * (s + p * (1.0 - s))).astype(BF16)
+        dgu[:, CHUNK:] = (dact * p).astype(BF16)
+        dgu[:, :CHUNK] = (dact * up * (s + p * (1.0 - s))).astype(BF16)
 
     def finish(g):
         rd, rf = d // n, CHUNK // n
@@ -245,16 +259,16 @@
     total = chunks * tiles
 
     def front1(i):
-        c, t, b = i // tiles, lax.rem(i, tiles), lax.rem(i, 2)
+        c, t = i // tiles, lax.rem(i, tiles)
         slot = lax.rem(c, 2)
         a = a1[rows(t), :]
-        elementwise(mm(a, w1[slot, :, :CHUNK]), mm(a, w1[slot, :, CHUNK:]), mm_nt(dy[rows(t), :], w1d[slot]), b)
+        elementwise(mm(a, w1[slot, :, :CHUNK]), mm(a, w1[slot, :, CHUNK:]), mm_nt(dy[rows(t), :], w1d[slot]))
 
     def back1(i):
-        c, t, b = i // tiles, lax.rem(i, tiles), lax.rem(i, 2)
-        accd[...] += mm_tn(act[b], dy[rows(t), :])
-        accgu[...] += mm(a1t[:, rows(t)], dgu[b])
-        acc[rows(t), :] += mm_nt(dgu[b], w1[lax.rem(c, 2)])
+        c, t = i // tiles, lax.rem(i, tiles)
+        accgu[...] += mm(a1t[:, rows(t)], dgu[...])
+        accd[...] += mm_tn(act[...], dy[rows(t), :])
+        acc[rows(t), :] += mm_nt(dgu[...], w1[lax.rem(c, 2)])
 
     def layer1(i, _):
         c, t = i // tiles, lax.rem(i, tiles)
@@ -264,8 +278,8 @@
             for copy in w1_copies(c + 1):
                 copy.wait()
 
+        back1(i)
         front1(jnp.minimum(i + 1, total - 1))
-        back1(i)
 
         @pl.when(t == tiles - 1)
         def _():
@@ -297,15 +311,15 @@
     lax.fori_loop(0, tiles, between, 0)
 
     def front0(i):
-        c, t, b = i // tiles, lax.rem(i, tiles), lax.rem(i, 2)
+        c, t = i // tiles, lax.rem(i, tiles)
         a = a0[rows(t), :]
-        elementwise(mm(a, w0g[:, cols(c)]), mm(a, w0u[:, cols(c)]), mm_nt(dy[rows(t), :], w0d[cols(c), :]), b)
+        elementwise(mm(a, w0g[:, cols(c)]), mm(a, w0u[:, cols(c)]), mm_nt(dy[rows(t), :], w0d[cols(c), :]))
 
     def layer0(i, _):
-        c, t, b = i // tiles, lax.rem(i, tiles), lax.rem(i, 2)
+        c, t = i // tiles, lax.rem(i, tiles)
+        accgu[...] += mm(a0t[:, rows(t)], dgu[...])
+        accd[...] += mm_tn(act[...], dy[rows(t), :])
         front0(jnp.minimum(i + 1, total - 1))
-        accd[...] += mm_tn(act[b], dy[rows(t), :])
-        accgu[...] += mm(a0t[:, rows(t)], dgu[b])
 
         @pl.when(t == tiles - 1)
         def _():
@@ -323,7 +337,7 @@
             src_ref=squares.at[0], dst_ref=squares.at[1 + q], send_sem=sq_send.at[away - 1], recv_sem=sq_recv.at[q],
             device_id={AXIS: lax.rem(me + away, n)}, device_id_type=pl.DeviceIdType.MESH)
 
-    last = max(groups + hops + 1, gathers + hops + 2)
+    last = max(groups + hops + 1, *(hops + 2 + 3 * e + 2 * hops * ((pairs + 1 - e) // 2) for e in range(2)))
 
     def drain(t, _):
         tick(t)
@@ -371,12 +385,12 @@
             v((tokens, d), BF16), v((tokens, d), BF16), v((tokens, d), F32),
             v((d, ff), BF16), v((d, ff), BF16), v((ff, d), BF16),
             v((2, d, 2 * CHUNK), BF16), v((2, CHUNK, d), BF16),
-            v((2, TILE, CHUNK), BF16), v((2, TILE, 2 * CHUNK), BF16),
+            v((TILE, CHUNK), BF16), v((TILE, 2 * CHUNK), BF16),
             v((CHUNK, d), F32), v((d, 2 * CHUNK), F32),
             v((2 * chunks, n * shard_rows, CHUNK), BF16),
             v((2, hops, 2, shard_rows, CHUNK), BF16), v((2, hops - 1, 2, shard_rows, CHUNK), BF16),
             v((n + 1, 8, CHUNK), F32),
-            dma((5,)), dma((2, 3)), dma((2, hops, 2)), dma((2, hops, 2)), dma((2, hops, 2)), dma((2, hops, 2)),
+            dma((5,)), dma((2, 3)), dma((2, hops, 2)), dma((2, hops, 2)), dma((2, hops, 2, 2)), dma((2, hops, 2, 2)),
             dma((n - 1,)), dma((n,)), dma((chunks // 2,)), dma((chunks,)),
         ],
         compiler_params=pltpu.CompilerParams(vmem_limit_bytes=VMEM_LIMIT, collective_id=0, has_side_effects=True),
@@ -384,77 +398,128 @@
     )(x, dy, wg, wu, wd)
 
 
-def adamw_body(n, factor_ref, g_ref, *refs):
+def adamw_update(factor, wmv, new, i, at, g):
+    g = g.astype(F32) * factor
+    w, m, v = (wmv[3 * k + i][at].astype(F32) for k in range(3))
+    m = 0.9 * m + 0.1 * g
+    v = 0.95 * v + 0.05 * g * g
+    w = w - 0.02 * (m * lax.rsqrt(v + 1e-8) + 0.1 * w)
+    for k, value in enumerate((w, m, v)):
+        new[3 * k + i][at] = value.astype(new[3 * k + i].dtype)
+
+
+def adamw_whole_body(n, factor_ref, g_ref, *refs):
     wmv, new = refs[:9], refs[-9:]
-    factor = factor_ref[0]
     rows_g = g_ref.shape[1] // n
     d = wmv[0].shape[1]
     rd, rf = d // n, CHUNK // n
-
-    def update(i, r, c, g):
-        g = g.astype(F32) * factor
-        w, m, v = (wmv[3 * k + i][0, r, c].astype(F32) for k in range(3))
-        m = 0.9 * m + 0.1 * g
-        v = 0.95 * v + 0.05 * g * g
-        w = w - 0.02 * (m * lax.rsqrt(v + 1e-8) + 0.1 * w)
-        for k, value in enumerate((w, m, v)):
-            new[3 * k + i][0, r, c] = value.astype(new[3 * k + i].dtype)
-
+    update = functools.partial(adamw_update, factor_ref[0], wmv, new)
     for r in range(n):
         at = r * rows_g
         for i in range(2):
-            update(i, slice(r * rd, (r + 1) * rd), slice(None), g_ref[0, at + i * rd : at + (i + 1) * rd, :])
+            update(i, (0, slice(r * rd, (r + 1) * rd)), g_ref[0, at + i * rd : at + (i + 1) * rd, :])
         for q in range(d // CHUNK):
-            update(2, slice(r * rf, (r + 1) * rf), slice(q * CHUNK, (q + 1) * CHUNK), g_ref[0, at + 2 * rd + q * rf : at + 2 * rd + (q + 1) * rf, :])
-
-
-def adamw(n, layer, factor, g, wmv, before):
+            update(2, (0, 0, slice(r * rf, (r + 1) * rf), slice(q * CHUNK, (q + 1) * CHUNK)), g_ref[0, at + 2 * rd + q * rf : at + 2 * rd + (q + 1) * rf, :])
+
+
+def adamw_shards_body(arrays, rs_ref, factor_ref, *refs):
+    gs, wmv, new = refs[:arrays], refs[arrays : arrays + 9], refs[-9:]
+    rd, rf = wmv[0].shape[1], wmv[2].shape[2]
+    d = wmv[2].shape[3]
+    update = functools.partial(adamw_update, factor_ref[0], wmv, new)
+    for k, g_ref in enumerate(gs):
+
+        @pl.when(pl.program_id(0) == k)
+        def _():
+            for c in range(g_ref.shape[0]):
+                for i in range(2):
+                    update(i, (0, slice(None), slice(c * CHUNK, (c + 1) * CHUNK)), g_ref[c, i * rd : (i + 1) * rd, :])
+                for q in range(d // CHUNK):
+                    update(2, (0, c, slice(None), slice(q * CHUNK, (q + 1) * CHUNK)), g_ref[c, 2 * rd + q * rf : 2 * rd + (q + 1) * rf, :])
+
+
+def adamw_call(name, body, grid, prefetch, gs, g_specs, blocks, wmv, before, part):
+    count = int(sum(w.size for w in wmv[:3]) * part)
+    first = len(prefetch) + 1 + len(gs) + 9
+    return pl.pallas_call(
+        body,
+        grid_spec=pltpu.PrefetchScalarGridSpec(
+            num_scalar_prefetch=len(prefetch) - 1,
+            grid=grid,
+            in_specs=[pl.BlockSpec(memory_space=pltpu.SMEM), *g_specs, *blocks, *[pl.BlockSpec(memory_space=pl.ANY)] * len(before)],
+            out_specs=blocks,
+        ),
+        out_shape=[jax.ShapeDtypeStruct(a.shape, a.dtype) for a in wmv],
+        input_output_aliases={first - 1 + i: i for i in range(len(before))},
+        compiler_params=pltpu.CompilerParams(vmem_limit_bytes=ADAMW_VMEM, dimension_semantics=("arbitrary",) * len(grid)),
+        cost_estimate=pl.CostEstimate(flops=400 * count, bytes_accessed=22 * count, transcendentals=count),
+        name=name,
+    )(*prefetch, *gs, *wmv, *before)
+
+
+def adamw_whole(n, layer, chunks, factor, g, wmv, before):
+    lo, hi = chunks
+    _, d, ff = wmv[0].shape
+    wide = pl.BlockSpec((1, d, CHUNK), lambda c: (layer, 0, c + lo))
+    tall = pl.BlockSpec((1, 1, CHUNK, d), lambda c: (layer, c + lo, 0, 0))
+    g_spec = pl.BlockSpec((1, g.shape[1], CHUNK), lambda c: (c + lo, 0, 0))
+    part = (hi - lo) * CHUNK / (ff * wmv[0].shape[0])
+    return adamw_call(f"adamw_{layer}_{lo}", functools.partial(adamw_whole_body, n), (hi - lo,), (factor,), (g,), [g_spec], [wide, wide, tall] * 3, wmv, before, part)
+
+
+def adamw_shards(n, layer, parts, steps, factor, wmv, before):
     layers, d, ff = wmv[0].shape
-    wide = pl.BlockSpec((1, d, CHUNK), lambda c: (layer, 0, c))
-    tall = pl.BlockSpec((1, CHUNK, d), lambda c: (layer, c, 0))
-    nine = [wide, wide, tall] * 3
-    count = layers * d * ff
-    return pl.pallas_call(
-        functools.partial(adamw_body, n),
-        grid=(ff // CHUNK,),
-        out_shape=[jax.ShapeDtypeStruct(a.shape, a.dtype) for a in wmv],
-        in_specs=[pl.BlockSpec(memory_space=pltpu.SMEM), pl.BlockSpec((1, g.shape[1], CHUNK), lambda c: (c, 0, 0)), *nine]
-        + [pl.BlockSpec(memory_space=pl.ANY)] * len(before),
-        out_specs=nine,
-        input_output_aliases={11 + i: i for i in range(len(before))},
-        compiler_params=pltpu.CompilerParams(vmem_limit_bytes=VMEM_LIMIT, dimension_semantics=("arbitrary",)),
-        cost_estimate=pl.CostEstimate(flops=60 * count, bytes_accessed=33 * count, transcendentals=3 * count),
-        name=f"adamw{layer}",
-    )(factor, g, *wmv, *before)
-
-
-def gathered(n, own):
+    chunks = ff // CHUNK
+    each = parts[0][2].shape[0] // steps
+    start = parts[1][1] - parts[0][1] if len(parts) > 1 else 0
+
+    def block(k, c):
+        return c + k * (start // each)
+
+    rs = jnp.stack([r for r, _, _ in parts]).astype(jnp.int32)
+    wide = pl.BlockSpec((1, d // n, each * CHUNK), lambda k, c, rs: (layer, rs[k], block(k, c)))
+    tall = pl.BlockSpec((1, each, CHUNK // n, d), lambda k, c, rs: (layer, block(k, c), rs[k], 0))
+    shape = (each, *parts[0][2].shape[1:])
+    g_specs = [pl.BlockSpec(shape, lambda k, c, rs, i=i: (jnp.where(k == i, c, jnp.where(k < i, 0, steps - 1)), 0, 0)) for i in range(len(parts))]
+    part = sum(g.shape[0] for _, _, g in parts) / (chunks * n * layers)
+    return adamw_call(f"adamw_{layer}_of_{len(parts)}", functools.partial(adamw_shards_body, len(parts)), (len(parts), steps), (rs, factor), [g for _, _, g in parts], g_specs, [wide, wide, tall] * 3, wmv, before, part)
+
+
+def solution(mesh):
+    n = mesh.shape[AXIS]
     hops = n // 2
-    half = own.shape[1] // 2
     right = [(i, (i + 1) % n) for i in range(n)]
     left = [(i, (i - 1) % n) for i in range(n)]
-    me = lax.axis_index(AXIS)
-    parts = {0: own}
-    a = b = own
-    for j in range(1, hops):
-        a, b = lax.ppermute(a, AXIS, right), lax.ppermute(b, AXIS, left)
-        parts[-j], parts[j] = a, b
-    a, b = lax.ppermute(a[:, :half], AXIS, right), lax.ppermute(b[:, half:], AXIS, left)
-    parts[hops] = jnp.concatenate([a, b], axis=1)
-    by_away = jnp.stack([parts[j] for j in range(1 - hops, hops + 1)])
-    return jnp.roll(by_away, me + 1 - hops, axis=0).transpose(1, 0, 2, 3).reshape(own.shape[0], -1, own.shape[2])
-
-
-def solution(mesh):
-    n = mesh.shape[AXIS]
 
     def step(x, dy, *wmv):
         full, own, squares = gradients_of(n, x, dy, *wmv[:3])
+        layers, d, ff = wmv[0].shape
+        chunks = ff // CHUNK
         count = sum(w.size for w in wmv[:3])
         factor = jnp.minimum(1.0, 0.5 * lax.rsqrt(jnp.sum(squares) / count + 1e-30)).reshape(1)
-        new = adamw(n, 1, factor, full, wmv, ())
-        new = adamw(n, 0, factor, gathered(n, own), wmv, new)
-        return tuple(new)
+        wmv = [a.reshape(layers, chunks, CHUNK, d) if i % 3 == 2 else a for i, a in enumerate(wmv)]
+        me = lax.axis_index(AXIS)
+
+        def of(away):
+            return lax.rem(me + away + n, n)
+
+        a, b = lax.ppermute(own, AXIS, right), lax.ppermute(own, AXIS, left)
+        most = chunks - 2
+        new = adamw_whole(n, 1, (0, most), factor, full, wmv, ())
+        a, b, *new = lax.optimization_barrier((a, b, *new))
+        here = [(of(0), 0, own), (of(-1), 0, a), (of(1), 0, b)]
+        for j in range(1, hops):
+            if j < hops - 1:
+                a2, b2 = lax.ppermute(a, AXIS, right), lax.ppermute(b, AXIS, left)
+            else:
+                a2, b2 = lax.ppermute(a[: chunks // 2], AXIS, right), lax.ppermute(b[chunks // 2 :], AXIS, left)
+            if j == 1:
+                new = adamw_whole(n, 1, (most, chunks), factor, full, wmv, new)
+            new = adamw_shards(n, 0, here, 4, factor, wmv, new)
+            a, b, *new = lax.optimization_barrier((a2, b2, *new))
+            here = [(of(-1 - j), 0, a), (of(1 + j), 0, b)]
+        new = adamw_shards(n, 0, [(of(hops), 0, a), (of(hops), chunks // 2, b)], 2, factor, wmv, new)
+        return tuple(new_one.reshape(layers, ff, d) if i % 3 == 2 else new_one for i, new_one in enumerate(new))
 
     return jax.shard_map(
         step,

time: 413 us -> 357 us (0.86)
  waiting for transfers between devices: 29.7 us -> 2.95 us
  Pallas kernels: 348 us -> 331 us
  local copies, waits for them, and re-layouts: 20.1 us -> 3.56 us
    pallas_call x1, Pallas kernels: 299 us -> 266 us  [gradients_of(): pl.pallas_call(functools.partial(gradients_body, n), out_shape=(jax.Shape...]
    ppermute x8, waiting for transfers between devices: 29.7 us -> 2.95 us  [the longest x4 2.94 us: step(): a2, b2 = (lax.ppermute(a, AXIS, right), lax.ppermute(b, AXIS, left))]
    pallas_call x2 -> x6, Pallas kernels: 49.3 us -> 65.3 us  [adamw_call(): pl.pallas_call(body, grid_spec=pltpu.PrefetchScalarGridSpec(num_scalar_pr...]
    unnamed x24 -> x0, local copies, waits for them, and re-layouts: 14.1 us -> none
  transfers between devices with their start and end apart: 8 -> 8, of which waited for: 3 -> 1; matrix products, arithmetic and copies ran while one was open for 3% -> 2% of each run, Pallas kernels for 6% -> 17%
where the time goes in v2:
time: 357 us; the launch traced here: 356 us
  Pallas kernels  331 us (93%)
  starting transfers between devices  13.2 us (4%)
  other arithmetic  3.75 us (1%)
    pallas_call x1, Pallas kernels, gradients_of(): pl.pallas_call(functools.partial(gradients_body, n), out_shape=(jax.Shape...  266 us
    pallas_call x6, Pallas kernels, adamw_call(): pl.pallas_call(body, grid_spec=pltpu.PrefetchScalarGridSpec(num_scalar_pr...  65.3 us
  transfers between devices with their start and end apart: 8, of which 1 were waited for; matrix products, arithmetic and copies ran while one was open for 2% of the time, Pallas kernels for 17%

profile of v2, /device:TPU:22, one launch (start us, length us, event | category | flops | bytes accessed | tf_op | source)
XLA Modules:
  0.0 355.9 jit_solution(6399841805879639639)
XLA Ops:
  0.6 265.5 %gradients.1 = (bf16[8,1536,256]{2,1,0:T(8,128)(2,1)}, bf16[8,192,256]{2,1,0:T(8,128)(2,1)}, f32[8,256]{1,0:T(8,128)}) custom-call(bf16[1,4096,512]{2,1,0:T(8,128)(2,1)} %x_hbm.1, bf16[1,4096,512]{2,1,0:T(8,128)(2,1)} %dy_hbm.1, bf16[2,512,2048]{2,1,0:T(8,128)(2,1)} %refs_2_.5, bf16[2,512,2048]{2,1,0:T(8,128)(2,1)} %refs_3_.11, bf16[2,2048,512]{2,1,0:T(8,128)(2,1)} %wd_hbm.1), custom_call_target="tpu_custom_call" | custom-call | tf_op jit(solution)/shard_map/gradients/pallas_call | solution.py:374
  266.2 0.1 collective-permute-start
  266.3 3.2 collective-permute-start.1
  269.5 1.3 reduce_sum.9
  271.5 18.6 %adamw_1_0.1 = (bf16[2,512,2048]{2,1,0:T(8,128)(2,1)}, bf16[2,512,2048]{2,1,0:T(8,128)(2,1)}, bf16[2,8,256,512]{3,2,1,0:T(8,128)(2,1)}, f32[2,512,2048]{2,1,0:T(...) custom-call(f32[1]{0:T(128)} %bitcast.1.factor_ref, ...), custom_call_target="tpu_custom_call" | custom-call | flops 943718400 | bytes 51904512 | tf_op jit(solution)/shard_map/adamw_1_0/pallas_call | solution.py:444
  290.1 0.0 collective-permute-done.refs_1_
  290.2 0.1 collective-permute-start.2
  290.3 3.2 collective-permute-start.3
  293.5 0.6 pad_add_fusion.1.rs_ref
  294.1 6.5 %adamw_1_6.1 = (bf16[2,512,2048]{2,1,0:T(8,128)(2,1)}, bf16[2,512,2048]{2,1,0:T(8,128)(2,1)}, bf16[2,8,256,512]{3,2,1,0:T(8,128)(2,1)}, f32[2,512,2048]{2,1,0:T(...) custom-call(f32[1]{0:T(128)} %bitcast.1.factor_ref, ...), custom_call_target="tpu_custom_call", output_to_operand_aliasing={{0}: (11, {}), {1}: (12, {}), {2}: (13, {}), {3}: (14, {}),... | custom-call | flops 314572800 | bytes 17301504 | tf_op jit(solution)/shard_map/adamw_1_6/pallas_call | solution.py:444
  300.6 13.9 %adamw_0_of_3.1 = (bf16[2,512,2048]{2,1,0:T(8,128)(2,1)}, bf16[2,512,2048]{2,1,0:T(8,128)(2,1)}, bf16[2,8,256,512]{3,2,1,0:T(8,128)(2,1)}, f32[2,512,2048]{2,1,0...) custom-call(s32[3]{0:T(128)} %pad_add_fusion.1.rs_ref, ...), custom_call_target="tpu_custom_call", output_to_operand_aliasing={{0}: (14, {}), {1}: (15, {}), {2}: (16, {}), {3}: (17, {}),... | custom-call | flops 471859200 | bytes 25952256 | tf_op jit(solution)/shard_map/adamw_0_of_3/pallas_call | solution.py:444
  314.6 0.0 collective-permute-done.3.refs_1_
  314.6 0.1 collective-permute-start.4
  314.7 3.2 collective-permute-start.5
  317.9 0.6 pad_add_fusion.2.rs_ref
  318.5 10.1 %adamw_0_of_2.3 = (bf16[2,512,2048]{2,1,0:T(8,128)(2,1)}, bf16[2,512,2048]{2,1,0:T(8,128)(2,1)}, bf16[2,8,256,512]{3,2,1,0:T(8,128)(2,1)}, f32[2,512,2048]{2,1,0...) custom-call(s32[2]{0:T(128)} %pad_add_fusion.2.rs_ref, ...), custom_call_target="tpu_custom_call", output_to_operand_aliasing={{0}: (13, {}), {1}: (14, {}), {2}: (15, {}), {3}: (16, {}),... | custom-call | flops 314572800 | bytes 17301504 | tf_op jit(solution)/shard_map/adamw_0_of_2/pallas_call | solution.py:444
  328.6 2.9 collective-permute-done.4.refs_0_
  331.5 1.8 slice.6
  333.3 1.8 slice.7
  335.1 3.2 collective-permute-start.7
  338.3 0.6 pad_add_fusion.rs_ref
  338.9 0.6 pad_add_fusion.3.rs_ref
  339.5 10.1 %adamw_0_of_2.4 = (bf16[2,512,2048]{2,1,0:T(8,128)(2,1)}, bf16[2,512,2048]{2,1,0:T(8,128)(2,1)}, bf16[2,8,256,512]{3,2,1,0:T(8,128)(2,1)}, f32[2,512,2048]{2,1,0...) custom-call(s32[2]{0:T(128)} %pad_add_fusion.3.rs_ref, ...), custom_call_target="tpu_custom_call", output_to_operand_aliasing={{0}: (13, {}), {1}: (14, {}), {2}: (15, {}), {3}: (16, {}),... | custom-call | flops 314572800 | bytes 17301504 | tf_op jit(solution)/shard_map/adamw_0_of_2/pallas_call | solution.py:444
  349.6 6.1 %adamw_0_of_2.5 = (bf16[2,512,2048]{2,1,0:T(8,128)(2,1)}, bf16[2,512,2048]{2,1,0:T(8,128)(2,1)}, bf16[2,8,256,512]{3,2,1,0:T(8,128)(2,1)}, f32[2,512,2048]{2,1,0...) custom-call(s32[2]{0:T(128)} %pad_add_fusion.rs_ref, ...), custom_call_target="tpu_custom_call", output_to_operand_aliasing={{0}: (13, {}), {1}: (14, {}), {2}: (15, {}), {3}: (16, {}),... | custom-call | flops 157286400 | bytes 8650752 | tf_op jit(solution)/shard_map/adamw_0_of_2/pallas_call | solution.py:444
  (6 shorter events, 0.0 us)
Async XLA Ops:
  266.2 24.0 %collective-permute-start = (bf16[8,192,256]{2,1,0:T(8,128)(2,1)}, bf16[8,192,256]{2,1,0:T(8,128)(2,1)}, u32[]{:S(2)}, u32[]{:S(2)}) collective-permute-start(bf16[8,192,256]{2,1,0:T(8,128)(2,1)} %get-tuple-element.111.refs_0_), channel_id=1, source_target_pairs={{0,1},{1,2},{2,3},{3,4},{4,5},{5,6},{6,7},{7,0},{8,9},{9,10},{10,1... | collective-permute-start | bytes 2359304 | tf_op jit(solution)/shard_map/ppermute | solution.py:506
  266.3 23.8 %collective-permute-start.1 = (bf16[8,192,256]{2,1,0:T(8,128)(2,1)}, bf16[8,192,256]{2,1,0:T(8,128)(2,1)}, u32[]{:S(2)}, u32[]{:S(2)}) collective-permute-start(bf16[8,192,256]{2,1,0:T(8,128)(2,1)} %get-tuple-element.111.refs_0_), channel_id=1, source_target_pairs={{0,7},{1,0},{2,1},{3,2},{4,3},{5,4},{6,5},{7,6},{8,15},{9,8},{10,9... | collective-permute-start | bytes 2359304 | tf_op jit(solution)/shard_map/ppermute | solution.py:506
  290.2 24.4 %collective-permute-start.2 = (bf16[8,192,256]{2,1,0:T(8,128)(2,1)}, bf16[8,192,256]{2,1,0:T(8,128)(2,1)}, u32[]{:S(2)}, u32[]{:S(2)}) collective-permute-start(bf16[8,192,256]{2,1,0:T(8,128)(2,1)} %collective-permute-done.refs_1_), channel_id=1, source_target_pairs={{0,1},{1,2},{2,3},{3,4},{4,5},{5,6},{6,7},{7,0},{8,9},{9,10},{10,1... | collective-permute-start | bytes 2359304 | tf_op jit(solution)/shard_map/ppermute | solution.py:513
  290.3 24.3 %collective-permute-start.3 = (bf16[8,192,256]{2,1,0:T(8,128)(2,1)}, bf16[8,192,256]{2,1,0:T(8,128)(2,1)}, u32[]{:S(2)}, u32[]{:S(2)}) collective-permute-start(bf16[8,192,256]{2,1,0:T(8,128)(2,1)} %collective-permute-done.1.refs_2_), channel_id=1, source_target_pairs={{0,7},{1,0},{2,1},{3,2},{4,3},{5,4},{6,5},{7,6},{8,15},{9,8},{10,9... | collective-permute-start | bytes 2359304 | tf_op jit(solution)/shard_map/ppermute | solution.py:513
  314.6 16.9 %collective-permute-start.4 = (bf16[8,192,256]{2,1,0:T(8,128)(2,1)}, bf16[8,192,256]{2,1,0:T(8,128)(2,1)}, u32[]{:S(2)}, u32[]{:S(2)}) collective-permute-start(bf16[8,192,256]{2,1,0:T(8,128)(2,1)} %collective-permute-done.2.refs_0_), channel_id=1, source_target_pairs={{0,1},{1,2},{2,3},{3,4},{4,5},{5,6},{6,7},{7,0},{8,9},{9,10},{10,1... | collective-permute-start | bytes 2359304 | tf_op jit(solution)/shard_map/ppermute | solution.py:513
  314.7 16.8 %collective-permute-start.5 = (bf16[8,192,256]{2,1,0:T(8,128)(2,1)}, bf16[8,192,256]{2,1,0:T(8,128)(2,1)}, u32[]{:S(2)}, u32[]{:S(2)}) collective-permute-start(bf16[8,192,256]{2,1,0:T(8,128)(2,1)} %collective-permute-done.3.refs_1_), channel_id=1, source_target_pairs={{0,7},{1,0},{2,1},{3,2},{4,3},{5,4},{6,5},{7,6},{8,15},{9,8},{10,9... | collective-permute-start | bytes 2359304 | tf_op jit(solution)/shard_map/ppermute | solution.py:513
  333.3 16.3 %collective-permute-start.6 = (bf16[4,192,256]{2,1,0:T(8,128)(2,1)}, bf16[4,192,256]{2,1,0:T(8,128)(2,1)}, u32[]{:S(2)}, u32[]{:S(2)}) collective-permute-start(bf16[4,192,256]{2,1,0:T(8,128)(2,1)} %slice.6), channel_id=1, source_target_pairs={{0,1},{1,2},{2,3},{3,4},{4,5},{5,6},{6,7},{7,0},{8,9},{9,10},{10,1... | collective-permute-start | bytes 1179656 | tf_op jit(solution)/shard_map/ppermute | solution.py:515
  335.1 14.5 %collective-permute-start.7 = (bf16[4,192,256]{2,1,0:T(8,128)(2,1)}, bf16[4,192,256]{2,1,0:T(8,128)(2,1)}, u32[]{:S(2)}, u32[]{:S(2)}) collective-permute-start(bf16[4,192,256]{2,1,0:T(8,128)(2,1)} %slice.7), channel_id=1, source_target_pairs={{0,7},{1,0},{2,1},{3,2},{4,3},{5,4},{6,5},{7,6},{8,15},{9,8},{10,9... | collective-permute-start | bytes 1179656 | tf_op jit(solution)/shard_map/ppermute | solution.py:515

commit v3 on v2

v3 whole, which is shorter than its diff:
```python
import functools

import jax
import jax.numpy as jnp
from jax import lax
from jax.experimental import pallas as pl
from jax.experimental.pallas import tpu as pltpu
from jax.sharding import PartitionSpec as P

F32, BF16 = jnp.float32, jnp.bfloat16
AXIS = "dp"
FTILE = 512
TILE = 1024
SPACING = 3
RING = 5
AG_SPACING = 6
CHUNK = 256
VMEM_LIMIT = 67043328
STEPS = 2


def mm(a, b):
    return jnp.dot(a, b, preferred_element_type=F32)


def mm_nt(a, b):
    return lax.dot_general(a, b, (((1,), (1,)), ((), ())), preferred_element_type=F32)


def mm_tn(a, b):
    return lax.dot_general(a, b, (((0,), (0,)), ((), ())), preferred_element_type=F32)


def sigmoid(x):
    return 0.5 * jnp.tanh(0.5 * x) + 0.5


def normed(wide):
    scale = lax.rsqrt(jnp.mean(wide * wide, -1, keepdims=True) + 1e-6)
    return (wide * scale).astype(BF16)


def gradients_body(n, x_hbm, dy_hbm, wg_hbm, wu_hbm, wd_hbm, full_hbm, own_lo_hbm, own_hi_hbm, factor_ref, me_ref, kept_hbm,
                   a0, a0t, a1, a1t, dy, h1, w0g, w0u, w0d, w1, w1d, act, dgu, piece, accd, accgu, grads, slots, sums, squares,
                   first_sem, w1_sem, w1d_sem, rs_send, rs_recv, ag_send, ag_recv, sq_send, sq_recv, full_sem, own_sem, keep_sem, piece_sem):
    tokens, d = h1.shape
    ff = w0d.shape[0]
    tiles, chunks = tokens // TILE, ff // CHUNK
    groups = 2 * chunks
    hops = n // 2
    shard_rows = grads.shape[1] // n
    half = shard_rows // 2
    me = lax.axis_index(AXIS)
    own_hbm = (own_lo_hbm, own_hi_hbm)
    to = (lax.rem(me + 1, n), lax.rem(me + n - 1, n))

    def rows(t):
        return pl.ds(pl.multiple_of(t * TILE, TILE), TILE)

    def frows(t):
        return pl.ds(pl.multiple_of(t * FTILE, FTILE), FTILE)

    def cols(c):
        return pl.ds(pl.multiple_of(c * CHUNK, CHUNK), CHUNK)

    def shard(away):
        return pl.multiple_of(lax.rem(me + away + n, n) * shard_rows, shard_rows)

    def place(g):
        return jnp.where(g < chunks, g, chunks + lax.rem(g - chunks + RING, RING))

    def remote(src, dst, send, recv, way):
        return pltpu.make_async_remote_copy(src_ref=src, dst_ref=dst, send_sem=send, recv_sem=recv, device_id={AXIS: to[way]}, device_id_type=pl.DeviceIdType.MESH)

    def rs_copy(s, g, way):
        p = lax.rem(g, 2)
        if s == 1:
            part = pl.ds(way * half, half)
            src, dst = grads.at[place(g), pl.ds(shard(hops) + way * half, half)], slots.at[way, 0, p, part]
        else:
            src, dst = sums.at[way, s - 2], slots.at[way, s - 1, p]
        return remote(src, dst, rs_send.at[way, s - 1, p], rs_recv.at[way, s - 1, p], way)

    def rs_add(s, g):
        p = lax.rem(g, 2)
        for way in range(2):
            own = grads[place(g), pl.ds(shard((1 - 2 * way) * (hops + 1 - s)), shard_rows)]
            if s == 2:
                here = slice(way * half, way * half + half)
                there = slice(half - way * half, shard_rows - way * half)
                sums[way, 0, there] = own[there]
                sums[way, 0, here] = (slots[way, 0, p, here].astype(F32) + own[here].astype(F32)).astype(BF16)
            else:
                sums[way, s - 2] = (slots[way, s - 2, p].astype(F32) + own.astype(F32)).astype(BF16)

    def rs_final(g):
        p = lax.rem(g, 2)
        mine = pl.ds(shard(0), shard_rows)
        total = slots[0, hops - 1, p].astype(F32) + slots[1, hops - 1, p].astype(F32) + grads[place(g), mine].astype(F32)
        total = total.astype(BF16)
        grads[place(g), mine] = total
        wide = total.astype(F32)
        squares[0] += jnp.sum((wide * wide).reshape(shard_rows // 8, 8, CHUNK), axis=0)

    def ag_copies(pair, j, whole):
        copies = []
        for b in range(2):
            for way in range(2):
                at = shard((2 * way - 1) * j)
                part = pl.ds(at, shard_rows) if whole else pl.ds(at + way * half, half)
                ref = grads.at[2 * pair + b, part]
                copies.append(remote(ref, ref, ag_send.at[way, j, b, lax.rem(pair, 2)], ag_recv.at[way, j, b, lax.rem(pair, 2)], way))
        return copies

    def full_copy(pair):
        return pltpu.make_async_copy(grads.at[pl.ds(2 * pair, 2)], full_hbm.at[pl.ds(2 * pair, 2)], full_sem.at[pair])

    def own_copy(g, part):
        return pltpu.make_async_copy(grads.at[place(g), pl.ds(shard(0), shard_rows)], own_hbm[part].at[g - chunks - part * (chunks // 2)], own_sem.at[g - chunks])

    def own_copies(g, f):
        for part in range(2):
            lo = chunks + part * (chunks // 2)

            @pl.when((g >= lo) & (g < lo + chunks // 2))
            def _():
                f(own_copy(g, part))

    pairs = chunks // 2

    total, ftiles = chunks * tiles, tokens // FTILE
    later = total + ftiles
    over = later + total

    ag_lag = -((2 - hops * SPACING) // tiles) + 1
    in_layer0 = (total - 2) // AG_SPACING + 1

    def tick(i):
        def group(s, f):
            step = i - (s - 1) * SPACING - (tiles - 1)
            last_layer = (step >= 0) & (step < total)
            first_layer = (step >= later) & (step < over)
            step = jnp.where(first_layer, step - ftiles, step)
            pl.when((last_layer | first_layer) & (lax.rem(step + tiles * groups, tiles) == 0))(functools.partial(f, step // tiles))

        def hop(s, g):
            if s > 1:
                for way in range(2):
                    rs_copy(s - 1, g, way).wait()
                rs_add(s, g)
            for way in range(2):
                rs_copy(s, g, way).start()

        def final(g):
            for way in range(2):
                rs_copy(hops, g, way).wait()
            rs_final(g)
            own_copies(g - 1, lambda copy: copy.wait())
            own_copies(g, lambda copy: copy.start())

        group(hops + 1, final)
        for s in range(hops, 0, -1):
            group(s, functools.partial(hop, s))

        chance = jnp.where(
            i < total, i // tiles - 1, jnp.where(
                i < later, chunks - 1 + (i - total) // 2, jnp.where(
                    i < over, chunks - 1 + ftiles // 2 + (i - later) // AG_SPACING, chunks - 1 + ftiles // 2 + in_layer0 + (i - over) // 2)))
        due = jnp.where(
            i < total, lax.rem(i, tiles) == 1, jnp.where(
                i < later, lax.rem(i - total, 2) == 1, jnp.where(
                    i < over, lax.rem(i - later, AG_SPACING) == 1, lax.rem(i - over, 2) == 1)))
        chance = chance - ag_lag

        @pl.when(due & (chance >= 0))
        def _():
            e = lax.rem(chance + 2 * groups, 2)
            u = (chance - 3 * e) // 2

            def gathering(u, f):
                pair, j = 2 * (u // hops) + e, lax.rem(u + 2 * hops, hops)
                for whole in (True, False):
                    pl.when((chance >= 3 * e) & (u >= 0) & (pair < pairs) & ((j < hops - 1) == whole))(functools.partial(f, pair, j, whole))

            def landed(pair, j, whole):
                for copy in ag_copies(pair, j, whole):
                    copy.wait()
                if not whole:
                    full_copy(pair).start()

            def pass_on(pair, j, whole):
                for copy in ag_copies(pair, j, whole):
                    copy.start()

            gathering(u - 1, landed)
            gathering(u, pass_on)

    def both(c):
        return pl.ds(pl.multiple_of(c * 2 * CHUNK, 2 * CHUNK), 2 * CHUNK)

    def w1_copies(c):
        return (
            pltpu.make_async_copy(wg_hbm.at[1, :, cols(c)], w1.at[:, pl.ds(c * 2 * CHUNK, CHUNK)], w1_sem.at[c, 0]),
            pltpu.make_async_copy(wu_hbm.at[1, :, cols(c)], w1.at[:, pl.ds(c * 2 * CHUNK + CHUNK, CHUNK)], w1_sem.at[c, 1]),
        )

    def w1d_copy(c):
        slot = lax.rem(c, 2)
        return pltpu.make_async_copy(wd_hbm.at[1, cols(c), :], w1d.at[slot], w1d_sem.at[slot])

    squares[...] = jnp.zeros_like(squares)
    barrier = pltpu.get_barrier_semaphore()
    for away in range(1, n):
        pl.semaphore_signal(barrier, inc=1, device_id={AXIS: lax.rem(me + away, n)}, device_id_type=pl.DeviceIdType.MESH)

    first = (
        pltpu.make_async_copy(x_hbm.at[0, pl.ds(0, 2 * FTILE)], h1.at[pl.ds(0, 2 * FTILE)], first_sem.at[0]),
        pltpu.make_async_copy(wg_hbm.at[0], w0g, first_sem.at[1]),
        pltpu.make_async_copy(wu_hbm.at[0], w0u, first_sem.at[2]),
        pltpu.make_async_copy(wd_hbm.at[0], w0d, first_sem.at[3]),
        pltpu.make_async_copy(x_hbm.at[0, pl.ds(2 * FTILE, tokens - 2 * FTILE)], h1.at[pl.ds(2 * FTILE, tokens - 2 * FTILE)], first_sem.at[4]),
        pltpu.make_async_copy(dy_hbm.at[0], dy, first_sem.at[5]),
    )
    for copy in first[:3]:
        copy.start()

    def norm0(t):
        a = normed(h1[frows(t), :].astype(F32))
        a0[frows(t), :] = a
        a0t[:, frows(t)] = a.T

    def expand(t):
        a = a0[frows(t), :]
        for c in range(chunks):
            s = pl.ds(c * CHUNK, CHUNK)
            gate, up = mm(a, w0g[:, s]), mm(a, w0u[:, s])
            piece[:, pl.ds(pl.multiple_of(lax.rem(t, 2) * ff + c * CHUNK, CHUNK), CHUNK)] = (gate * sigmoid(gate) * up).astype(BF16)

    def contract(t):
        out = mm(piece[:, pl.ds(pl.multiple_of(lax.rem(t, 2) * ff, CHUNK), ff)], w0d[...])
        h = (h1[frows(t), :].astype(F32) + out.astype(BF16).astype(F32)).astype(BF16)
        h1[frows(t), :] = h
        a = normed(h.astype(F32))
        a1[frows(t), :] = a
        a1t[:, frows(t)] = a.T

    first[0].wait()
    for copy in first[3:5]:
        copy.start()
    norm0(0)
    norm0(1)
    first[1].wait()
    first[2].wait()
    for copy in first[5:]:
        copy.start()
    for c in range(chunks):
        for copy in w1_copies(c):
            copy.start()
        if c < 2:
            w1d_copy(c).start()
    expand(0)
    accd[...] = jnp.zeros_like(accd)
    accgu[...] = jnp.zeros_like(accgu)
    first[3].wait()
    first[4].wait()

    def forward(t, _):
        contract(t)
        expand(t + 1)
        norm0(jnp.minimum(t + 2, ftiles - 1))
        return 0

    lax.fori_loop(0, ftiles - 1, forward, 0)
    contract(ftiles - 1)
    first[5].wait()
    pl.semaphore_wait(barrier, n - 1)

    def elementwise(gate, up, dact, b):
        s = sigmoid(gate)
        p = gate * s
        act[...] = (p * up).astype(BF16)
        dact = dact.astype(BF16).astype(F32)
        dgu[b, :, CHUNK:] = (dact * p).astype(BF16)
        dgu[b, :, :CHUNK] = (dact * up * (s + p * (1.0 - s))).astype(BF16)

    def finish(g):
        rd, rf, to_group = d // n, CHUNK // n, place(g)
        for r in range(n):
            at = r * shard_rows
            grads[to_group, at : at + rd, :] = accgu[r * rd : (r + 1) * rd, :CHUNK].astype(BF16)
            grads[to_group, at + rd : at + 2 * rd, :] = accgu[r * rd : (r + 1) * rd, CHUNK:].astype(BF16)
            for q in range(d // CHUNK):
                grads[to_group, at + 2 * rd + q * rf : at + 2 * rd + (q + 1) * rf, :] = accd[r * rf : (r + 1) * rf, q * CHUNK : (q + 1) * CHUNK].astype(BF16)
        accd[...] = jnp.zeros_like(accd)
        accgu[...] = jnp.zeros_like(accgu)

    def kept(i):
        c, t, b = i // tiles, lax.rem(i, tiles), lax.rem(i, 2)
        return pltpu.make_async_copy(dgu.at[b], kept_hbm.at[rows(t), both(c)], keep_sem.at[b])

    def front1(i, b):
        c, t = i // tiles, lax.rem(i, tiles)
        a = a1[rows(t), :]
        w = w1[:, both(c)]
        elementwise(mm(a, w[:, :CHUNK]), mm(a, w[:, CHUNK:]), mm_nt(dy[rows(t), :], w1d[lax.rem(c, 2)]), b)

    def layer1(i, _):
        c, t, b = i // tiles, lax.rem(i, tiles), lax.rem(i, 2)

        @pl.when((t == tiles - 1) & (c + 1 < chunks))
        def _():
            for copy in w1_copies(c + 1):
                copy.wait()
            w1d_copy(c + 1).wait()

        kept(i).start()

        @pl.when(i > 0)
        def _():
            kept(i - 1).wait()

        accgu[...] += mm(a1t[:, rows(t)], dgu[b])
        accd[...] += mm_tn(act[...], dy[rows(t), :])
        front1(jnp.minimum(i + 1, total - 1), 1 - b)

        @pl.when(t == tiles - 1)
        def _():
            finish(c)

            @pl.when(c + 2 < chunks)
            def _():
                w1d_copy(c + 2).start()

        tick(i)
        return 0

    for copy in w1_copies(0):
        copy.wait()
    w1d_copy(0).wait()
    front1(0, 0)
    lax.fori_loop(0, total, layer1, 0)
    kept(total - 1).wait()

    def piece_copy(t, place):
        return pltpu.make_async_copy(kept_hbm.at[frows(t), :], place, piece_sem.at[lax.rem(t, 2)])

    def through_norm(t):
        by_a = accgu[...].astype(BF16).astype(F32)
        wide = h1[frows(t), :].astype(F32)
        scale = lax.rsqrt(jnp.mean(wide * wide, -1, keepdims=True) + 1e-6)
        along = jnp.sum(by_a * wide, -1, keepdims=True) * (scale * scale * scale / d)
        through = (by_a * scale - wide * along).astype(BF16).astype(F32)
        dy[frows(t), :] = (dy[frows(t), :].astype(F32) + through).astype(BF16)

    def between(k, _):
        for half_way, (place, other) in enumerate(((piece, a1t), (a1t, piece))):
            t = 2 * k + half_way
            piece_copy(t, place).wait()

            @pl.when(t + 1 < ftiles)
            def _():
                piece_copy(t + 1, other).start()

            product = mm_nt(place[...], w1[...])
            if half_way:
                through_norm(t - 1)
            else:
                pl.when(k > 0)(lambda: through_norm(t - 1))
            accgu[...] = product
            tick(total + t)
        return 0

    piece_copy(0, piece).start()
    lax.fori_loop(0, ftiles // 2, between, 0)
    through_norm(ftiles - 1)
    accgu[...] = jnp.zeros_like(accgu)

    def front0(i, b):
        c, t = i // tiles, lax.rem(i, tiles)
        a = a0[rows(t), :]
        elementwise(mm(a, w0g[:, cols(c)]), mm(a, w0u[:, cols(c)]), mm_nt(dy[rows(t), :], w0d[cols(c), :]), b)

    def layer0(i, _):
        c, t, b = i // tiles, lax.rem(i, tiles), lax.rem(i, 2)
        accgu[...] += mm(a0t[:, rows(t)], dgu[b])
        accd[...] += mm_tn(act[...], dy[rows(t), :])
        front0(jnp.minimum(i + 1, total - 1), 1 - b)

        @pl.when(t == tiles - 1)
        def _():
            finish(chunks + c)

        tick(total + ftiles + i)
        return 0

    front0(0, 0)
    lax.fori_loop(0, total, layer0, 0)

    def sq_copy(away, mine):
        q = me if mine else lax.rem(me + away, n)
        return pltpu.make_async_remote_copy(
            src_ref=squares.at[0], dst_ref=squares.at[1 + q], send_sem=sq_send.at[away - 1], recv_sem=sq_recv.at[q],
            device_id={AXIS: lax.rem(me + away, n)}, device_id_type=pl.DeviceIdType.MESH)

    end = over - 1 + hops * SPACING
    chances = (ag_lag + 3 * e + 2 * hops * ((pairs + 1 - e) // 2) for e in range(2))
    last = max(end, over + 1 + 2 * (max(chances) - (chunks - 1 + ftiles // 2 + in_layer0)))

    def drain(i, _):
        tick(i)

        @pl.when(i == end)
        def _():
            for away in range(1, n):
                sq_copy(away, True).start()

        return 0

    lax.fori_loop(over, last + 1, drain, 0)
    for away in range(1, n):
        sq_copy(away, True).wait_send()
        sq_copy(away, False).wait_recv()
    squares[pl.ds(1 + me, 1)] = squares[0:1]
    everyone = squares[1]
    for q in range(1, n):
        everyone += squares[1 + q]
    mean = jnp.sum(jnp.sum(everyone, axis=1, keepdims=True), axis=0, keepdims=True) / (6 * d * ff)
    factor_ref[...] = jnp.broadcast_to(jnp.minimum(1.0, 0.5 * lax.rsqrt(mean + 1e-30)), factor_ref.shape)
    me_ref[0] = me
    for pair in range(pairs):
        full_copy(pair).wait()
    own_copy(groups - 1, 1).wait()


def gradients_of(n, x, dy, wg, wu, wd):
    _, tokens, d = x.shape
    _, ff, _ = wd.shape
    chunks, hops = ff // CHUNK, n // 2
    shard_rows = 3 * d // n
    v, dma = pltpu.VMEM, pltpu.SemaphoreType.DMA
    anyspace = pl.BlockSpec(memory_space=pl.ANY)
    return pl.pallas_call(
        functools.partial(gradients_body, n),
        out_shape=(
            jax.ShapeDtypeStruct((chunks, n * shard_rows, CHUNK), BF16),
            jax.ShapeDtypeStruct((chunks // 2, shard_rows, CHUNK), BF16),
            jax.ShapeDtypeStruct((chunks // 2, shard_rows, CHUNK), BF16),
            jax.ShapeDtypeStruct((8, 128), F32),
            jax.ShapeDtypeStruct((1,), jnp.int32),
            jax.ShapeDtypeStruct((tokens, 2 * ff), BF16),
        ),
        in_specs=[anyspace] * 5,
        out_specs=(anyspace, anyspace, anyspace, pl.BlockSpec(memory_space=pltpu.VMEM), pl.BlockSpec(memory_space=pltpu.SMEM), anyspace),
        scratch_shapes=[
            v((tokens, d), BF16), v((d, tokens), BF16), v((tokens, d), BF16), v((d, tokens), BF16),
            v((tokens, d), BF16), v((tokens, d), BF16),
            v((d, ff), BF16), v((d, ff), BF16), v((ff, d), BF16),
            v((d, 2 * ff), BF16), v((2, CHUNK, d), BF16),
            v((TILE, CHUNK), BF16), v((2, TILE, 2 * CHUNK), BF16), v((FTILE, 2 * ff), BF16),
            v((CHUNK, d), F32), v((d, 2 * CHUNK), F32),
            v((chunks + RING, n * shard_rows, CHUNK), BF16),
            v((2, hops, 2, shard_rows, CHUNK), BF16), v((2, hops - 1, shard_rows, CHUNK), BF16),
            v((n + 1, 8, CHUNK), F32),
            dma((6,)), dma((chunks, 2)), dma((2,)), dma((2, hops, 2)), dma((2, hops, 2)), dma((2, hops, 2, 2)), dma((2, hops, 2, 2)),
            dma((n - 1,)), dma((n,)), dma((chunks // 2,)), dma((chunks,)), dma((2,)), dma((2,)),
        ],
        compiler_params=pltpu.CompilerParams(vmem_limit_bytes=VMEM_LIMIT, collective_id=0, has_side_effects=True),
        name="gradients",
    )(x, dy, wg, wu, wd)


def adamw_update(factor, wmv, new, i, at, g):
    g = g.astype(F32) * factor
    w, m, v = (wmv[3 * k + i][at].astype(F32) for k in range(3))
    m = 0.9 * m + 0.1 * g
    v = 0.95 * v + 0.05 * g * g
    w = w - 0.02 * (m * lax.rsqrt(v + 1e-8) + 0.1 * w)
    for k, value in enumerate((w, m, v)):
        new[3 * k + i][at] = value.astype(new[3 * k + i].dtype)


def adamw_body(parts, me_ref, factor_ref, *refs):
    arrays = sum(parts)
    gs, wmv, new = refs[:arrays], refs[arrays : arrays + 9], refs[-9:]
    rd, rf = wmv[0].shape[1], wmv[2].shape[2]
    d = wmv[2].shape[3]
    step = pl.program_id(1)
    update = functools.partial(adamw_update, factor_ref[0:1, 0:1], wmv, new)
    for k, many in enumerate(parts):

        def shard(refs=gs[sum(parts[:k]) : sum(parts[: k + 1])]):
            c = 0
            for g_ref in refs:
                base = pl.multiple_of(step * rd, rd)
                for q in range(g_ref.shape[0]):
                    for i in range(2):
                        update(i, (0, slice(None), slice(c * CHUNK, (c + 1) * CHUNK)), g_ref[q, pl.ds(base + i * rd * STEPS, rd), :])
                    for p in range(d // CHUNK):
                        at = pl.multiple_of(2 * rd * STEPS + p * rf * STEPS + step * rf, rf)
                        update(2, (0, c, slice(None), slice(p * CHUNK, (p + 1) * CHUNK)), g_ref[q, pl.ds(at, rf), :])
                    c += 1

        if len(parts) == 1:
            shard()
        else:
            pl.when(pl.program_id(0) == k)(shard)


def adamw(name, n, layer, device, shards, parts, gs, g_specs, me, factor, wmv, before):
    layers, d, ff = wmv[0].shape
    chunks = ff // CHUNK
    rd, rf = d // n // STEPS, CHUNK // n // STEPS
    wide = pl.BlockSpec((1, rd, ff), lambda k, s, me: (layer, device(k, me[0]) * STEPS + s, 0))
    tall = pl.BlockSpec((1, chunks, rf, d), lambda k, s, me: (layer, 0, device(k, me[0]) * STEPS + s, 0))
    blocks = [wide, wide, tall] * 3
    count = 3 * d * ff * shards // n
    return pl.pallas_call(
        functools.partial(adamw_body, parts),
        grid_spec=pltpu.PrefetchScalarGridSpec(
            num_scalar_prefetch=1,
            grid=(shards, STEPS),
            in_specs=[pl.BlockSpec((8, 128), lambda k, s, me: (0, 0)), *g_specs, *blocks, *[pl.BlockSpec(memory_space=pl.ANY)] * len(before)],
            out_specs=blocks,
        ),
        out_shape=[jax.ShapeDtypeStruct(a.shape, a.dtype) for a in wmv],
        input_output_aliases={2 + len(gs) + 9 + i: i for i in range(len(before))},
        compiler_params=pltpu.CompilerParams(vmem_limit_bytes=VMEM_LIMIT, dimension_semantics=("arbitrary",) * 2),
        cost_estimate=pl.CostEstimate(flops=400 * count, bytes_accessed=22 * count, transcendentals=count),
        name=name,
    )(me, factor, *gs, *wmv, *before)


def adamw_gathered(n, layer, lo, hi, g, me, factor, wmv, before):
    spec = pl.BlockSpec((g.shape[0], g.shape[1] // n, CHUNK), lambda k, s, me: (0, lo + k, 0))
    return adamw(f"adamw_{layer}_{lo}", n, layer, lambda k, me: lo + k, hi - lo, (1,), (g,), [spec], me, factor, wmv, before)


def adamw_shards(n, layer, aways, arrays, me, factor, wmv, before):
    def device(k, me):
        away = aways[-1]
        for i, other in enumerate(aways[:-1]):
            away = jnp.where(k == i, other, away)
        return lax.rem(me + away + n, n)

    gs = [g for some in arrays for g in some]
    specs = [pl.BlockSpec(g.shape, lambda k, s, me: (0, 0, 0)) for g in gs]
    return adamw(f"adamw_{layer}_{len(aways)}_{n + aways[0]}", n, layer, device, len(aways), tuple(len(some) for some in arrays), gs, specs, me, factor, wmv, before)


def solution(mesh):
    n = mesh.shape[AXIS]
    hops = n // 2
    right = [(i, (i + 1) % n) for i in range(n)]
    left = [(i, (i - 1) % n) for i in range(n)]

    def step(x, dy, *wmv):
        full, *own, factor, me, _ = gradients_of(n, x, dy, *wmv[:3])
        layers, d, ff = wmv[0].shape
        wmv = [a.reshape(layers, ff // CHUNK, CHUNK, d) if i % 3 == 2 else a for i, a in enumerate(wmv)]

        def permuted(arrays, pairs):
            return [lax.ppermute(a, AXIS, pairs) for a in arrays]

        a, b = permuted(own, right), permuted(own, left)
        most = n - n // 4
        new = adamw_gathered(n, 1, 0, most, full, me, factor, wmv, ())
        (a, b), new = lax.optimization_barrier(((a, b), new))
        aways, arrays = (0, -1, 1), (own, a, b)
        for j in range(1, hops):
            a, b = (permuted(a, right), permuted(b, left)) if j < hops - 1 else (permuted(a[:1], right), permuted(b[1:], left))
            if j == 1:
                new = adamw_gathered(n, 1, most, n, full, me, factor, wmv, new)
            new = adamw_shards(n, 0, aways, arrays, me, factor, wmv, new)
            (a, b), new = lax.optimization_barrier(((a, b), new))
            aways, arrays = (-1 - j, 1 + j), (a, b)
        new = adamw_shards(n, 0, (hops,), (a + b,), me, factor, wmv, new)
        return tuple(new_one.reshape(layers, ff, d) if i % 3 == 2 else new_one for i, new_one in enumerate(new))

    return jax.shard_map(
        step,
        mesh=mesh,
        in_specs=(P(("rep", "dp"), None, None),) * 2 + (P(None, None, None),) * 9,
        out_specs=(P("rep", None, None),) * 9,
        check_vma=False,
    )
```

time: 357 us -> 339 us (0.950)
  Pallas kernels: 331 us -> 315 us
  starting transfers between devices: 13.2 us -> 18.1 us
  other arithmetic: 3.75 us -> 0 us
    pallas_call x1, Pallas kernels: 266 us -> 247 us  [gradients_of(): pl.pallas_call(functools.partial(gradients_body, n), out_shape=(jax.Shape...]
    ppermute x8 -> x14, starting transfers between devices: 13.2 us -> 18.1 us  [permuted(): return [lax.ppermute(a, AXIS, pairs) for a in arrays]]
  transfers between devices with their start and end apart: 8 -> 14, of which waited for: 1 -> 2; matrix products, arithmetic and copies ran while one was open for 2% -> 0% of each run, Pallas kernels for 17% -> 18%
where the time goes in v3:
time: 339 us
  Pallas kernels  315 us (93%)
  starting transfers between devices  18.1 us (5%)
  waiting for transfers between devices  4.84 us (1%)
    pallas_call x1, Pallas kernels, gradients_of(): pl.pallas_call(functools.partial(gradients_body, n), out_shape=(jax.Shape...  247 us
    pallas_call x6, Pallas kernels, adamw(): pl.pallas_call(functools.partial(adamw_body, parts), grid_spec=pltpu.Pref...  67.3 us
    ppermute x14, starting transfers between devices, permuted(): return [lax.ppermute(a, AXIS, pairs) for a in arrays]  18.1 us
  transfers between devices with their start and end apart: 14, of which 2 were waited for; matrix products, arithmetic and copies ran while one was open for 0% of the time, Pallas kernels for 18%

profile of v3, /device:TPU:22, one launch (start us, length us, event | category | flops | bytes accessed | tf_op | source)
XLA Modules:
  0.0 338.5 jit_solution(5593084695502244363)
XLA Ops:
  0.6 247.3 %gradients.1 = (bf16[8,1536,256]{2,1,0:T(8,128)(2,1)}, bf16[4,192,256]{2,1,0:T(8,128)(2,1)}, bf16[4,192,256]{2,1,0:T(8,128)(2,1)}, f32[8,128]{1,0:T(8,128)}, s32[1]{0:T(128)}, /*index=5*/bf16[4096,4096]{1,0:T(8,128)(2,1)}) custom-call(bf16[1,4096,512]{2,1,0:T(8,128)(2,1)} %x_hbm.1, bf16[1,4096,512]{2,1,0:T(8,128)(2,1)} %dy_hbm.1, ...), custom_call_target="tpu_custom_call" | custom-call | tf_op jit(solution)/shard_map/gradients/pallas_call | solution.py:442
  248.0 0.6 collective-permute-start.2
  248.5 1.5 collective-permute-start
  250.1 1.7 collective-permute-start.3
  251.8 0.3 collective-permute-start.1
  252.1 23.0 %adamw_1_0.1 = (bf16[2,512,2048]{2,1,0:T(8,128)(2,1)}, bf16[2,512,2048]{2,1,0:T(8,128)(2,1)}, bf16[2,8,256,512]{3,2,1,0:T(8,128)(2,1)}, f32[2,512,2048]{2,1,0:T(...) custom-call(s32[1]{0:T(128)} %get-tuple-element.118.me_ref, ...), custom_call_target="tpu_custom_call" | custom-call | flops 943718400 | bytes 51904512 | tf_op jit(solution)/shard_map/adamw_1_0/pallas_call | solution.py:517
  275.1 0.0 collective-permute-done.2.refs_4_
  275.1 0.7 collective-permute-start.4
  275.8 2.2 collective-permute-start.5
  278.0 1.0 collective-permute-start.6
  279.0 1.5 collective-permute-start.7
  280.5 8.4 %adamw_1_6.1 = (bf16[2,512,2048]{2,1,0:T(8,128)(2,1)}, bf16[2,512,2048]{2,1,0:T(8,128)(2,1)}, bf16[2,8,256,512]{3,2,1,0:T(8,128)(2,1)}, f32[2,512,2048]{2,1,0:T(...) custom-call(s32[1]{0:T(128)} %get-tuple-element.118.me_ref, ...), custom_call_target="tpu_custom_call", output_to_operand_aliasing={{0}: (12, {}), {1}: (13, {}), {2}: (14, {}), {3}: (15, {}),... | custom-call | flops 314572800 | bytes 17301504 | tf_op jit(solution)/shard_map/adamw_1_6/pallas_call | solution.py:517
  288.9 12.7 %adamw_0_3_8.1 = (bf16[2,512,2048]{2,1,0:T(8,128)(2,1)}, bf16[2,512,2048]{2,1,0:T(8,128)(2,1)}, bf16[2,8,256,512]{3,2,1,0:T(8,128)(2,1)}, f32[2,512,2048]{2,1,0:...) custom-call(s32[1]{0:T(128)} %get-tuple-element.118.me_ref, ...), custom_call_target="tpu_custom_call", output_to_operand_aliasing={{0}: (17, {}), {1}: (18, {}), {2}: (19, {}), {3}: (20, {}),... | custom-call | flops 471859200 | bytes 25952256 | tf_op jit(solution)/shard_map/adamw_0_3_8/pallas_call | solution.py:517
  301.7 0.9 collective-permute-start.8
  302.6 2.0 collective-permute-start.9
  304.6 1.2 collective-permute-start.10
  305.8 1.2 collective-permute-start.11
  307.0 9.0 %adamw_0_2_6.1 = (bf16[2,512,2048]{2,1,0:T(8,128)(2,1)}, bf16[2,512,2048]{2,1,0:T(8,128)(2,1)}, bf16[2,8,256,512]{3,2,1,0:T(8,128)(2,1)}, f32[2,512,2048]{2,1,0:...) custom-call(s32[1]{0:T(128)} %get-tuple-element.118.me_ref, ...), custom_call_target="tpu_custom_call", output_to_operand_aliasing={{0}: (15, {}), {1}: (16, {}), {2}: (17, {}), {3}: (18, {}),... | custom-call | flops 314572800 | bytes 17301504 | tf_op jit(solution)/shard_map/adamw_0_2_6/pallas_call | solution.py:517
  316.1 3.3 collective-permute-done.9.refs_1_
  319.4 1.5 collective-permute-done.11.refs_3_
  320.9 1.6 collective-permute-start.12
  322.4 1.7 collective-permute-start.13
  324.1 9.0 %adamw_0_2_5.1 = (bf16[2,512,2048]{2,1,0:T(8,128)(2,1)}, bf16[2,512,2048]{2,1,0:T(8,128)(2,1)}, bf16[2,8,256,512]{3,2,1,0:T(8,128)(2,1)}, f32[2,512,2048]{2,1,0:...) custom-call(s32[1]{0:T(128)} %get-tuple-element.118.me_ref, ...), custom_call_target="tpu_custom_call", output_to_operand_aliasing={{0}: (15, {}), {1}: (16, {}), {2}: (17, {}), {3}: (18, {}),... | custom-call | flops 314572800 | bytes 17301504 | tf_op jit(solution)/shard_map/adamw_0_2_5/pallas_call | solution.py:517
  333.2 5.2 %adamw_0_1_12.1 = (bf16[2,512,2048]{2,1,0:T(8,128)(2,1)}, bf16[2,512,2048]{2,1,0:T(8,128)(2,1)}, bf16[2,8,256,512]{3,2,1,0:T(8,128)(2,1)}, f32[2,512,2048]{2,1,0...) custom-call(s32[1]{0:T(128)} %get-tuple-element.118.me_ref, ...), custom_call_target="tpu_custom_call", output_to_operand_aliasing={{0}: (13, {}), {1}: (14, {}), {2}: (15, {}), {3}: (16, {}),... | custom-call | flops 157286400 | bytes 8650752 | tf_op jit(solution)/shard_map/adamw_0_1_12/pallas_call | solution.py:517
  (11 shorter events, 0.0 us)
Async XLA Ops:
  248.0 27.1 %collective-permute-start.2 = (bf16[4,192,256]{2,1,0:T(8,128)(2,1)}, bf16[4,192,256]{2,1,0:T(8,128)(2,1)}, u32[]{:S(2)}, u32[]{:S(2)}) collective-permute-start(bf16[4,192,256]{2,1,0:T(8,128)(2,1)} %get-tuple-element.120.refs_0_), channel_id=1, source_target_pairs={{0,7},{1,0},{2,1},{3,2},{4,3},{5,4},{6,5},{7,6},{8,15},{9,8},{10,9... | collective-permute-start | bytes 1179656 | tf_op jit(solution)/shard_map/ppermute | solution.py:562
  248.5 26.6 %collective-permute-start = (bf16[4,192,256]{2,1,0:T(8,128)(2,1)}, bf16[4,192,256]{2,1,0:T(8,128)(2,1)}, u32[]{:S(2)}, u32[]{:S(2)}) collective-permute-start(bf16[4,192,256]{2,1,0:T(8,128)(2,1)} %get-tuple-element.120.refs_0_), channel_id=1, source_target_pairs={{0,1},{1,2},{2,3},{3,4},{4,5},{5,6},{6,7},{7,0},{8,9},{9,10},{10,1... | collective-permute-start | bytes 1179656 | tf_op jit(solution)/shard_map/ppermute | solution.py:562
  250.1 25.0 %collective-permute-start.3 = (bf16[4,192,256]{2,1,0:T(8,128)(2,1)}, bf16[4,192,256]{2,1,0:T(8,128)(2,1)}, u32[]{:S(2)}, u32[]{:S(2)}) collective-permute-start(bf16[4,192,256]{2,1,0:T(8,128)(2,1)} %get-tuple-element.121.refs_1_), channel_id=1, source_target_pairs={{0,7},{1,0},{2,1},{3,2},{4,3},{5,4},{6,5},{7,6},{8,15},{9,8},{10,9... | collective-permute-start | bytes 1179656 | tf_op jit(solution)/shard_map/ppermute | solution.py:562
  251.8 23.3 %collective-permute-start.1 = (bf16[4,192,256]{2,1,0:T(8,128)(2,1)}, bf16[4,192,256]{2,1,0:T(8,128)(2,1)}, u32[]{:S(2)}, u32[]{:S(2)}) collective-permute-start(bf16[4,192,256]{2,1,0:T(8,128)(2,1)} %get-tuple-element.121.refs_1_), channel_id=1, source_target_pairs={{0,1},{1,2},{2,3},{3,4},{4,5},{5,6},{6,7},{7,0},{8,9},{9,10},{10,1... | collective-permute-start | bytes 1179656 | tf_op jit(solution)/shard_map/ppermute | solution.py:562
  275.1 26.5 %collective-permute-start.4 = (bf16[4,192,256]{2,1,0:T(8,128)(2,1)}, bf16[4,192,256]{2,1,0:T(8,128)(2,1)}, u32[]{:S(2)}, u32[]{:S(2)}) collective-permute-start(bf16[4,192,256]{2,1,0:T(8,128)(2,1)} %collective-permute-done.refs_2_), channel_id=1, source_target_pairs={{0,1},{1,2},{2,3},{3,4},{4,5},{5,6},{6,7},{7,0},{8,9},{9,10},{10,1... | collective-permute-start | bytes 1179656 | tf_op jit(solution)/shard_map/ppermute | solution.py:562
  275.8 25.9 %collective-permute-start.5 = (bf16[4,192,256]{2,1,0:T(8,128)(2,1)}, bf16[4,192,256]{2,1,0:T(8,128)(2,1)}, u32[]{:S(2)}, u32[]{:S(2)}) collective-permute-start(bf16[4,192,256]{2,1,0:T(8,128)(2,1)} %collective-permute-done.1.refs_3_), channel_id=1, source_target_pairs={{0,1},{1,2},{2,3},{3,4},{4,5},{5,6},{6,7},{7,0},{8,9},{9,10},{10,1... | collective-permute-start | bytes 1179656 | tf_op jit(solution)/shard_map/ppermute | solution.py:562
  278.0 23.6 %collective-permute-start.6 = (bf16[4,192,256]{2,1,0:T(8,128)(2,1)}, bf16[4,192,256]{2,1,0:T(8,128)(2,1)}, u32[]{:S(2)}, u32[]{:S(2)}) collective-permute-start(bf16[4,192,256]{2,1,0:T(8,128)(2,1)} %collective-permute-done.2.refs_4_), channel_id=1, source_target_pairs={{0,7},{1,0},{2,1},{3,2},{4,3},{5,4},{6,5},{7,6},{8,15},{9,8},{10,9... | collective-permute-start | bytes 1179656 | tf_op jit(solution)/shard_map/ppermute | solution.py:562
  279.0 22.6 %collective-permute-start.7 = (bf16[4,192,256]{2,1,0:T(8,128)(2,1)}, bf16[4,192,256]{2,1,0:T(8,128)(2,1)}, u32[]{:S(2)}, u32[]{:S(2)}) collective-permute-start(bf16[4,192,256]{2,1,0:T(8,128)(2,1)} %collective-permute-done.3.refs_5_), channel_id=1, source_target_pairs={{0,7},{1,0},{2,1},{3,2},{4,3},{5,4},{6,5},{7,6},{8,15},{9,8},{10,9... | collective-permute-start | bytes 1179656 | tf_op jit(solution)/shard_map/ppermute | solution.py:562
  301.7 14.4 %collective-permute-start.8 = (bf16[4,192,256]{2,1,0:T(8,128)(2,1)}, bf16[4,192,256]{2,1,0:T(8,128)(2,1)}, u32[]{:S(2)}, u32[]{:S(2)}) collective-permute-start(bf16[4,192,256]{2,1,0:T(8,128)(2,1)} %collective-permute-done.4.refs_0_), channel_id=1, source_target_pairs={{0,1},{1,2},{2,3},{3,4},{4,5},{5,6},{6,7},{7,0},{8,9},{9,10},{10,1... | collective-permute-start | bytes 1179656 | tf_op jit(solution)/shard_map/ppermute | solution.py:562
  302.6 16.8 %collective-permute-start.9 = (bf16[4,192,256]{2,1,0:T(8,128)(2,1)}, bf16[4,192,256]{2,1,0:T(8,128)(2,1)}, u32[]{:S(2)}, u32[]{:S(2)}) collective-permute-start(bf16[4,192,256]{2,1,0:T(8,128)(2,1)} %collective-permute-done.5.refs_1_), channel_id=1, source_target_pairs={{0,1},{1,2},{2,3},{3,4},{4,5},{5,6},{6,7},{7,0},{8,9},{9,10},{10,1... | collective-permute-start | bytes 1179656 | tf_op jit(solution)/shard_map/ppermute | solution.py:562
  304.6 14.8 %collective-permute-start.10 = (bf16[4,192,256]{2,1,0:T(8,128)(2,1)}, bf16[4,192,256]{2,1,0:T(8,128)(2,1)}, u32[]{:S(2)}, u32[]{:S(2)}) collective-permute-start(bf16[4,192,256]{2,1,0:T(8,128)(2,1)} %collective-permute-done.6.refs_2_), channel_id=1, source_target_pairs={{0,7},{1,0},{2,1},{3,2},{4,3},{5,4},{6,5},{7,6},{8,15},{9,8},{10,9... | collective-permute-start | bytes 1179656 | tf_op jit(solution)/shard_map/ppermute | solution.py:562
  305.8 15.1 %collective-permute-start.11 = (bf16[4,192,256]{2,1,0:T(8,128)(2,1)}, bf16[4,192,256]{2,1,0:T(8,128)(2,1)}, u32[]{:S(2)}, u32[]{:S(2)}) collective-permute-start(bf16[4,192,256]{2,1,0:T(8,128)(2,1)} %collective-permute-done.7.refs_3_), channel_id=1, source_target_pairs={{0,7},{1,0},{2,1},{3,2},{4,3},{5,4},{6,5},{7,6},{8,15},{9,8},{10,9... | collective-permute-start | bytes 1179656 | tf_op jit(solution)/shard_map/ppermute | solution.py:562
  320.9 12.3 %collective-permute-start.12 = (bf16[4,192,256]{2,1,0:T(8,128)(2,1)}, bf16[4,192,256]{2,1,0:T(8,128)(2,1)}, u32[]{:S(2)}, u32[]{:S(2)}) collective-permute-start(bf16[4,192,256]{2,1,0:T(8,128)(2,1)} %collective-permute-done.8.refs_0_), channel_id=1, source_target_pairs={{0,1},{1,2},{2,3},{3,4},{4,5},{5,6},{6,7},{7,0},{8,9},{9,10},{10,1... | collective-permute-start | bytes 1179656 | tf_op jit(solution)/shard_map/ppermute | solution.py:562
  322.4 10.7 %collective-permute-start.13 = (bf16[4,192,256]{2,1,0:T(8,128)(2,1)}, bf16[4,192,256]{2,1,0:T(8,128)(2,1)}, u32[]{:S(2)}, u32[]{:S(2)}) collective-permute-start(bf16[4,192,256]{2,1,0:T(8,128)(2,1)} %collective-permute-done.11.refs_3_), channel_id=1, source_target_pairs={{0,7},{1,0},{2,1},{3,2},{4,3},{5,4},{6,5},{7,6},{8,15},{9,8},{10,9... | collective-permute-start | bytes 1179656 | tf_op jit(solution)/shard_map/ppermute | solution.py:562

commit v4 on v3

--- a/solution.py
+++ b/solution.py
@@ -16,7 +16,6 @@
 AG_SPACING = 6
 CHUNK = 256
 VMEM_LIMIT = 67043328
-STEPS = 2
 
 
 def mm(a, b):
@@ -40,7 +39,7 @@
     return (wide * scale).astype(BF16)
 
 
-def gradients_body(n, x_hbm, dy_hbm, wg_hbm, wu_hbm, wd_hbm, full_hbm, own_lo_hbm, own_hi_hbm, factor_ref, me_ref, kept_hbm,
+def gradients_body(n, x_hbm, dy_hbm, wg_hbm, wu_hbm, wd_hbm, full_hbm, own_hbm, factor_ref, me_ref, kept_hbm,
                    a0, a0t, a1, a1t, dy, h1, w0g, w0u, w0d, w1, w1d, act, dgu, piece, accd, accgu, grads, slots, sums, squares,
                    first_sem, w1_sem, w1d_sem, rs_send, rs_recv, ag_send, ag_recv, sq_send, sq_recv, full_sem, own_sem, keep_sem, piece_sem):
     tokens, d = h1.shape
@@ -51,7 +50,6 @@
     shard_rows = grads.shape[1] // n
     half = shard_rows // 2
     me = lax.axis_index(AXIS)
-    own_hbm = (own_lo_hbm, own_hi_hbm)
     to = (lax.rem(me + 1, n), lax.rem(me + n - 1, n))
 
     def rows(t):
@@ -115,16 +113,8 @@
     def full_copy(pair):
         return pltpu.make_async_copy(grads.at[pl.ds(2 * pair, 2)], full_hbm.at[pl.ds(2 * pair, 2)], full_sem.at[pair])
 
-    def own_copy(g, part):
-        return pltpu.make_async_copy(grads.at[place(g), pl.ds(shard(0), shard_rows)], own_hbm[part].at[g - chunks - part * (chunks // 2)], own_sem.at[g - chunks])
-
-    def own_copies(g, f):
-        for part in range(2):
-            lo = chunks + part * (chunks // 2)
-
-            @pl.when((g >= lo) & (g < lo + chunks // 2))
-            def _():
-                f(own_copy(g, part))
+    def own_copy(g):
+        return pltpu.make_async_copy(grads.at[place(g), pl.ds(shard(0), shard_rows)], own_hbm.at[g - chunks], own_sem.at[g - chunks])
 
     pairs = chunks // 2
 
@@ -155,8 +145,8 @@
             for way in range(2):
                 rs_copy(hops, g, way).wait()
             rs_final(g)
-            own_copies(g - 1, lambda copy: copy.wait())
-            own_copies(g, lambda copy: copy.start())
+            pl.when(g > chunks)(lambda: own_copy(g - 1).wait())
+            pl.when(g >= chunks)(lambda: own_copy(g).start())
 
         group(hops + 1, final)
         for s in range(hops, 0, -1):
@@ -429,7 +419,7 @@
     me_ref[0] = me
     for pair in range(pairs):
         full_copy(pair).wait()
-    own_copy(groups - 1, 1).wait()
+    own_copy(groups - 1).wait()
 
 
 def gradients_of(n, x, dy, wg, wu, wd):
@@ -443,14 +433,13 @@
         functools.partial(gradients_body, n),
         out_shape=(
             jax.ShapeDtypeStruct((chunks, n * shard_rows, CHUNK), BF16),
-            jax.ShapeDtypeStruct((chunks // 2, shard_rows, CHUNK), BF16),
-            jax.ShapeDtypeStruct((chunks // 2, shard_rows, CHUNK), BF16),
+            jax.ShapeDtypeStruct((chunks, shard_rows, CHUNK), BF16),
             jax.ShapeDtypeStruct((8, 128), F32),
             jax.ShapeDtypeStruct((1,), jnp.int32),
             jax.ShapeDtypeStruct((tokens, 2 * ff), BF16),
         ),
         in_specs=[anyspace] * 5,
-        out_specs=(anyspace, anyspace, anyspace, pl.BlockSpec(memory_space=pltpu.VMEM), pl.BlockSpec(memory_space=pltpu.SMEM), anyspace),
+        out_specs=(anyspace, anyspace, pl.BlockSpec(memory_space=pltpu.VMEM), pl.BlockSpec(memory_space=pltpu.SMEM), anyspace),
         scratch_shapes=[
             v((tokens, d), BF16), v((d, tokens), BF16), v((tokens, d), BF16), v((d, tokens), BF16),
             v((tokens, d), BF16), v((tokens, d), BF16),
@@ -479,7 +468,7 @@
         new[3 * k + i][at] = value.astype(new[3 * k + i].dtype)
 
 
-def adamw_body(parts, me_ref, factor_ref, *refs):
+def adamw_body(parts, steps, me_ref, factor_ref, *refs):
     arrays = sum(parts)
     gs, wmv, new = refs[:arrays], refs[arrays : arrays + 9], refs[-9:]
     rd, rf = wmv[0].shape[1], wmv[2].shape[2]
@@ -494,9 +483,9 @@
                 base = pl.multiple_of(step * rd, rd)
                 for q in range(g_ref.shape[0]):
                     for i in range(2):
-                        update(i, (0, slice(None), slice(c * CHUNK, (c + 1) * CHUNK)), g_ref[q, pl.ds(base + i * rd * STEPS, rd), :])
+                        update(i, (0, slice(None), slice(c * CHUNK, (c + 1) * CHUNK)), g_ref[q, pl.ds(base + i * rd * steps, rd), :])
                     for p in range(d // CHUNK):
-                        at = pl.multiple_of(2 * rd * STEPS + p * rf * STEPS + step * rf, rf)
+                        at = pl.multiple_of(2 * rd * steps + p * rf * steps + step * rf, rf)
                         update(2, (0, c, slice(None), slice(p * CHUNK, (p + 1) * CHUNK)), g_ref[q, pl.ds(at, rf), :])
                     c += 1
 
@@ -509,16 +498,17 @@
 def adamw(name, n, layer, device, shards, parts, gs, g_specs, me, factor, wmv, before):
     layers, d, ff = wmv[0].shape
     chunks = ff // CHUNK
-    rd, rf = d // n // STEPS, CHUNK // n // STEPS
-    wide = pl.BlockSpec((1, rd, ff), lambda k, s, me: (layer, device(k, me[0]) * STEPS + s, 0))
-    tall = pl.BlockSpec((1, chunks, rf, d), lambda k, s, me: (layer, 0, device(k, me[0]) * STEPS + s, 0))
+    steps = 2 if shards == 1 else 1
+    rd, rf = d // n // steps, CHUNK // n // steps
+    wide = pl.BlockSpec((1, rd, ff), lambda k, s, me: (layer, device(k, me[0]) * steps + s, 0))
+    tall = pl.BlockSpec((1, chunks, rf, d), lambda k, s, me: (layer, 0, device(k, me[0]) * steps + s, 0))
     blocks = [wide, wide, tall] * 3
     count = 3 * d * ff * shards // n
     return pl.pallas_call(
-        functools.partial(adamw_body, parts),
+        functools.partial(adamw_body, parts, steps),
         grid_spec=pltpu.PrefetchScalarGridSpec(
             num_scalar_prefetch=1,
-            grid=(shards, STEPS),
+            grid=(shards, steps),
             in_specs=[pl.BlockSpec((8, 128), lambda k, s, me: (0, 0)), *g_specs, *blocks, *[pl.BlockSpec(memory_space=pl.ANY)] * len(before)],
             out_specs=blocks,
         ),
@@ -547,6 +537,24 @@
     return adamw(f"adamw_{layer}_{len(aways)}_{n + aways[0]}", n, layer, device, len(aways), tuple(len(some) for some in arrays), gs, specs, me, factor, wmv, before)
 
 
+def halves(a, b):
+    def copy(a_ref, b_ref, first_ref, second_ref):
+        first_ref[...] = a_ref[...]
+        second_ref[...] = b_ref[...]
+
+    half = (a.shape[0] // 2, *a.shape[1:])
+    zero = (0,) * (a.ndim - 1)
+    return pl.pallas_call(
+        copy,
+        grid=(1,),
+        out_shape=[jax.ShapeDtypeStruct(half, a.dtype)] * 2,
+        in_specs=[pl.BlockSpec(half, lambda k: (0, *zero)), pl.BlockSpec(half, lambda k: (1, *zero))],
+        out_specs=[pl.BlockSpec(half, lambda k: (0, *zero))] * 2,
+        compiler_params=pltpu.CompilerParams(vmem_limit_bytes=VMEM_LIMIT),
+        name="halves",
+    )(a, b)
+
+
 def solution(mesh):
     n = mesh.shape[AXIS]
     hops = n // 2
@@ -554,26 +562,28 @@
     left = [(i, (i - 1) % n) for i in range(n)]
 
     def step(x, dy, *wmv):
-        full, *own, factor, me, _ = gradients_of(n, x, dy, *wmv[:3])
+        full, own, factor, me, _ = gradients_of(n, x, dy, *wmv[:3])
         layers, d, ff = wmv[0].shape
-        wmv = [a.reshape(layers, ff // CHUNK, CHUNK, d) if i % 3 == 2 else a for i, a in enumerate(wmv)]
-
-        def permuted(arrays, pairs):
-            return [lax.ppermute(a, AXIS, pairs) for a in arrays]
-
-        a, b = permuted(own, right), permuted(own, left)
-        most = n - n // 4
+        chunks = ff // CHUNK
+        wmv = [a.reshape(layers, chunks, CHUNK, d) if i % 3 == 2 else a for i, a in enumerate(wmv)]
+
+        a, b = lax.ppermute(own, AXIS, right), lax.ppermute(own, AXIS, left)
+        most = n - n // 4 - 1
         new = adamw_gathered(n, 1, 0, most, full, me, factor, wmv, ())
         (a, b), new = lax.optimization_barrier(((a, b), new))
-        aways, arrays = (0, -1, 1), (own, a, b)
+        ready, some = (0,), (own,)
         for j in range(1, hops):
-            a, b = (permuted(a, right), permuted(b, left)) if j < hops - 1 else (permuted(a[:1], right), permuted(b[1:], left))
+            ready, some = ready + (-j, j), some + (a, b)
+            if j == hops - 1:
+                a, b = halves(a, b)
+            a, b = lax.ppermute(a, AXIS, right), lax.ppermute(b, AXIS, left)
             if j == 1:
                 new = adamw_gathered(n, 1, most, n, full, me, factor, wmv, new)
-            new = adamw_shards(n, 0, aways, arrays, me, factor, wmv, new)
-            (a, b), new = lax.optimization_barrier(((a, b), new))
-            aways, arrays = (-1 - j, 1 + j), (a, b)
-        new = adamw_shards(n, 0, (hops,), (a + b,), me, factor, wmv, new)
+            take = 1 if j == 1 else 4 if j == 2 else len(ready)
+            new = adamw_shards(n, 0, ready[:take], [(g,) for g in some[:take]], me, factor, wmv, new)
+            ready, some = ready[take:], some[take:]
+            (a, b), new, some = lax.optimization_barrier(((a, b), new, some))
+        new = adamw_shards(n, 0, (*ready, hops), [*[(g,) for g in some], (a, b)], me, factor, wmv, new)
         return tuple(new_one.reshape(layers, ff, d) if i % 3 == 2 else new_one for i, new_one in enumerate(new))
 
     return jax.shard_map(

time: 339 us -> 325 us (0.959)
  starting transfers between devices: 18.1 us -> 12 us
  waiting for transfers between devices: 4.84 us -> 0.02 us
    ppermute x14 -> x8, starting transfers between devices: 18.1 us -> 12 us  [the longest x6 9.89 us: step(): a, b = (lax.ppermute(a, AXIS, right), lax.ppermute(b, AXIS, left))]
    ppermute x14 -> x8, waiting for transfers between devices: 4.84 us -> 0.02 us  [the longest x6 0.02 us: step(): a, b = (lax.ppermute(a, AXIS, right), lax.ppermute(b, AXIS, left))]
    pallas_call x6 -> x7, Pallas kernels: 67.3 us -> 64.5 us  [the longest x6 62.4 us: adamw(): pl.pallas_call(functools.partial(adamw_body, parts, steps), grid_spec=plt...]
  transfers between devices with their start and end apart: 14 -> 8, of which waited for: 2 -> 0; matrix products, arithmetic and copies ran while one was open for 0% -> 0% of each run, Pallas kernels for 18% -> 18%
where the time goes in v4:
time: 325 us
  Pallas kernels  312 us (96%)
  starting transfers between devices  12 us (4%)
    pallas_call x1, Pallas kernels, gradients_of(): pl.pallas_call(functools.partial(gradients_body, n), out_shape=(jax.Shape...  247 us
    pallas_call x6, Pallas kernels, adamw(): pl.pallas_call(functools.partial(adamw_body, parts, steps), grid_spec=plt...  62.4 us
    ppermute x6, starting transfers between devices, step(): a, b = (lax.ppermute(a, AXIS, right), lax.ppermute(b, AXIS, left))  9.89 us
  transfers between devices with their start and end apart: 8, of which 0 were waited for; matrix products, arithmetic and copies ran while one was open for 0% of the time, Pallas kernels for 18%

profile of v4, /device:TPU:22, one launch (start us, length us, event | category | flops | bytes accessed | tf_op | source)
XLA Modules:
  0.0 324.7 jit_solution(531783615091210479)
XLA Ops:
  0.6 247.3 %gradients.1 = (bf16[8,1536,256]{2,1,0:T(8,128)(2,1)}, bf16[8,192,256]{2,1,0:T(8,128)(2,1)}, f32[8,128]{1,0:T(8,128)}, s32[1]{0:T(128)}, bf16[4096,4096]{1,0:T(8,128)(2,1)}) custom-call(bf16[1,4096,512]{2,1,0:T(8,128)(2,1)} %x_hbm.1, bf16[1,4096,512]{2,1,0:T(8,128)(2,1)} %dy_hbm.1, bf16[2,512,2048]{2,1,0:T(8,128)(2,1)} %refs_2_.9, ...), custom_call_target="tpu_custom_call" | custom-call | tf_op jit(solution)/shard_map/gradients/pallas_call | solution.py:432
  247.9 0.6 collective-permute-start.1
  248.5 1.6 collective-permute-start
  250.1 18.2 %adamw_1_0.1 = (bf16[2,512,2048]{2,1,0:T(8,128)(2,1)}, bf16[2,512,2048]{2,1,0:T(8,128)(2,1)}, bf16[2,8,256,512]{3,2,1,0:T(8,128)(2,1)}, f32[2,512,2048]{2,1,0:T(...) custom-call(s32[1]{0:T(128)} %get-tuple-element.115.me_ref, ...), custom_call_target="tpu_custom_call" | custom-call | flops 786432000 | bytes 43253760 | tf_op jit(solution)/shard_map/adamw_1_0/pallas_call | solution.py:507
  268.2 0.0 collective-permute-done.1.refs_1_
  268.3 0.0 collective-permute-done.refs_0_
  268.3 0.6 collective-permute-start.2
  268.9 2.7 collective-permute-start.3
  271.6 11.9 %adamw_1_5.1 = (bf16[2,512,2048]{2,1,0:T(8,128)(2,1)}, bf16[2,512,2048]{2,1,0:T(8,128)(2,1)}, bf16[2,8,256,512]{3,2,1,0:T(8,128)(2,1)}, f32[2,512,2048]{2,1,0:T(...) custom-call(s32[1]{0:T(128)} %get-tuple-element.115.me_ref, ...), custom_call_target="tpu_custom_call", output_to_operand_aliasing={{0}: (12, {}), {1}: (13, {}), {2}: (14, {}), {3}: (15, {}),... | custom-call | flops 471859200 | bytes 25952256 | tf_op jit(solution)/shard_map/adamw_1_5/pallas_call | solution.py:507
  283.5 5.2 %adamw_0_1_8.1 = (bf16[2,512,2048]{2,1,0:T(8,128)(2,1)}, bf16[2,512,2048]{2,1,0:T(8,128)(2,1)}, bf16[2,8,256,512]{3,2,1,0:T(8,128)(2,1)}, f32[2,512,2048]{2,1,0:...) custom-call(s32[1]{0:T(128)} %get-tuple-element.115.me_ref, ...), custom_call_target="tpu_custom_call", output_to_operand_aliasing={{0}: (12, {}), {1}: (13, {}), {2}: (14, {}), {3}: (15, {}),... | custom-call | flops 157286400 | bytes 8650752 | tf_op jit(solution)/shard_map/adamw_0_1_8/pallas_call | solution.py:507
  288.7 0.0 collective-permute-done.2.refs_2_
  288.7 0.0 collective-permute-done.3.refs_3_
  288.7 0.1 collective-permute-start.4
  288.8 3.2 collective-permute-start.5
  292.1 14.0 %adamw_0_4_7.1 = (bf16[2,512,2048]{2,1,0:T(8,128)(2,1)}, bf16[2,512,2048]{2,1,0:T(8,128)(2,1)}, bf16[2,8,256,512]{3,2,1,0:T(8,128)(2,1)}, f32[2,512,2048]{2,1,0:...) custom-call(s32[1]{0:T(128)} %get-tuple-element.115.me_ref, ...), custom_call_target="tpu_custom_call", output_to_operand_aliasing={{0}: (15, {}), {1}: (16, {}), {2}: (17, {}), {3}: (18, {}),... | custom-call | flops 629145600 | bytes 34603008 | tf_op jit(solution)/shard_map/adamw_0_4_7/pallas_call | solution.py:507
  306.1 0.0 collective-permute-done.4.a_ref.refs_0_
  306.1 0.0 collective-permute-done.5.b_ref.refs_1_
  306.1 2.0 halves.1
  308.2 0.0 collective-permute-start.6
  308.2 3.2 collective-permute-start.7
  311.4 7.9 %adamw_0_2_5.1 = (bf16[2,512,2048]{2,1,0:T(8,128)(2,1)}, bf16[2,512,2048]{2,1,0:T(8,128)(2,1)}, bf16[2,8,256,512]{3,2,1,0:T(8,128)(2,1)}, f32[2,512,2048]{2,1,0:...) custom-call(s32[1]{0:T(128)} %get-tuple-element.115.me_ref, ...), custom_call_target="tpu_custom_call", output_to_operand_aliasing={{0}: (13, {}), {1}: (14, {}), {2}: (15, {}), {3}: (16, {}),... | custom-call | flops 314572800 | bytes 17301504 | tf_op jit(solution)/shard_map/adamw_0_2_5/pallas_call | solution.py:507
  319.3 0.0 collective-permute-done.6.refs_0_
  319.3 0.0 collective-permute-done.7.refs_1_
  319.3 5.2 %adamw_0_1_12.1 = (bf16[2,512,2048]{2,1,0:T(8,128)(2,1)}, bf16[2,512,2048]{2,1,0:T(8,128)(2,1)}, bf16[2,8,256,512]{3,2,1,0:T(8,128)(2,1)}, f32[2,512,2048]{2,1,0...) custom-call(s32[1]{0:T(128)} %get-tuple-element.115.me_ref, ...), custom_call_target="tpu_custom_call", output_to_operand_aliasing={{0}: (13, {}), {1}: (14, {}), {2}: (15, {}), {3}: (16, {}),... | custom-call | flops 157286400 | bytes 8650752 | tf_op jit(solution)/shard_map/adamw_0_1_12/pallas_call | solution.py:507
Async XLA Ops:
  247.9 20.3 %collective-permute-start.1 = (bf16[8,192,256]{2,1,0:T(8,128)(2,1)}, bf16[8,192,256]{2,1,0:T(8,128)(2,1)}, u32[]{:S(2)}, u32[]{:S(2)}) collective-permute-start(bf16[8,192,256]{2,1,0:T(8,128)(2,1)} %get-tuple-element.117.refs_0_), channel_id=1, source_target_pairs={{0,7},{1,0},{2,1},{3,2},{4,3},{5,4},{6,5},{7,6},{8,15},{9,8},{10,9... | collective-permute-start | bytes 2359304 | tf_op jit(solution)/shard_map/ppermute | solution.py:570
  248.5 19.8 %collective-permute-start = (bf16[8,192,256]{2,1,0:T(8,128)(2,1)}, bf16[8,192,256]{2,1,0:T(8,128)(2,1)}, u32[]{:S(2)}, u32[]{:S(2)}) collective-permute-start(bf16[8,192,256]{2,1,0:T(8,128)(2,1)} %get-tuple-element.117.refs_0_), channel_id=1, source_target_pairs={{0,1},{1,2},{2,3},{3,4},{4,5},{5,6},{6,7},{7,0},{8,9},{9,10},{10,1... | collective-permute-start | bytes 2359304 | tf_op jit(solution)/shard_map/ppermute | solution.py:570
  268.3 20.4 %collective-permute-start.2 = (bf16[8,192,256]{2,1,0:T(8,128)(2,1)}, bf16[8,192,256]{2,1,0:T(8,128)(2,1)}, u32[]{:S(2)}, u32[]{:S(2)}) collective-permute-start(bf16[8,192,256]{2,1,0:T(8,128)(2,1)} %collective-permute-done.refs_0_), channel_id=1, source_target_pairs={{0,1},{1,2},{2,3},{3,4},{4,5},{5,6},{6,7},{7,0},{8,9},{9,10},{10,1... | collective-permute-start | bytes 2359304 | tf_op jit(solution)/shard_map/ppermute | solution.py:579
  268.9 19.8 %collective-permute-start.3 = (bf16[8,192,256]{2,1,0:T(8,128)(2,1)}, bf16[8,192,256]{2,1,0:T(8,128)(2,1)}, u32[]{:S(2)}, u32[]{:S(2)}) collective-permute-start(bf16[8,192,256]{2,1,0:T(8,128)(2,1)} %collective-permute-done.1.refs_1_), channel_id=1, source_target_pairs={{0,7},{1,0},{2,1},{3,2},{4,3},{5,4},{6,5},{7,6},{8,15},{9,8},{10,9... | collective-permute-start | bytes 2359304 | tf_op jit(solution)/shard_map/ppermute | solution.py:579
  288.7 17.4 %collective-permute-start.4 = (bf16[8,192,256]{2,1,0:T(8,128)(2,1)}, bf16[8,192,256]{2,1,0:T(8,128)(2,1)}, u32[]{:S(2)}, u32[]{:S(2)}) collective-permute-start(bf16[8,192,256]{2,1,0:T(8,128)(2,1)} %collective-permute-done.2.refs_2_), channel_id=1, source_target_pairs={{0,1},{1,2},{2,3},{3,4},{4,5},{5,6},{6,7},{7,0},{8,9},{9,10},{10,1... | collective-permute-start | bytes 2359304 | tf_op jit(solution)/shard_map/ppermute | solution.py:579
  288.8 17.3 %collective-permute-start.5 = (bf16[8,192,256]{2,1,0:T(8,128)(2,1)}, bf16[8,192,256]{2,1,0:T(8,128)(2,1)}, u32[]{:S(2)}, u32[]{:S(2)}) collective-permute-start(bf16[8,192,256]{2,1,0:T(8,128)(2,1)} %collective-permute-done.3.refs_3_), channel_id=1, source_target_pairs={{0,7},{1,0},{2,1},{3,2},{4,3},{5,4},{6,5},{7,6},{8,15},{9,8},{10,9... | collective-permute-start | bytes 2359304 | tf_op jit(solution)/shard_map/ppermute | solution.py:579
  308.2 11.2 %collective-permute-start.6 = (bf16[4,192,256]{2,1,0:T(8,128)(2,1)}, bf16[4,192,256]{2,1,0:T(8,128)(2,1)}, u32[]{:S(2)}, u32[]{:S(2)}) collective-permute-start(bf16[4,192,256]{2,1,0:T(8,128)(2,1)} %get-tuple-element.181), channel_id=1, source_target_pairs={{0,1},{1,2},{2,3},{3,4},{4,5},{5,6},{6,7},{7,0},{8,9},{9,10},{10,1... | collective-permute-start | bytes 1179656 | tf_op jit(solution)/shard_map/ppermute | solution.py:579
  308.2 11.2 %collective-permute-start.7 = (bf16[4,192,256]{2,1,0:T(8,128)(2,1)}, bf16[4,192,256]{2,1,0:T(8,128)(2,1)}, u32[]{:S(2)}, u32[]{:S(2)}) collective-permute-start(bf16[4,192,256]{2,1,0:T(8,128)(2,1)} %get-tuple-element.182), channel_id=1, source_target_pairs={{0,7},{1,0},{2,1},{3,2},{4,3},{5,4},{6,5},{7,6},{8,15},{9,8},{10,9... | collective-permute-start | bytes 1179656 | tf_op jit(solution)/shard_map/ppermute | solution.py:579

commit v5 on v4

--- a/solution.py
+++ b/solution.py
@@ -204,24 +204,23 @@
         pl.semaphore_signal(barrier, inc=1, device_id={AXIS: lax.rem(me + away, n)}, device_id_type=pl.DeviceIdType.MESH)
 
     first = (
-        pltpu.make_async_copy(x_hbm.at[0, pl.ds(0, 2 * FTILE)], h1.at[pl.ds(0, 2 * FTILE)], first_sem.at[0]),
-        pltpu.make_async_copy(wg_hbm.at[0], w0g, first_sem.at[1]),
-        pltpu.make_async_copy(wu_hbm.at[0], w0u, first_sem.at[2]),
-        pltpu.make_async_copy(wd_hbm.at[0], w0d, first_sem.at[3]),
-        pltpu.make_async_copy(x_hbm.at[0, pl.ds(2 * FTILE, tokens - 2 * FTILE)], h1.at[pl.ds(2 * FTILE, tokens - 2 * FTILE)], first_sem.at[4]),
-        pltpu.make_async_copy(dy_hbm.at[0], dy, first_sem.at[5]),
+        *(pltpu.make_async_copy(x_hbm.at[0, part], h1.at[part], first_sem.at[k]) for k, part in enumerate((pl.ds(0, FTILE), pl.ds(FTILE, FTILE), pl.ds(2 * FTILE, tokens - 2 * FTILE)))),
+        *(pltpu.make_async_copy(src.at[0, :, pl.ds(k * ff // 2, ff // 2)], dst.at[:, pl.ds(k * ff // 2, ff // 2)], first_sem.at[3 + 2 * k + q])
+          for k in range(2) for q, (src, dst) in enumerate(((wg_hbm, w0g), (wu_hbm, w0u)))),
+        pltpu.make_async_copy(wd_hbm.at[0], w0d, first_sem.at[7]),
+        pltpu.make_async_copy(dy_hbm.at[0], dy, first_sem.at[8]),
     )
-    for copy in first[:3]:
-        copy.start()
+    for k in (0, 3, 4, 1, 5, 6):
+        first[k].start()
 
     def norm0(t):
         a = normed(h1[frows(t), :].astype(F32))
         a0[frows(t), :] = a
         a0t[:, frows(t)] = a.T
 
-    def expand(t):
+    def expand(t, lo=0, hi=chunks):
         a = a0[frows(t), :]
-        for c in range(chunks):
+        for c in range(lo, hi):
             s = pl.ds(c * CHUNK, CHUNK)
             gate, up = mm(a, w0g[:, s]), mm(a, w0u[:, s])
             piece[:, pl.ds(pl.multiple_of(lax.rem(t, 2) * ff + c * CHUNK, CHUNK), CHUNK)] = (gate * sigmoid(gate) * up).astype(BF16)
@@ -235,24 +234,25 @@
         a1t[:, frows(t)] = a.T
 
     first[0].wait()
-    for copy in first[3:5]:
-        copy.start()
     norm0(0)
-    norm0(1)
-    first[1].wait()
-    first[2].wait()
-    for copy in first[5:]:
-        copy.start()
+    first[3].wait()
+    first[4].wait()
+    expand(0, 0, chunks // 2)
+    for k in (1, 5, 6):
+        first[k].wait()
+    for k in (7, 2, 8):
+        first[k].start()
     for c in range(chunks):
         for copy in w1_copies(c):
             copy.start()
         if c < 2:
             w1d_copy(c).start()
-    expand(0)
+    expand(0, chunks // 2, chunks)
+    norm0(1)
     accd[...] = jnp.zeros_like(accd)
     accgu[...] = jnp.zeros_like(accgu)
-    first[3].wait()
-    first[4].wait()
+    first[7].wait()
+    first[2].wait()
 
     def forward(t, _):
         contract(t)
@@ -262,7 +262,7 @@
 
     lax.fori_loop(0, ftiles - 1, forward, 0)
     contract(ftiles - 1)
-    first[5].wait()
+    first[8].wait()
     pl.semaphore_wait(barrier, n - 1)
 
     def elementwise(gate, up, dact, b):
@@ -450,7 +450,7 @@
             v((chunks + RING, n * shard_rows, CHUNK), BF16),
             v((2, hops, 2, shard_rows, CHUNK), BF16), v((2, hops - 1, shard_rows, CHUNK), BF16),
             v((n + 1, 8, CHUNK), F32),
-            dma((6,)), dma((chunks, 2)), dma((2,)), dma((2, hops, 2)), dma((2, hops, 2)), dma((2, hops, 2, 2)), dma((2, hops, 2, 2)),
+            dma((9,)), dma((chunks, 2)), dma((2,)), dma((2, hops, 2)), dma((2, hops, 2)), dma((2, hops, 2, 2)), dma((2, hops, 2, 2)),
             dma((n - 1,)), dma((n,)), dma((chunks // 2,)), dma((chunks,)), dma((2,)), dma((2,)),
         ],
         compiler_params=pltpu.CompilerParams(vmem_limit_bytes=VMEM_LIMIT, collective_id=0, has_side_effects=True),
@@ -468,61 +468,71 @@
         new[3 * k + i][at] = value.astype(new[3 * k + i].dtype)
 
 
-def adamw_body(parts, steps, me_ref, factor_ref, *refs):
+def adamw_gathered_body(n, factor_ref, g_ref, *refs):
+    wmv, new = refs[:9], refs[-9:]
+    rows_g = g_ref.shape[1] // n
+    d = wmv[0].shape[1]
+    rd, rf = d // n, CHUNK // n
+    update = functools.partial(adamw_update, factor_ref[0:1, 0:1], wmv, new)
+    for r in range(n):
+        at = r * rows_g
+        for i in range(2):
+            update(i, (0, slice(r * rd, (r + 1) * rd)), g_ref[0, at + i * rd : at + (i + 1) * rd, :])
+        for q in range(d // CHUNK):
+            update(2, (0, 0, slice(r * rf, (r + 1) * rf), slice(q * CHUNK, (q + 1) * CHUNK)), g_ref[0, at + 2 * rd + q * rf : at + 2 * rd + (q + 1) * rf, :])
+
+
+def adamw_shards_body(parts, steps, me_ref, factor_ref, *refs):
     arrays = sum(parts)
-    gs, wmv, new = refs[:arrays], refs[arrays : arrays + 9], refs[-9:]
+    gs, wmv, new, g_all = refs[:arrays], refs[arrays : arrays + 9], refs[-10:-1], refs[-1]
     rd, rf = wmv[0].shape[1], wmv[2].shape[2]
     d = wmv[2].shape[3]
     step = pl.program_id(1)
     update = functools.partial(adamw_update, factor_ref[0:1, 0:1], wmv, new)
     for k, many in enumerate(parts):
 
-        def shard(refs=gs[sum(parts[:k]) : sum(parts[: k + 1])]):
-            c = 0
-            for g_ref in refs:
-                base = pl.multiple_of(step * rd, rd)
-                for q in range(g_ref.shape[0]):
-                    for i in range(2):
-                        update(i, (0, slice(None), slice(c * CHUNK, (c + 1) * CHUNK)), g_ref[q, pl.ds(base + i * rd * steps, rd), :])
-                    for p in range(d // CHUNK):
-                        at = pl.multiple_of(2 * rd * steps + p * rf * steps + step * rf, rf)
-                        update(2, (0, c, slice(None), slice(p * CHUNK, (p + 1) * CHUNK)), g_ref[q, pl.ds(at, rf), :])
-                    c += 1
-
-        if len(parts) == 1:
-            shard()
-        else:
-            pl.when(pl.program_id(0) == k)(shard)
-
-
-def adamw(name, n, layer, device, shards, parts, gs, g_specs, me, factor, wmv, before):
-    layers, d, ff = wmv[0].shape
-    chunks = ff // CHUNK
-    steps = 2 if shards == 1 else 1
-    rd, rf = d // n // steps, CHUNK // n // steps
-    wide = pl.BlockSpec((1, rd, ff), lambda k, s, me: (layer, device(k, me[0]) * steps + s, 0))
-    tall = pl.BlockSpec((1, chunks, rf, d), lambda k, s, me: (layer, 0, device(k, me[0]) * steps + s, 0))
-    blocks = [wide, wide, tall] * 3
-    count = 3 * d * ff * shards // n
+        @pl.when((pl.program_id(0) == k) & (step == 0))
+        def _():
+            first = sum(parts[:k])
+            each = g_all.shape[0] // many
+            for j in range(many):
+                g_all[j * each : (j + 1) * each] = gs[first + j][...]
+
+    for c in range(g_all.shape[0]):
+        base = pl.multiple_of(step * rd, rd)
+        for i in range(2):
+            update(i, (0, slice(None), slice(c * CHUNK, (c + 1) * CHUNK)), g_all[c, pl.ds(base + i * rd * steps, rd), :])
+        for p in range(d // CHUNK):
+            at = pl.multiple_of(2 * rd * steps + p * rf * steps + step * rf, rf)
+            update(2, (0, c, slice(None), slice(p * CHUNK, (p + 1) * CHUNK)), g_all[c, pl.ds(at, rf), :])
+
+
+def adamw(name, body, grid, prefetch, gs, g_specs, blocks, scratch, share, factor, wmv, before):
+    count = int(share * sum(a.size for a in wmv[:3]))
     return pl.pallas_call(
-        functools.partial(adamw_body, parts, steps),
+        body,
         grid_spec=pltpu.PrefetchScalarGridSpec(
-            num_scalar_prefetch=1,
-            grid=(shards, steps),
-            in_specs=[pl.BlockSpec((8, 128), lambda k, s, me: (0, 0)), *g_specs, *blocks, *[pl.BlockSpec(memory_space=pl.ANY)] * len(before)],
+            num_scalar_prefetch=len(prefetch),
+            grid=grid,
+            in_specs=[pl.BlockSpec((8, 128), lambda *i: (0, 0)), *g_specs, *blocks, *[pl.BlockSpec(memory_space=pl.ANY)] * len(before)],
             out_specs=blocks,
+            scratch_shapes=scratch,
         ),
         out_shape=[jax.ShapeDtypeStruct(a.shape, a.dtype) for a in wmv],
-        input_output_aliases={2 + len(gs) + 9 + i: i for i in range(len(before))},
-        compiler_params=pltpu.CompilerParams(vmem_limit_bytes=VMEM_LIMIT, dimension_semantics=("arbitrary",) * 2),
+        input_output_aliases={len(prefetch) + 1 + len(gs) + 9 + i: i for i in range(len(before))},
+        compiler_params=pltpu.CompilerParams(vmem_limit_bytes=VMEM_LIMIT, dimension_semantics=("arbitrary",) * len(grid)),
         cost_estimate=pl.CostEstimate(flops=400 * count, bytes_accessed=22 * count, transcendentals=count),
         name=name,
-    )(me, factor, *gs, *wmv, *before)
-
-
-def adamw_gathered(n, layer, lo, hi, g, me, factor, wmv, before):
-    spec = pl.BlockSpec((g.shape[0], g.shape[1] // n, CHUNK), lambda k, s, me: (0, lo + k, 0))
-    return adamw(f"adamw_{layer}_{lo}", n, layer, lambda k, me: lo + k, hi - lo, (1,), (g,), [spec], me, factor, wmv, before)
+    )(*prefetch, factor, *gs, *wmv, *before)
+
+
+def adamw_gathered(n, layer, lo, hi, g, factor, wmv, before):
+    layers, d, ff = wmv[0].shape
+    wide = pl.BlockSpec((1, d, CHUNK), lambda c: (layer, 0, c + lo))
+    tall = pl.BlockSpec((1, 1, CHUNK, d), lambda c: (layer, c + lo, 0, 0))
+    g_spec = pl.BlockSpec((1, g.shape[1], CHUNK), lambda c: (c + lo, 0, 0))
+    share = (hi - lo) * CHUNK / (ff * layers)
+    return adamw(f"adamw_{layer}_{lo}", functools.partial(adamw_gathered_body, n), (hi - lo,), (), (g,), [g_spec], [wide, wide, tall] * 3, [], share, factor, wmv, before)
 
 
 def adamw_shards(n, layer, aways, arrays, me, factor, wmv, before):
@@ -532,9 +542,17 @@
             away = jnp.where(k == i, other, away)
         return lax.rem(me + away + n, n)
 
+    layers, d, ff = wmv[0].shape
+    chunks = ff // CHUNK
+    steps = 2 if len(aways) == 1 else 1
+    rd, rf = d // n // steps, CHUNK // n // steps
+    wide = pl.BlockSpec((1, rd, ff), lambda k, s, me: (layer, device(k, me[0]) * steps + s, 0))
+    tall = pl.BlockSpec((1, chunks, rf, d), lambda k, s, me: (layer, 0, device(k, me[0]) * steps + s, 0))
     gs = [g for some in arrays for g in some]
-    specs = [pl.BlockSpec(g.shape, lambda k, s, me: (0, 0, 0)) for g in gs]
-    return adamw(f"adamw_{layer}_{len(aways)}_{n + aways[0]}", n, layer, device, len(aways), tuple(len(some) for some in arrays), gs, specs, me, factor, wmv, before)
+    g_specs = [pl.BlockSpec(g.shape, lambda k, s, me: (0, 0, 0)) for g in gs]
+    body = functools.partial(adamw_shards_body, tuple(len(some) for some in arrays), steps)
+    scratch = [pltpu.VMEM((chunks, *gs[0].shape[1:]), BF16)]
+    return adamw(f"adamw_{layer}_{len(aways)}_{n + aways[0]}", body, (len(aways), steps), (me,), gs, g_specs, [wide, wide, tall] * 3, scratch, len(aways) / (n * layers), factor, wmv, before)
 
 
 def halves(a, b):
@@ -568,8 +586,8 @@
         wmv = [a.reshape(layers, chunks, CHUNK, d) if i % 3 == 2 else a for i, a in enumerate(wmv)]
 
         a, b = lax.ppermute(own, AXIS, right), lax.ppermute(own, AXIS, left)
-        most = n - n // 4 - 1
-        new = adamw_gathered(n, 1, 0, most, full, me, factor, wmv, ())
+        most = chunks - chunks // 4 - 1
+        new = adamw_gathered(n, 1, 0, most, full, factor, wmv, ())
         (a, b), new = lax.optimization_barrier(((a, b), new))
         ready, some = (0,), (own,)
         for j in range(1, hops):
@@ -578,7 +596,7 @@
                 a, b = halves(a, b)
             a, b = lax.ppermute(a, AXIS, right), lax.ppermute(b, AXIS, left)
             if j == 1:
-                new = adamw_gathered(n, 1, most, n, full, me, factor, wmv, new)
+                new = adamw_gathered(n, 1, most, chunks, full, factor, wmv, new)
             take = 1 if j == 1 else 4 if j == 2 else len(ready)
             new = adamw_shards(n, 0, ready[:take], [(g,) for g in some[:take]], me, factor, wmv, new)
             ready, some = ready[take:], some[take:]

time: 325 us -> 322 us (level)
    pallas_call x6, Pallas kernels: 62.4 us -> 58.9 us  [adamw(): pl.pallas_call(body, grid_spec=pltpu.PrefetchScalarGridSpec(num_scalar_pr...]
  transfers between devices with their start and end apart: 8 -> 8, of which waited for: 0 -> 0; matrix products, arithmetic and copies ran while one was open for 0% -> 0% of each run, Pallas kernels for 18% -> 17%
where the time goes in v5:
time: 322 us
  Pallas kernels  309 us (96%)
  starting transfers between devices  12 us (4%)
    pallas_call x1, Pallas kernels, gradients_of(): pl.pallas_call(functools.partial(gradients_body, n), out_shape=(jax.Shape...  248 us
    pallas_call x6, Pallas kernels, adamw(): pl.pallas_call(body, grid_spec=pltpu.PrefetchScalarGridSpec(num_scalar_pr...  58.9 us
    ppermute x6, starting transfers between devices, step(): a, b = (lax.ppermute(a, AXIS, right), lax.ppermute(b, AXIS, left))  9.89 us
  transfers between devices with their start and end apart: 8, of which 0 were waited for; matrix products, arithmetic and copies ran while one was open for 0% of the time, Pallas kernels for 17%

profile of v5, /device:TPU:22, one launch (start us, length us, event | category | flops | bytes accessed | tf_op | source)
XLA Modules:
  0.0 321.7 jit_solution(506190754784022541)
XLA Ops:
  0.6 247.8 %gradients.1 = (bf16[8,1536,256]{2,1,0:T(8,128)(2,1)}, bf16[8,192,256]{2,1,0:T(8,128)(2,1)}, f32[8,128]{1,0:T(8,128)}, s32[1]{0:T(128)}, bf16[4096,4096]{1,0:T(8,128)(2,1)}) custom-call(bf16[1,4096,512]{2,1,0:T(8,128)(2,1)} %x_hbm.1, bf16[1,4096,512]{2,1,0:T(8,128)(2,1)} %dy_hbm.1, bf16[2,512,2048]{2,1,0:T(8,128)(2,1)} %refs_2_.5, ...), custom_call_target="tpu_custom_call" | custom-call | tf_op jit(solution)/shard_map/gradients/pallas_call | solution.py:432
  248.4 0.6 collective-permute-start.1
  249.0 1.5 collective-permute-start
  250.6 16.4 %adamw_1_0.1 = (bf16[2,512,2048]{2,1,0:T(8,128)(2,1)}, bf16[2,512,2048]{2,1,0:T(8,128)(2,1)}, bf16[2,8,256,512]{3,2,1,0:T(8,128)(2,1)}, f32[2,512,2048]{2,1,0:T(...) custom-call(f32[8,128]{1,0:T(8,128)} %get-tuple-element.116.factor_r, ...), custom_call_target="tpu_custom_call" | custom-call | flops 786432000 | bytes 43253760 | tf_op jit(solution)/shard_map/adamw_1_0/pallas_call | solution.py:512
  266.9 0.0 collective-permute-done.1.refs_1_
  267.0 0.0 collective-permute-done.refs_0_
  267.0 0.6 collective-permute-start.2
  267.6 2.7 collective-permute-start.3
  270.3 10.3 %adamw_1_5.1 = (bf16[2,512,2048]{2,1,0:T(8,128)(2,1)}, bf16[2,512,2048]{2,1,0:T(8,128)(2,1)}, bf16[2,8,256,512]{3,2,1,0:T(8,128)(2,1)}, f32[2,512,2048]{2,1,0:T(...) custom-call(f32[8,128]{1,0:T(8,128)} %get-tuple-element.116.factor_r, ...), custom_call_target="tpu_custom_call", output_to_operand_aliasing={{0}: (11, {}), {1}: (12, {}), {2}: (13, {}), {3}: (14, {}),... | custom-call | flops 471859200 | bytes 25952256 | tf_op jit(solution)/shard_map/adamw_1_5/pallas_call | solution.py:512
  280.6 5.2 %adamw_0_1_8.1 = (bf16[2,512,2048]{2,1,0:T(8,128)(2,1)}, bf16[2,512,2048]{2,1,0:T(8,128)(2,1)}, bf16[2,8,256,512]{3,2,1,0:T(8,128)(2,1)}, f32[2,512,2048]{2,1,0:...) custom-call(s32[1]{0:T(128)} %get-tuple-element.115.me_ref, ...), custom_call_target="tpu_custom_call", output_to_operand_aliasing={{0}: (12, {}), {1}: (13, {}), {2}: (14, {}), {3}: (15, {}),... | custom-call | flops 157286400 | bytes 8650752 | tf_op jit(solution)/shard_map/adamw_0_1_8/pallas_call | solution.py:512
  285.9 0.0 collective-permute-done.2.refs_2_
  285.9 0.0 collective-permute-done.3.refs_3_
  285.9 0.1 collective-permute-start.4
  286.0 3.2 collective-permute-start.5
  289.2 14.0 %adamw_0_4_7.1 = (bf16[2,512,2048]{2,1,0:T(8,128)(2,1)}, bf16[2,512,2048]{2,1,0:T(8,128)(2,1)}, bf16[2,8,256,512]{3,2,1,0:T(8,128)(2,1)}, f32[2,512,2048]{2,1,0:...) custom-call(s32[1]{0:T(128)} %get-tuple-element.115.me_ref, ...), custom_call_target="tpu_custom_call", output_to_operand_aliasing={{0}: (15, {}), {1}: (16, {}), {2}: (17, {}), {3}: (18, {}),... | custom-call | flops 629145600 | bytes 34603008 | tf_op jit(solution)/shard_map/adamw_0_4_7/pallas_call | solution.py:512
  303.3 0.0 collective-permute-done.4.a_ref.refs_0_
  303.3 0.0 collective-permute-done.5.b_ref.refs_1_
  303.3 2.0 halves.1
  305.3 0.0 collective-permute-start.6
  305.3 3.2 %collective-permute-start.7 = (bf16[4,192,256]{2,1,0:T(8,128)(2,1)}, bf16[4,192,256]{2,1,0:T(8,128)(2,1)}, u32[]{:S(2)}, u32[]{:S(2)}) collective-permute-start(bf16[4,192,256]{2,1,0:T(8,128)(2,1)} %get-tuple-element.182), channel_id=1, source_target_pairs={{0,7},{1,0},{2,1},{3,2},{4,3},{5,4},{6,5},{7,6},{8,15},{9,8},{10,9... | collective-permute-start | bytes 1179656 | tf_op jit(solution)/shard_map/ppermute | solution.py:597
  308.6 7.7 %adamw_0_2_5.1 = (bf16[2,512,2048]{2,1,0:T(8,128)(2,1)}, bf16[2,512,2048]{2,1,0:T(8,128)(2,1)}, bf16[2,8,256,512]{3,2,1,0:T(8,128)(2,1)}, f32[2,512,2048]{2,1,0:...) custom-call(s32[1]{0:T(128)} %get-tuple-element.115.me_ref, ...), custom_call_target="tpu_custom_call", output_to_operand_aliasing={{0}: (13, {}), {1}: (14, {}), {2}: (15, {}), {3}: (16, {}),... | custom-call | flops 314572800 | bytes 17301504 | tf_op jit(solution)/shard_map/adamw_0_2_5/pallas_call | solution.py:512
  316.3 0.0 collective-permute-done.6.refs_0_
  316.3 0.0 collective-permute-done.7.refs_1_
  316.3 5.2 %adamw_0_1_12.1 = (bf16[2,512,2048]{2,1,0:T(8,128)(2,1)}, bf16[2,512,2048]{2,1,0:T(8,128)(2,1)}, bf16[2,8,256,512]{3,2,1,0:T(8,128)(2,1)}, f32[2,512,2048]{2,1,0...) custom-call(s32[1]{0:T(128)} %get-tuple-element.115.me_ref, ...), custom_call_target="tpu_custom_call", output_to_operand_aliasing={{0}: (13, {}), {1}: (14, {}), {2}: (15, {}), {3}: (16, {}),... | custom-call | flops 157286400 | bytes 8650752 | tf_op jit(solution)/shard_map/adamw_0_1_12/pallas_call | solution.py:512
Async XLA Ops:
  248.4 18.5 %collective-permute-start.1 = (bf16[8,192,256]{2,1,0:T(8,128)(2,1)}, bf16[8,192,256]{2,1,0:T(8,128)(2,1)}, u32[]{:S(2)}, u32[]{:S(2)}) collective-permute-start(bf16[8,192,256]{2,1,0:T(8,128)(2,1)} %get-tuple-element.117.refs_0_), channel_id=1, source_target_pairs={{0,7},{1,0},{2,1},{3,2},{4,3},{5,4},{6,5},{7,6},{8,15},{9,8},{10,9... | collective-permute-start | bytes 2359304 | tf_op jit(solution)/shard_map/ppermute | solution.py:588
  249.0 17.9 %collective-permute-start = (bf16[8,192,256]{2,1,0:T(8,128)(2,1)}, bf16[8,192,256]{2,1,0:T(8,128)(2,1)}, u32[]{:S(2)}, u32[]{:S(2)}) collective-permute-start(bf16[8,192,256]{2,1,0:T(8,128)(2,1)} %get-tuple-element.117.refs_0_), channel_id=1, source_target_pairs={{0,1},{1,2},{2,3},{3,4},{4,5},{5,6},{6,7},{7,0},{8,9},{9,10},{10,1... | collective-permute-start | bytes 2359304 | tf_op jit(solution)/shard_map/ppermute | solution.py:588
  267.0 18.9 %collective-permute-start.2 = (bf16[8,192,256]{2,1,0:T(8,128)(2,1)}, bf16[8,192,256]{2,1,0:T(8,128)(2,1)}, u32[]{:S(2)}, u32[]{:S(2)}) collective-permute-start(bf16[8,192,256]{2,1,0:T(8,128)(2,1)} %collective-permute-done.refs_0_), channel_id=1, source_target_pairs={{0,1},{1,2},{2,3},{3,4},{4,5},{5,6},{6,7},{7,0},{8,9},{9,10},{10,1... | collective-permute-start | bytes 2359304 | tf_op jit(solution)/shard_map/ppermute | solution.py:597
  267.6 18.3 %collective-permute-start.3 = (bf16[8,192,256]{2,1,0:T(8,128)(2,1)}, bf16[8,192,256]{2,1,0:T(8,128)(2,1)}, u32[]{:S(2)}, u32[]{:S(2)}) collective-permute-start(bf16[8,192,256]{2,1,0:T(8,128)(2,1)} %collective-permute-done.1.refs_1_), channel_id=1, source_target_pairs={{0,7},{1,0},{2,1},{3,2},{4,3},{5,4},{6,5},{7,6},{8,15},{9,8},{10,9... | collective-permute-start | bytes 2359304 | tf_op jit(solution)/shard_map/ppermute | solution.py:597
  285.9 17.4 %collective-permute-start.4 = (bf16[8,192,256]{2,1,0:T(8,128)(2,1)}, bf16[8,192,256]{2,1,0:T(8,128)(2,1)}, u32[]{:S(2)}, u32[]{:S(2)}) collective-permute-start(bf16[8,192,256]{2,1,0:T(8,128)(2,1)} %collective-permute-done.2.refs_2_), channel_id=1, source_target_pairs={{0,1},{1,2},{2,3},{3,4},{4,5},{5,6},{6,7},{7,0},{8,9},{9,10},{10,1... | collective-permute-start | bytes 2359304 | tf_op jit(solution)/shard_map/ppermute | solution.py:597
  286.0 17.3 %collective-permute-start.5 = (bf16[8,192,256]{2,1,0:T(8,128)(2,1)}, bf16[8,192,256]{2,1,0:T(8,128)(2,1)}, u32[]{:S(2)}, u32[]{:S(2)}) collective-permute-start(bf16[8,192,256]{2,1,0:T(8,128)(2,1)} %collective-permute-done.3.refs_3_), channel_id=1, source_target_pairs={{0,7},{1,0},{2,1},{3,2},{4,3},{5,4},{6,5},{7,6},{8,15},{9,8},{10,9... | collective-permute-start | bytes 2359304 | tf_op jit(solution)/shard_map/ppermute | solution.py:597
  305.3 10.9 %collective-permute-start.6 = (bf16[4,192,256]{2,1,0:T(8,128)(2,1)}, bf16[4,192,256]{2,1,0:T(8,128)(2,1)}, u32[]{:S(2)}, u32[]{:S(2)}) collective-permute-start(bf16[4,192,256]{2,1,0:T(8,128)(2,1)} %get-tuple-element.181), channel_id=1, source_target_pairs={{0,1},{1,2},{2,3},{3,4},{4,5},{5,6},{6,7},{7,0},{8,9},{9,10},{10,1... | collective-permute-start | bytes 1179656 | tf_op jit(solution)/shard_map/ppermute | solution.py:597
  305.3 10.9 %collective-permute-start.7 = (bf16[4,192,256]{2,1,0:T(8,128)(2,1)}, bf16[4,192,256]{2,1,0:T(8,128)(2,1)}, u32[]{:S(2)}, u32[]{:S(2)}) collective-permute-start(bf16[4,192,256]{2,1,0:T(8,128)(2,1)} %get-tuple-element.182), channel_id=1, source_target_pairs={{0,7},{1,0},{2,1},{3,2},{4,3},{5,4},{6,5},{7,6},{8,15},{9,8},{10,9... | collective-permute-start | bytes 1179656 | tf_op jit(solution)/shard_map/ppermute | solution.py:597

commit v6 on v5

--- a/solution.py
+++ b/solution.py
@@ -40,7 +40,7 @@
 
 
 def gradients_body(n, x_hbm, dy_hbm, wg_hbm, wu_hbm, wd_hbm, full_hbm, own_hbm, factor_ref, me_ref, kept_hbm,
-                   a0, a0t, a1, a1t, dy, h1, w0g, w0u, w0d, w1, w1d, act, dgu, piece, accd, accgu, grads, slots, sums, squares,
+                   a0, a0t, a1, a1t, dy, h1, w0g, w0u, w0d, w1, w1d, act, dgu, piece, accd, accgu, grads, slots, sums, squares, sent,
                    first_sem, w1_sem, w1d_sem, rs_send, rs_recv, ag_send, ag_recv, sq_send, sq_recv, full_sem, own_sem, keep_sem, piece_sem):
     tokens, d = h1.shape
     ff = w0d.shape[0]
@@ -98,7 +98,7 @@
         total = total.astype(BF16)
         grads[place(g), mine] = total
         wide = total.astype(F32)
-        squares[0] += jnp.sum((wide * wide).reshape(shard_rows // 8, 8, CHUNK), axis=0)
+        squares[...] += jnp.sum((wide * wide).reshape(shard_rows // 8, 8, CHUNK), axis=0)
 
     def ag_copies(pair, j, whole):
         copies = []
@@ -164,13 +164,14 @@
 
         @pl.when(due & (chance >= 0))
         def _():
-            e = lax.rem(chance + 2 * groups, 2)
-            u = (chance - 3 * e) // 2
+            odd_pair = (chance > 0) & (lax.rem(chance, 2) == 0)
+            e = jnp.where(odd_pair, 1, 0)
+            u = jnp.where(odd_pair, (chance - 2) // 2, (chance + 1) // 2)
 
             def gathering(u, f):
                 pair, j = 2 * (u // hops) + e, lax.rem(u + 2 * hops, hops)
                 for whole in (True, False):
-                    pl.when((chance >= 3 * e) & (u >= 0) & (pair < pairs) & ((j < hops - 1) == whole))(functools.partial(f, pair, j, whole))
+                    pl.when((u >= 0) & (pair < pairs) & ((j < hops - 1) == whole))(functools.partial(f, pair, j, whole))
 
             def landed(pair, j, whole):
                 for copy in ag_copies(pair, j, whole):
@@ -204,23 +205,24 @@
         pl.semaphore_signal(barrier, inc=1, device_id={AXIS: lax.rem(me + away, n)}, device_id_type=pl.DeviceIdType.MESH)
 
     first = (
-        *(pltpu.make_async_copy(x_hbm.at[0, part], h1.at[part], first_sem.at[k]) for k, part in enumerate((pl.ds(0, FTILE), pl.ds(FTILE, FTILE), pl.ds(2 * FTILE, tokens - 2 * FTILE)))),
-        *(pltpu.make_async_copy(src.at[0, :, pl.ds(k * ff // 2, ff // 2)], dst.at[:, pl.ds(k * ff // 2, ff // 2)], first_sem.at[3 + 2 * k + q])
-          for k in range(2) for q, (src, dst) in enumerate(((wg_hbm, w0g), (wu_hbm, w0u)))),
-        pltpu.make_async_copy(wd_hbm.at[0], w0d, first_sem.at[7]),
-        pltpu.make_async_copy(dy_hbm.at[0], dy, first_sem.at[8]),
+        pltpu.make_async_copy(x_hbm.at[0, pl.ds(0, 2 * FTILE)], h1.at[pl.ds(0, 2 * FTILE)], first_sem.at[0]),
+        pltpu.make_async_copy(wg_hbm.at[0], w0g, first_sem.at[1]),
+        pltpu.make_async_copy(wu_hbm.at[0], w0u, first_sem.at[2]),
+        pltpu.make_async_copy(wd_hbm.at[0], w0d, first_sem.at[3]),
+        pltpu.make_async_copy(x_hbm.at[0, pl.ds(2 * FTILE, tokens - 2 * FTILE)], h1.at[pl.ds(2 * FTILE, tokens - 2 * FTILE)], first_sem.at[4]),
+        pltpu.make_async_copy(dy_hbm.at[0], dy, first_sem.at[5]),
     )
-    for k in (0, 3, 4, 1, 5, 6):
-        first[k].start()
+    for copy in first[:3]:
+        copy.start()
 
     def norm0(t):
         a = normed(h1[frows(t), :].astype(F32))
         a0[frows(t), :] = a
         a0t[:, frows(t)] = a.T
 
-    def expand(t, lo=0, hi=chunks):
+    def expand(t):
         a = a0[frows(t), :]
-        for c in range(lo, hi):
+        for c in range(chunks):
             s = pl.ds(c * CHUNK, CHUNK)
             gate, up = mm(a, w0g[:, s]), mm(a, w0u[:, s])
             piece[:, pl.ds(pl.multiple_of(lax.rem(t, 2) * ff + c * CHUNK, CHUNK), CHUNK)] = (gate * sigmoid(gate) * up).astype(BF16)
@@ -234,25 +236,24 @@
         a1t[:, frows(t)] = a.T
 
     first[0].wait()
+    for copy in first[3:5]:
+        copy.start()
     norm0(0)
-    first[3].wait()
-    first[4].wait()
-    expand(0, 0, chunks // 2)
-    for k in (1, 5, 6):
-        first[k].wait()
-    for k in (7, 2, 8):
-        first[k].start()
+    norm0(1)
+    first[1].wait()
+    first[2].wait()
+    for copy in first[5:]:
+        copy.start()
     for c in range(chunks):
         for copy in w1_copies(c):
             copy.start()
         if c < 2:
             w1d_copy(c).start()
-    expand(0, chunks // 2, chunks)
-    norm0(1)
+    expand(0)
     accd[...] = jnp.zeros_like(accd)
     accgu[...] = jnp.zeros_like(accgu)
-    first[7].wait()
-    first[2].wait()
+    first[3].wait()
+    first[4].wait()
 
     def forward(t, _):
         contract(t)
@@ -262,7 +263,7 @@
 
     lax.fori_loop(0, ftiles - 1, forward, 0)
     contract(ftiles - 1)
-    first[8].wait()
+    first[5].wait()
     pl.semaphore_wait(barrier, n - 1)
 
     def elementwise(gate, up, dact, b):
@@ -389,11 +390,11 @@
     def sq_copy(away, mine):
         q = me if mine else lax.rem(me + away, n)
         return pltpu.make_async_remote_copy(
-            src_ref=squares.at[0], dst_ref=squares.at[1 + q], send_sem=sq_send.at[away - 1], recv_sem=sq_recv.at[q],
+            src_ref=sent.at[0], dst_ref=sent.at[1 + q], send_sem=sq_send.at[away - 1], recv_sem=sq_recv.at[q],
             device_id={AXIS: lax.rem(me + away, n)}, device_id_type=pl.DeviceIdType.MESH)
 
     end = over - 1 + hops * SPACING
-    chances = (ag_lag + 3 * e + 2 * hops * ((pairs + 1 - e) // 2) for e in range(2))
+    chances = (ag_lag + 2 * hops * ((pairs + 1) // 2) - 1, ag_lag + 2 * hops * (pairs // 2) + 2)
     last = max(end, over + 1 + 2 * (max(chances) - (chunks - 1 + ftiles // 2 + in_layer0)))
 
     def drain(i, _):
@@ -401,6 +402,7 @@
 
         @pl.when(i == end)
         def _():
+            sent[0] = jnp.sum(squares[...], axis=0, keepdims=True)
             for away in range(1, n):
                 sq_copy(away, True).start()
 
@@ -410,11 +412,11 @@
     for away in range(1, n):
         sq_copy(away, True).wait_send()
         sq_copy(away, False).wait_recv()
-    squares[pl.ds(1 + me, 1)] = squares[0:1]
-    everyone = squares[1]
+    sent[pl.ds(1 + me, 1)] = sent[0:1]
+    everyone = sent[1]
     for q in range(1, n):
-        everyone += squares[1 + q]
-    mean = jnp.sum(jnp.sum(everyone, axis=1, keepdims=True), axis=0, keepdims=True) / (6 * d * ff)
+        everyone += sent[1 + q]
+    mean = jnp.sum(everyone, axis=1, keepdims=True) / (6 * d * ff)
     factor_ref[...] = jnp.broadcast_to(jnp.minimum(1.0, 0.5 * lax.rsqrt(mean + 1e-30)), factor_ref.shape)
     me_ref[0] = me
     for pair in range(pairs):
@@ -449,8 +451,8 @@
             v((CHUNK, d), F32), v((d, 2 * CHUNK), F32),
             v((chunks + RING, n * shard_rows, CHUNK), BF16),
             v((2, hops, 2, shard_rows, CHUNK), BF16), v((2, hops - 1, shard_rows, CHUNK), BF16),
-            v((n + 1, 8, CHUNK), F32),
-            dma((9,)), dma((chunks, 2)), dma((2,)), dma((2, hops, 2)), dma((2, hops, 2)), dma((2, hops, 2, 2)), dma((2, hops, 2, 2)),
+            v((8, CHUNK), F32), v((n + 1, 1, CHUNK), F32),
+            dma((6,)), dma((chunks, 2)), dma((2,)), dma((2, hops, 2)), dma((2, hops, 2)), dma((2, hops, 2, 2)), dma((2, hops, 2, 2)),
             dma((n - 1,)), dma((n,)), dma((chunks // 2,)), dma((chunks,)), dma((2,)), dma((2,)),
         ],
         compiler_params=pltpu.CompilerParams(vmem_limit_bytes=VMEM_LIMIT, collective_id=0, has_side_effects=True),

time: 322 us -> 324 us (level)
  transfers between devices with their start and end apart: 8 -> 8, of which waited for: 0 -> 1; matrix products, arithmetic and copies ran while one was open for 0% -> 0% of each run, Pallas kernels for 17% -> 17%
where the time goes in v6:
time: 324 us
  Pallas kernels  310 us (96%)
  starting transfers between devices  12.5 us (4%)
    pallas_call x1, Pallas kernels, gradients_of(): pl.pallas_call(functools.partial(gradients_body, n), out_shape=(jax.Shape...  249 us
    pallas_call x6, Pallas kernels, adamw(): pl.pallas_call(body, grid_spec=pltpu.PrefetchScalarGridSpec(num_scalar_pr...  58.9 us
    ppermute x6, starting transfers between devices, step(): a, b = (lax.ppermute(a, AXIS, right), lax.ppermute(b, AXIS, left))  9.8 us
  transfers between devices with their start and end apart: 8, of which 1 were waited for; matrix products, arithmetic and copies ran while one was open for 0% of the time, Pallas kernels for 17%

profile of v6, /device:TPU:22, one launch (start us, length us, event | category | flops | bytes accessed | tf_op | source)
XLA Modules:
  0.0 323.6 jit_solution(17447348472045935636)
XLA Ops:
  0.6 248.8 %gradients.1 = (bf16[8,1536,256]{2,1,0:T(8,128)(2,1)}, bf16[8,192,256]{2,1,0:T(8,128)(2,1)}, f32[8,128]{1,0:T(8,128)}, s32[1]{0:T(128)}, bf16[4096,4096]{1,0:T(8,128)(2,1)}) custom-call(bf16[1,4096,512]{2,1,0:T(8,128)(2,1)} %x_hbm.1, bf16[1,4096,512]{2,1,0:T(8,128)(2,1)} %dy_hbm.1, bf16[2,512,2048]{2,1,0:T(8,128)(2,1)} %refs_2_.5, ...), custom_call_target="tpu_custom_call" | custom-call | tf_op jit(solution)/shard_map/gradients/pallas_call | solution.py:434
  249.4 2.7 collective-permute-start.1
  252.1 0.0 collective-permute-start
  252.1 16.4 %adamw_1_0.1 = (bf16[2,512,2048]{2,1,0:T(8,128)(2,1)}, bf16[2,512,2048]{2,1,0:T(8,128)(2,1)}, bf16[2,8,256,512]{3,2,1,0:T(8,128)(2,1)}, f32[2,512,2048]{2,1,0:T(...) custom-call(f32[8,128]{1,0:T(8,128)} %get-tuple-element.116.factor_r, ...), custom_call_target="tpu_custom_call" | custom-call | flops 786432000 | bytes 43253760 | tf_op jit(solution)/shard_map/adamw_1_0/pallas_call | solution.py:514
  268.5 0.0 collective-permute-done.1.refs_1_
  268.5 0.5 collective-permute-done.refs_0_
  269.0 0.5 collective-permute-start.2
  269.5 2.7 collective-permute-start.3
  272.2 10.3 %adamw_1_5.1 = (bf16[2,512,2048]{2,1,0:T(8,128)(2,1)}, bf16[2,512,2048]{2,1,0:T(8,128)(2,1)}, bf16[2,8,256,512]{3,2,1,0:T(8,128)(2,1)}, f32[2,512,2048]{2,1,0:T(...) custom-call(f32[8,128]{1,0:T(8,128)} %get-tuple-element.116.factor_r, ...), custom_call_target="tpu_custom_call", output_to_operand_aliasing={{0}: (11, {}), {1}: (12, {}), {2}: (13, {}), {3}: (14, {}),... | custom-call | flops 471859200 | bytes 25952256 | tf_op jit(solution)/shard_map/adamw_1_5/pallas_call | solution.py:514
  282.6 5.2 %adamw_0_1_8.1 = (bf16[2,512,2048]{2,1,0:T(8,128)(2,1)}, bf16[2,512,2048]{2,1,0:T(8,128)(2,1)}, bf16[2,8,256,512]{3,2,1,0:T(8,128)(2,1)}, f32[2,512,2048]{2,1,0:...) custom-call(s32[1]{0:T(128)} %get-tuple-element.115.me_ref, ...), custom_call_target="tpu_custom_call", output_to_operand_aliasing={{0}: (12, {}), {1}: (13, {}), {2}: (14, {}), {3}: (15, {}),... | custom-call | flops 157286400 | bytes 8650752 | tf_op jit(solution)/shard_map/adamw_0_1_8/pallas_call | solution.py:514
  287.8 0.0 collective-permute-done.2.refs_2_
  287.8 0.0 collective-permute-done.3.refs_3_
  287.8 0.1 collective-permute-start.4
  288.0 3.2 collective-permute-start.5
  291.2 14.0 %adamw_0_4_7.1 = (bf16[2,512,2048]{2,1,0:T(8,128)(2,1)}, bf16[2,512,2048]{2,1,0:T(8,128)(2,1)}, bf16[2,8,256,512]{3,2,1,0:T(8,128)(2,1)}, f32[2,512,2048]{2,1,0:...) custom-call(s32[1]{0:T(128)} %get-tuple-element.115.me_ref, ...), custom_call_target="tpu_custom_call", output_to_operand_aliasing={{0}: (15, {}), {1}: (16, {}), {2}: (17, {}), {3}: (18, {}),... | custom-call | flops 629145600 | bytes 34603008 | tf_op jit(solution)/shard_map/adamw_0_4_7/pallas_call | solution.py:514
  305.2 0.0 collective-permute-done.4.a_ref.refs_0_
  305.2 0.0 collective-permute-done.5.b_ref.refs_1_
  305.2 2.0 halves.1
  307.3 0.0 collective-permute-start.6
  307.3 3.2 collective-permute-start.7
  310.5 7.7 %adamw_0_2_5.1 = (bf16[2,512,2048]{2,1,0:T(8,128)(2,1)}, bf16[2,512,2048]{2,1,0:T(8,128)(2,1)}, bf16[2,8,256,512]{3,2,1,0:T(8,128)(2,1)}, f32[2,512,2048]{2,1,0:...) custom-call(s32[1]{0:T(128)} %get-tuple-element.115.me_ref, ...), custom_call_target="tpu_custom_call", output_to_operand_aliasing={{0}: (13, {}), {1}: (14, {}), {2}: (15, {}), {3}: (16, {}),... | custom-call | flops 314572800 | bytes 17301504 | tf_op jit(solution)/shard_map/adamw_0_2_5/pallas_call | solution.py:514
  318.2 0.0 collective-permute-done.6.refs_0_
  318.2 0.0 collective-permute-done.7.refs_1_
  318.2 5.2 %adamw_0_1_12.1 = (bf16[2,512,2048]{2,1,0:T(8,128)(2,1)}, bf16[2,512,2048]{2,1,0:T(8,128)(2,1)}, bf16[2,8,256,512]{3,2,1,0:T(8,128)(2,1)}, f32[2,512,2048]{2,1,0...) custom-call(s32[1]{0:T(128)} %get-tuple-element.115.me_ref, ...), custom_call_target="tpu_custom_call", output_to_operand_aliasing={{0}: (13, {}), {1}: (14, {}), {2}: (15, {}), {3}: (16, {}),... | custom-call | flops 157286400 | bytes 8650752 | tf_op jit(solution)/shard_map/adamw_0_1_12/pallas_call | solution.py:514
Async XLA Ops:
  249.4 19.1 %collective-permute-start.1 = (bf16[8,192,256]{2,1,0:T(8,128)(2,1)}, bf16[8,192,256]{2,1,0:T(8,128)(2,1)}, u32[]{:S(2)}, u32[]{:S(2)}) collective-permute-start(bf16[8,192,256]{2,1,0:T(8,128)(2,1)} %get-tuple-element.117.refs_0_), channel_id=1, source_target_pairs={{0,7},{1,0},{2,1},{3,2},{4,3},{5,4},{6,5},{7,6},{8,15},{9,8},{10,9... | collective-permute-start | bytes 2359304 | tf_op jit(solution)/shard_map/ppermute | solution.py:590
  252.1 16.9 %collective-permute-start = (bf16[8,192,256]{2,1,0:T(8,128)(2,1)}, bf16[8,192,256]{2,1,0:T(8,128)(2,1)}, u32[]{:S(2)}, u32[]{:S(2)}) collective-permute-start(bf16[8,192,256]{2,1,0:T(8,128)(2,1)} %get-tuple-element.117.refs_0_), channel_id=1, source_target_pairs={{0,1},{1,2},{2,3},{3,4},{4,5},{5,6},{6,7},{7,0},{8,9},{9,10},{10,1... | collective-permute-start | bytes 2359304 | tf_op jit(solution)/shard_map/ppermute | solution.py:590
  269.0 18.8 %collective-permute-start.2 = (bf16[8,192,256]{2,1,0:T(8,128)(2,1)}, bf16[8,192,256]{2,1,0:T(8,128)(2,1)}, u32[]{:S(2)}, u32[]{:S(2)}) collective-permute-start(bf16[8,192,256]{2,1,0:T(8,128)(2,1)} %collective-permute-done.refs_0_), channel_id=1, source_target_pairs={{0,1},{1,2},{2,3},{3,4},{4,5},{5,6},{6,7},{7,0},{8,9},{9,10},{10,1... | collective-permute-start | bytes 2359304 | tf_op jit(solution)/shard_map/ppermute | solution.py:599
  269.5 18.3 %collective-permute-start.3 = (bf16[8,192,256]{2,1,0:T(8,128)(2,1)}, bf16[8,192,256]{2,1,0:T(8,128)(2,1)}, u32[]{:S(2)}, u32[]{:S(2)}) collective-permute-start(bf16[8,192,256]{2,1,0:T(8,128)(2,1)} %collective-permute-done.1.refs_1_), channel_id=1, source_target_pairs={{0,7},{1,0},{2,1},{3,2},{4,3},{5,4},{6,5},{7,6},{8,15},{9,8},{10,9... | collective-permute-start | bytes 2359304 | tf_op jit(solution)/shard_map/ppermute | solution.py:599
  287.8 17.4 %collective-permute-start.4 = (bf16[8,192,256]{2,1,0:T(8,128)(2,1)}, bf16[8,192,256]{2,1,0:T(8,128)(2,1)}, u32[]{:S(2)}, u32[]{:S(2)}) collective-permute-start(bf16[8,192,256]{2,1,0:T(8,128)(2,1)} %collective-permute-done.2.refs_2_), channel_id=1, source_target_pairs={{0,1},{1,2},{2,3},{3,4},{4,5},{5,6},{6,7},{7,0},{8,9},{9,10},{10,1... | collective-permute-start | bytes 2359304 | tf_op jit(solution)/shard_map/ppermute | solution.py:599
  288.0 17.3 %collective-permute-start.5 = (bf16[8,192,256]{2,1,0:T(8,128)(2,1)}, bf16[8,192,256]{2,1,0:T(8,128)(2,1)}, u32[]{:S(2)}, u32[]{:S(2)}) collective-permute-start(bf16[8,192,256]{2,1,0:T(8,128)(2,1)} %collective-permute-done.3.refs_3_), channel_id=1, source_target_pairs={{0,7},{1,0},{2,1},{3,2},{4,3},{5,4},{6,5},{7,6},{8,15},{9,8},{10,9... | collective-permute-start | bytes 2359304 | tf_op jit(solution)/shard_map/ppermute | solution.py:599
  307.3 10.9 %collective-permute-start.6 = (bf16[4,192,256]{2,1,0:T(8,128)(2,1)}, bf16[4,192,256]{2,1,0:T(8,128)(2,1)}, u32[]{:S(2)}, u32[]{:S(2)}) collective-permute-start(bf16[4,192,256]{2,1,0:T(8,128)(2,1)} %get-tuple-element.181), channel_id=1, source_target_pairs={{0,1},{1,2},{2,3},{3,4},{4,5},{5,6},{6,7},{7,0},{8,9},{9,10},{10,1... | collective-permute-start | bytes 1179656 | tf_op jit(solution)/shard_map/ppermute | solution.py:599
  307.3 10.9 %collective-permute-start.7 = (bf16[4,192,256]{2,1,0:T(8,128)(2,1)}, bf16[4,192,256]{2,1,0:T(8,128)(2,1)}, u32[]{:S(2)}, u32[]{:S(2)}) collective-permute-start(bf16[4,192,256]{2,1,0:T(8,128)(2,1)} %get-tuple-element.182), channel_id=1, source_target_pairs={{0,7},{1,0},{2,1},{3,2},{4,3},{5,4},{6,5},{7,6},{8,15},{9,8},{10,9... | collective-permute-start | bytes 1179656 | tf_op jit(solution)/shard_map/ppermute | solution.py:599
